TPU v7x, 32 devices: a whole 2x2x4 slice. The times are simulated.
32 devices in a mesh: seq: 8 (over z, x), fsdp: 4 (over y, core).
Axes of the slice: x: 2, y: 2, z: 4, core: 2. Of those that a mesh axis runs over, the one named last changes fastest.
Arguments:
- tokens: bfloat16 [4, 1024, 1536], P('fsdp', 'seq'), may hold values from -6 to 6
- in_weight: bfloat16 [1536, 6400], P('fsdp'), may hold values from -0.15625 to 0.15625
- step_weight: bfloat16 [1536, 48], P('fsdp'), may hold values from -0.15625 to 0.15625
- conv_kernel: bfloat16 [4, 3328], P(None, 'fsdp'), may hold values from -3 to 3
- conv_bias: bfloat16 [3328], P('fsdp'), may hold values from -3 to 3
- step_bias: bfloat16 [48], P('fsdp'), may hold values from -6 to -3
- log_decay: bfloat16 [48], P('fsdp'), may hold values from -7 to 1
- skip_gain: bfloat16 [48], P('fsdp'), may hold values from 0.5 to 1.5
- gate_gain: bfloat16 [3072], P('fsdp'), may hold values from 0.5 to 1.5
- norm_gain: bfloat16 [1536], P('fsdp'), may hold values from 0.5 to 1.5
- out_weight: bfloat16 [3072, 1536], P('fsdp'), may hold values from -0.109375 to 0.109375
- cotangent: bfloat16 [4, 1024, 1536], P('fsdp', 'seq'), may hold values from -6 to 6
Outputs:
- block_out: bfloat16 [4, 1024, 1536], P('fsdp', 'seq')
- input_grad: float32 [4, 1024, 1536], P('fsdp', 'seq')
- in_weight_grad: float32 [1536, 6400], P('fsdp')
- step_weight_grad: float32 [1536, 48], P('fsdp')
- conv_kernel_grad: float32 [4, 3328], P(None, 'fsdp')
- conv_bias_grad: float32 [3328], P('fsdp')
- step_bias_grad: float32 [48], P('fsdp')
- log_decay_grad: float32 [48], P('fsdp')
- skip_gain_grad: float32 [48], P('fsdp')
- gate_gain_grad: float32 [3072], P('fsdp')
- norm_gain_grad: float32 [1536], P('fsdp')
- out_weight_grad: float32 [3072, 1536], P('fsdp')
All inputs are finite; a program needn't handle non-finite values.
Results may differ from a plain program's by a relative error of at most 0.012.
The roundings to bfloat16 on the way count: a program that leaves them out, or rounds other values in their place, can miss the bound.
Values may be sent and summed in bfloat16 or wider, within the bound.
A program may use at most 320 MiB of HBM per device.

v0:
```python
import jax
import jax.numpy as jnp
from jax import lax
from jax.sharding import PartitionSpec as P

N = 128
BLOCK = 256


epsilon = 1e-05
highest = lax.Precision.HIGHEST


def block_step(carried, pieces, decay_rate):
    x_blk, step_blk, b_blk, c_blk = pieces
    cumulative = jnp.cumsum(step_blk * decay_rate[None, :], axis=0).T
    positions = jnp.arange(step_blk.shape[0])
    triangle = positions[:, None] >= positions[None, :]
    log_gap = jnp.where(triangle[None], cumulative[:, :, None] - cumulative[:, None, :], -1e30)
    scores = jnp.dot(c_blk, b_blk.T, precision=highest)
    mixing = jnp.exp(log_gap) * scores[None] * step_blk.T[:, None, :]
    y_inside = jnp.einsum("hij,jhp->ihp", mixing, x_blk, precision=highest)
    y_carried = jnp.exp(cumulative).T[:, :, None] * jnp.einsum(
        "in,hpn->ihp", c_blk, carried, precision=highest
    )
    weighting = jnp.exp(cumulative[:, -1:] - cumulative) * step_blk.T
    renewed = jnp.exp(cumulative[:, -1])[:, None, None] * carried + jnp.einsum(
        "hj,jhp,jn->hpn", weighting, x_blk, b_blk, precision=highest
    )
    return (renewed, y_inside + y_carried)


def ssd_scan(x_heads, step_size, decay_rate, b_conv, c_conv, carried):
    length = step_size.shape[0]
    extent = min(BLOCK, length)
    number = length // extent
    pieces = (
        x_heads.reshape((number, extent) + x_heads.shape[1:]),
        step_size.reshape((number, extent) + step_size.shape[1:]),
        b_conv.reshape(number, extent, -1),
        c_conv.reshape(number, extent, -1),
    )

    def advance(ssm_state, block_in):
        return block_step(ssm_state, block_in, decay_rate)

    finals, outputs = lax.scan(jax.checkpoint(advance), carried, pieces)
    return outputs.reshape(x_heads.shape)


def prepare(extended, raw_steps, conv_kernel, conv_offset, step_bias, log_rates):
    kernel_width = conv_kernel.shape[0]
    length = extended.shape[0] - kernel_width + 1
    summed = conv_offset[None, :] + sum(
        (
            conv_kernel[offset][None, :] * extended[offset : offset + length]
            for offset in range(kernel_width)
        )
    )
    active = jax.nn.silu(summed)
    split_at = active.shape[1] - 2 * N
    step_size = jax.nn.softplus(raw_steps + step_bias[None, :])
    return (
        active[:, :split_at],
        active[:, split_at : split_at + N],
        active[:, split_at + N :],
        step_size,
        -jnp.exp(log_rates),
    )


def mix_out(x_conv, b_conv, c_conv, step_size, decay_rate, gate_in, skip_part, carried):
    length, head_count = step_size.shape
    x_heads = x_conv.reshape(length, head_count, -1)
    result = (
        ssd_scan(x_heads, step_size, decay_rate, b_conv, c_conv, carried)
        + skip_part[None, :, None] * x_heads
    )
    return result.reshape(length, -1) * jax.nn.silu(gate_in)


def rms_forward(values, gains):
    scaling = lax.rsqrt(jnp.mean(values * values, axis=-1, keepdims=True) + epsilon)
    return (values * scaling * gains[None, :], scaling)


def rms_backward(values, gains, scaling, upstream):
    weighted = upstream * gains[None, :]
    gain_grad = jnp.sum(upstream * values * scaling, axis=0)
    inner_mean = jnp.mean(weighted * values, axis=-1, keepdims=True)
    return (scaling * weighted - scaling**3 * values * inner_mean, gain_grad)


def contract(left, right, left_dim, right_dim):
    return lax.dot_general(
        left, right, (((left_dim,), (right_dim,)), ((), ())), preferred_element_type=jnp.float32
    )


def reorder(gradient, axis_pos, outer_count, inner_count):
    moved_axis = jnp.moveaxis(gradient, axis_pos, 0)
    regrouped = moved_axis.reshape((outer_count, inner_count, -1) + moved_axis.shape[1:])
    swapped = jnp.swapaxes(regrouped, 0, 1).reshape(moved_axis.shape)
    return jnp.moveaxis(swapped, 0, axis_pos)


def place_slice(part, total_len, start_at, axis_pos):
    zeros_shape = part.shape[:axis_pos] + (total_len,) + part.shape[axis_pos + 1 :]
    anchor = tuple((start_at if index_pos == axis_pos else 0 for index_pos in range(part.ndim)))
    return lax.dynamic_update_slice(jnp.zeros(zeros_shape, jnp.float32), part, anchor)


def shards(
    tokens,
    in_weight,
    step_weight,
    conv_kernel,
    conv_bias,
    step_bias,
    log_decay,
    skip_gain,
    gate_gain,
    norm_gain,
    out_weight,
    cotangent,
):
    gathered = (
        lax.all_gather(in_weight, "fsdp", axis=0, tiled=True),
        lax.all_gather(step_weight, "fsdp", axis=0, tiled=True),
        lax.all_gather(conv_kernel, "fsdp", axis=1, tiled=True),
        lax.all_gather(conv_bias, "fsdp", axis=0, tiled=True),
        lax.all_gather(step_bias, "fsdp", axis=0, tiled=True),
        lax.all_gather(log_decay, "fsdp", axis=0, tiled=True),
        lax.all_gather(skip_gain, "fsdp", axis=0, tiled=True),
        lax.all_gather(gate_gain, "fsdp", axis=0, tiled=True),
        lax.all_gather(norm_gain, "fsdp", axis=0, tiled=True),
        lax.all_gather(out_weight, "fsdp", axis=0, tiled=True),
    )
    w_in = gathered[0]
    w_step = gathered[1]
    w_out = gathered[9]
    kernel_f = gathered[2].astype(jnp.float32)
    bias_f = gathered[3].astype(jnp.float32)
    step_bias_f = gathered[4].astype(jnp.float32)
    decay_f = gathered[5].astype(jnp.float32)
    skip_f = gathered[6].astype(jnp.float32)
    gate_f = gathered[7].astype(jnp.float32)
    norm_f = gathered[8].astype(jnp.float32)
    inner_width = w_out.shape[0]
    head_count = w_step.shape[1]
    head_size = inner_width // head_count
    kernel_width = kernel_f.shape[0]
    out_cotangent = cotangent[0]
    residual = tokens[0].astype(jnp.float32)
    normed, scale_in = rms_forward(residual, norm_f)
    hidden = normed.astype(jnp.bfloat16)
    projected = jnp.dot(hidden, w_in, preferred_element_type=jnp.float32).astype(jnp.bfloat16)
    raw_steps = jnp.dot(hidden, w_step, preferred_element_type=jnp.float32).astype(jnp.bfloat16)
    seq_count = lax.axis_size("seq")
    position = lax.axis_index("seq")
    head_group = head_count // seq_count
    columns = head_group * head_size
    col_start = position * columns
    head_start = position * head_group
    tiled_bc = jnp.tile(projected[:, 2 * inner_width :], (1, seq_count))
    gate_part, x_part, step_part, bc_part = (
        lax.all_to_all(projected[:, :inner_width], "seq", split_axis=1, concat_axis=0, tiled=True),
        lax.all_to_all(
            projected[:, inner_width : 2 * inner_width],
            "seq",
            split_axis=1,
            concat_axis=0,
            tiled=True,
        ),
        lax.all_to_all(raw_steps, "seq", split_axis=1, concat_axis=0, tiled=True),
        lax.all_to_all(tiled_bc, "seq", split_axis=1, concat_axis=0, tiled=True),
    )
    my_kernel = jnp.concatenate(
        [lax.dynamic_slice_in_dim(kernel_f, col_start, columns, 1), kernel_f[:, inner_width:]],
        axis=1,
    )
    my_bias = jnp.concatenate(
        [lax.dynamic_slice_in_dim(bias_f, col_start, columns, 0), bias_f[inner_width:]], axis=0
    )
    my_step_bias = lax.dynamic_slice_in_dim(step_bias_f, head_start, head_group, 0)
    my_decay = lax.dynamic_slice_in_dim(decay_f, head_start, head_group, 0)
    my_skip = lax.dynamic_slice_in_dim(skip_f, head_start, head_group, 0)
    padding = jnp.zeros((kernel_width - 1, columns + 2 * N), jnp.float32)
    extended = jnp.concatenate(
        [padding, jnp.concatenate([x_part, bc_part], axis=1).astype(jnp.float32)], axis=0
    )
    prepared, pull_prepare = jax.vjp(
        prepare, extended, step_part.astype(jnp.float32), my_kernel, my_bias, my_step_bias, my_decay
    )
    x_conv, b_conv, c_conv, step_size, decay_rate = prepared
    start_state = jnp.zeros((head_group, head_size, N), jnp.float32)
    gated_f, pull_mix = jax.vjp(
        mix_out,
        x_conv,
        b_conv,
        c_conv,
        step_size,
        decay_rate,
        gate_part.astype(jnp.float32),
        my_skip,
        start_state,
    )
    gated_out = lax.all_to_all(
        gated_f.astype(jnp.bfloat16), "seq", split_axis=0, concat_axis=1, tiled=True
    )
    gated_back = gated_out.astype(jnp.float32)
    mixed_f, scale_out = rms_forward(gated_back, gate_f)
    mixed_norm = mixed_f.astype(jnp.bfloat16)
    block_out = (residual + jnp.dot(mixed_norm, w_out, preferred_element_type=jnp.float32)).astype(
        jnp.bfloat16
    )
    out_grad = contract(mixed_norm, out_cotangent, 0, 0)
    mixed_grad = contract(out_cotangent, w_out, 1, 1)
    gated_grad, gate_gain_grad = rms_backward(gated_back, gate_f, scale_out, mixed_grad)
    gated_grad_b = lax.optimization_barrier(gated_grad.astype(jnp.bfloat16))
    gated_grad_h = lax.all_to_all(
        gated_grad_b, "seq", split_axis=1, concat_axis=0, tiled=True
    ).astype(jnp.float32)
    x_grad, b_grad, c_grad, step_grad, rate_grad, gate_in_grad, skip_grad_h, unused = pull_mix(
        gated_grad_h
    )
    ext_grad, raw_grad, kernel_grad_h, bias_grad_h, step_bias_grad_h, decay_grad_h = pull_prepare(
        (x_grad, b_grad, c_grad, step_grad, rate_grad)
    )
    body_grad = ext_grad[kernel_width - 1 :]
    gate_back, x_back, step_back = (
        lax.all_to_all(
            gate_in_grad.astype(jnp.bfloat16), "seq", split_axis=0, concat_axis=1, tiled=True
        ),
        lax.all_to_all(
            body_grad[:, :columns].astype(jnp.bfloat16),
            "seq",
            split_axis=0,
            concat_axis=1,
            tiled=True,
        ),
        lax.all_to_all(
            raw_grad.astype(jnp.bfloat16), "seq", split_axis=0, concat_axis=1, tiled=True
        ),
    )
    bc_back = lax.psum_scatter(
        body_grad[:, columns:].astype(jnp.bfloat16), "seq", scatter_dimension=0, tiled=True
    )
    proj_grad = jnp.concatenate([gate_back, x_back, bc_back], axis=1)
    kernel_grad = jnp.concatenate(
        [
            place_slice(kernel_grad_h[:, :columns], inner_width, col_start, 1),
            kernel_grad_h[:, columns:],
        ],
        axis=1,
    )
    bias_grad = jnp.concatenate(
        [place_slice(bias_grad_h[:columns], inner_width, col_start, 0), bias_grad_h[columns:]],
        axis=0,
    )
    step_bias_grad = place_slice(step_bias_grad_h, head_count, head_start, 0)
    decay_grad = place_slice(decay_grad_h, head_count, head_start, 0)
    skip_grad = place_slice(skip_grad_h, head_count, head_start, 0)
    in_grad = contract(hidden, proj_grad, 0, 0)
    step_w_grad = contract(hidden, step_back, 0, 0)
    hidden_grad = contract(proj_grad, w_in, 1, 1) + contract(step_back, w_step, 1, 1)
    resid_grad, norm_gain_grad = rms_backward(residual, norm_f, scale_in, hidden_grad)
    input_grad = out_cotangent.astype(jnp.float32) + resid_grad
    fsdp_count = lax.axis_size("fsdp")
    seq_total = lax.axis_size("seq")

    def spread_heads(gradient):
        return jnp.tile(gradient.reshape(fsdp_count, -1), (seq_total, 1)).reshape(-1)

    blocks = (
        lax.psum_scatter(
            reorder(in_grad, 0, fsdp_count, seq_total),
            ("seq", "fsdp"),
            scatter_dimension=0,
            tiled=True,
        ),
        lax.psum_scatter(
            reorder(step_w_grad, 0, fsdp_count, seq_total),
            ("seq", "fsdp"),
            scatter_dimension=0,
            tiled=True,
        ),
        lax.psum_scatter(
            reorder(kernel_grad, 1, fsdp_count, seq_total),
            ("seq", "fsdp"),
            scatter_dimension=1,
            tiled=True,
        ),
        lax.psum_scatter(
            reorder(bias_grad, 0, fsdp_count, seq_total),
            ("seq", "fsdp"),
            scatter_dimension=0,
            tiled=True,
        ),
        lax.psum_scatter(
            spread_heads(step_bias_grad), ("seq", "fsdp"), scatter_dimension=0, tiled=True
        ),
        lax.psum_scatter(
            spread_heads(decay_grad), ("seq", "fsdp"), scatter_dimension=0, tiled=True
        ),
        lax.psum_scatter(spread_heads(skip_grad), ("seq", "fsdp"), scatter_dimension=0, tiled=True),
        lax.psum_scatter(
            reorder(gate_gain_grad, 0, fsdp_count, seq_total),
            ("seq", "fsdp"),
            scatter_dimension=0,
            tiled=True,
        ),
        lax.psum_scatter(
            reorder(norm_gain_grad, 0, fsdp_count, seq_total),
            ("seq", "fsdp"),
            scatter_dimension=0,
            tiled=True,
        ),
        lax.psum_scatter(
            reorder(out_grad, 0, fsdp_count, seq_total),
            ("seq", "fsdp"),
            scatter_dimension=0,
            tiled=True,
        ),
    )
    joined = (
        lax.all_gather(blocks[0], "seq", axis=0, tiled=True),
        lax.all_gather(blocks[1], "seq", axis=0, tiled=True),
        lax.all_gather(blocks[2], "seq", axis=1, tiled=True),
        lax.all_gather(blocks[3], "seq", axis=0, tiled=True),
        lax.all_gather(blocks[7], "seq", axis=0, tiled=True),
        lax.all_gather(blocks[8], "seq", axis=0, tiled=True),
        lax.all_gather(blocks[9], "seq", axis=0, tiled=True),
    )
    totals = (
        joined[0],
        joined[1],
        joined[2],
        joined[3],
        blocks[4],
        blocks[5],
        blocks[6],
        joined[4],
        joined[5],
        joined[6],
    )
    return (
        block_out[None],
        input_grad[None],
        totals[0],
        totals[1],
        totals[2],
        totals[3],
        totals[4],
        totals[5],
        totals[6],
        totals[7],
        totals[8],
        totals[9],
    )


def solution(mesh):
    placed = (
        P("fsdp", "seq", None),
        P("fsdp", None),
        P("fsdp", None),
        P(None, "fsdp"),
        P("fsdp"),
        P("fsdp"),
        P("fsdp"),
        P("fsdp"),
        P("fsdp"),
        P("fsdp"),
        P("fsdp", None),
        P("fsdp", "seq", None),
    )
    return jax.shard_map(
        shards,
        mesh=mesh,
        in_specs=placed,
        out_specs=(
            P("fsdp", "seq", None),
            P("fsdp", "seq", None),
            P("fsdp", None),
            P("fsdp", None),
            P(None, "fsdp"),
            P("fsdp"),
            P("fsdp"),
            P("fsdp"),
            P("fsdp"),
            P("fsdp"),
            P("fsdp"),
            P("fsdp", None),
        ),
        check_vma=False,
    )
```

profile of v0, /device:TPU:0, one launch (start us, length us, event | category | flops | bytes accessed | tf_op | source)
XLA Modules:
  0.0 1683.3 jit_solution(14580512450812876870)
XLA Ops:
  8.0 6.2 all-gather
  14.2 5.8 all_gather.52
  21.6 6.0 all-to-all-start
  28.3 108.3 %all-gather.9.cloned.1.call-done = bf16[1536,6400]{1,0:T(8,128)(2,1)} async-done(((bf16[384,6400]{1,0:T(8,128)(2,1)}), bf16[1536,6400]{1,0:T(8,128)(2,1)}) %all-gather.9.cloned.1.call-update) | async-done | bytes 19660816 | tf_op jit(solution)/shard_map/all_gather | solution.py:128
  136.7 9.4 convolution_convert_fusion
  146.9 5.5 all-to-all-start.2
  154.5 12.8 all-to-all-done.2
  173.9 7.2 all-reduce.30
  181.1 5.5 all-gather.1
  211.1 74.2 %while.41 = (s32[]{:T(128)}, f32[6,64,128]{2,1,0:T(8,128)S(1)}, f32[4,256,6,64]{1,0,3,2:T(4,128)}, f32[4,6,64,128]{3,2,1,0:T(8,128)}, f32[4,256,6]{1,2,0:T(8,128...) while((s32[]{:T(128)}, f32[6,64,128]{2,1,0:T(8,128)S(1)}, ...), condition=%wide.region_4.5_spmd.clone, body=%wide.region_1.4_spmd.clone.sunk | while | flops 706957824 | bytes 5773208 | solution.py:47
  220.1 9.5 dynamic_update_slice.89
  238.7 9.5 dynamic_update_slice.89
  257.2 9.5 dynamic_update_slice.89
  275.8 9.5 dynamic_update_slice.89
  298.7 6.0 all-to-all-start.4
  304.7 5.7 all-gather.2
  310.5 13.8 all-to-all-done.4
  325.4 7.5 multiply_reduce_fusion.8
  346.6 14.6 all-to-all-done.5
  376.3 167.1 %while.42 = (s32[]{:T(128)}, f32[6]{0:T(128)}, f32[6,64,128]{2,1,0:T(8,128)S(1)}, f32[4,256,6,64]{1,0,3,2:T(4,128)}, f32[4,256,6]{1,2,0:T(8,128)}, /*index=5*/f3...) while((s32[]{:T(128)}, f32[6]{0:T(128)}, ...), condition=%wide.region_20.21_spmd.clone, body=%wide.region_7.20_spmd.clone.sunk | while | flops 1669247488 | bytes 18030544 | solution.py:47
  389.8 7.6 reduce-window.74
  402.5 9.5 dynamic_update_slice.93
  431.0 7.6 reduce-window.74
  444.3 9.5 dynamic_update_slice.93
  472.9 7.6 reduce-window.74
  486.2 9.5 dynamic_update_slice.93
  514.7 7.6 reduce-window.74
  528.0 9.5 dynamic_update_slice.93
  549.5 4.9 multiply_reduce_fusion.9
  567.3 7.1 copy.333
  575.2 9.9 all_to_all.141
  588.7 4.9 add_convert_fusion
  594.7 13.2 all-to-all-done.6
  613.2 21.1 %all-to-all-done.7 = bf16[8,128,384]{2,1,0:T(8,128)(2,1)} async-done(((bf16[8,128,384]{2,1,0:T(8,128)(2,1)}), bf16[8,128,384]{2,1,0:T(8,128)(2,1)}, u32[]{:S(2)}, u32[]{:S(2)}) %all-to-all-start.7) | async-done | bytes 786464 | tf_op jit(solution)/shard_map/all_to_all | solution.py:235
  638.9 12.3 fusion.152
  653.4 20.1 %convolution_bitcast_fusion.2 = f32[8,4,48,6400]{3,2,0,1:T(8,128)} fusion(bf16[4,8,48,128]{3,2,1,0:T(8,128)(2,1)S(1)} %bitcast.577, bf16[128,6400]{1,0:T(8,128)(2,1)} %constant_dynamic-update-slice_fusion), kind=kOutput, calls=%fused_computation.128 | convolution fusion | flops 2516582400 | bytes 41353216 | tf_op jit(solution)/shard_map/dot_general | solution.py:95
  673.5 28.6 %copy.323 = f32[8,4,48,6400]{3,2,1,0:T(8,128)} copy(f32[8,4,48,6400]{3,2,0,1:T(8,128)} %convolution_bitcast_fusion.2) | data formatting | bytes 78643200 | tf_op jit(solution)/shard_map/transpose | solution.py:103
  711.3 130.3 %reduce-scatter.12.cloned.1.call-done = f32[96,1536]{1,0:T(8,128)} async-done(((f32[3072,1536]{1,0:T(8,128)}), f32[96,1536]{1,0:T(8,128)}) %reduce-scatter.12.cloned.1.call-update) | async-done | bytes 589840 | tf_op jit(solution)/shard_map/reduce_scatter | solution.py:319
  841.7 364.2 %reduce-scatter.10.cloned.1.call-done = f32[48,6400]{1,0:T(8,128)} async-done(((f32[1536,6400]{1,0:T(8,128)}), f32[48,6400]{1,0:T(8,128)}) %reduce-scatter.10.cloned.1.call-update) | async-done | bytes 1228816 | tf_op jit(solution)/shard_map/reduce_scatter | solution.py:276
  1208.5 5.9 fusion.97
  1214.4 123.8 %all-reduce.33.cloned.1.call-done = (f32[4,3328]{1,0:T(4,128)}, f32[3328]{0:T(1024)}, f32[384]{0:T(512)}, f32[384]{0:T(512)}, f32[384]{0:T(512)}, /*index=5*/f32[3072]{0:T(1024)}, f32[1536]{0:T(1024)}) async-done(((f32[4,3328]{1,0:T(4,128)}, f32[3328]{0:T(1024)}, f32[384]{0:T(512)}, f32[384]{0:T(512)}, f32[384]{0:T(512)}, /*index=5*/f32[3072]{0:T(1024)}, f32[1536]{0:T(1024)}), (f32[4,3328]{1,0:T(4,128)}, ...) | async-done | bytes 89616
  1338.9 27.0 %all-gather.3 = f32[8,104,4]{1,2,0:T(4,128)S(1)} all-gather(f32[1,104,4]{1,2,0:T(4,128)S(1)} %dynamic-slice_bitcast_fusion.7), channel_id=1, replica_groups=mesh['seq'=8,'fsdp'=4] {'seq'}, dimensions={0}, use_global_device_ids=true | all-gather | bytes 14976 | tf_op jit(solution)/shard_map/all_gather | solution.py:329
  1373.0 35.5 %all-reduce.29 = (f32[832]{0:T(1024)}, f32[768]{0:T(1024)}, f32[384]{0:T(512)}) all-reduce(f32[832]{0:T(1024)S(1)} %dynamic-slice_dynamic-update-slice_fusion.2, f32[768]{0:T(1024)S(1)} %dynamic-slice_dynamic-update-slice_fusion.1, f32[384]{0:T(512)S(1)} %dynamic-slice_dynamic-update-slice_fusion), channel_id=1, replica_groups=mesh['seq'=8,'fsdp'=4] {'seq'}, use_global_device_ids=true, to_apply=%add.18 | all-reduce | flops 1984 | bytes 15872
  1408.5 32.7 %reduce-scatter.14.cloned.1.call-done = f32[48,48]{1,0:T(8,128)} async-done(((f32[1536,48]{1,0:T(8,128)}), f32[48,48]{1,0:T(8,128)}) %reduce-scatter.14.cloned.1.call-update) | async-done | bytes 9232 | tf_op jit(solution)/shard_map/reduce_scatter | solution.py:282
  1441.3 32.1 %all_gather.62 = f32[384,48]{1,0:T(8,128)S(1)} all-gather(f32[48,48]{1,0:T(8,128)} %reduce-scatter.14.cloned.1.call-done), channel_id=1, replica_groups=mesh['seq'=8,'fsdp'=4] {'seq'}, dimensions={0}, use_global_device_ids=true | all-gather | bytes 82944 | tf_op jit(solution)/shard_map/all_gather | solution.py:328
  1474.1 48.8 %all-gather.15.cloned.1.call-done = f32[768,1536]{1,0:T(8,128)} async-done(((f32[96,1536]{1,0:T(8,128)}), f32[768,1536]{1,0:T(8,128)}) %all-gather.15.cloned.1.call-update) | async-done | bytes 4718608 | tf_op jit(solution)/shard_map/all_gather | solution.py:333
  1522.9 142.8 %all-gather.13.cloned.1.call-done = f32[384,6400]{1,0:T(8,128)} async-done(((f32[48,6400]{1,0:T(8,128)}), f32[384,6400]{1,0:T(8,128)}) %all-gather.13.cloned.1.call-update) | async-done | bytes 9830416 | tf_op jit(solution)/shard_map/all_gather | solution.py:327
  1665.7 8.4 copy.536
  (632 shorter events, 269.2 us)
Async XLA Ops:
  7.2 12.8 copy-start.14
  7.2 129.5 %all-gather.9.cloned.1.call-start = ((), (), s32[]{:S(2)}) async-start(), calls=%async_computation.13 | async-start | bytes 24576000 | tf_op jit(solution)/shard_map/all_gather | solution.py:128
  14.2 122.5 %copy-start.41 = (f32[1536]{0:T(1024)}, f32[1536]{0:T(1024)S(1)}, u32[]{:S(2)}) copy-start(f32[1536]{0:T(1024)S(1)} %reshape.548) | copy-start | bytes 18436
  20.7 116.0 %copy-start.58 = (f32[128]{0:T(128)}, f32[128]{0:T(128)S(1)}, u32[]{:S(2)}) copy-start(f32[128]{0:T(128)S(1)} %get-tuple-element.798) | copy-start | bytes 1540
  21.6 124.5 %all-to-all-start = ((bf16[128,8,6]{0,2,1:T(8,128)(2,1)}), bf16[128,8,6]{0,2,1:T(8,128)(2,1)S(1)}, u32[]{:S(2)}, u32[]{:S(2)}) async-start(bf16[128,8,6]{0,2,1:T(8,128)(2,1)} %all_to_all.106), calls=%async_computation | async-start | bytes 32768 | tf_op jit(solution)/shard_map/all_to_all | solution.py:175
  27.6 297.3 %all-gather.11.cloned.1.call-start = ((), (), s32[]{:S(2)}) async-start(), calls=%async_computation.14 | async-start | bytes 11796480 | tf_op jit(solution)/shard_map/all_gather | solution.py:137
  146.1 41.3 %copy-start.43 = (bf16[128,8,6]{0,2,1:T(8,128)(2,1)}, bf16[128,8,6]{0,2,1:T(8,128)(2,1)S(1)}, u32[]{:S(2)}) copy-start(bf16[128,8,6]{0,2,1:T(8,128)(2,1)S(1)} %all-to-all-done) | copy-start | bytes 36868
  146.9 20.4 %all-to-all-start.2 = ((bf16[128,8,256]{2,0,1:T(8,128)(2,1)}), bf16[128,8,256]{2,0,1:T(8,128)(2,1)S(1)}, u32[]{:S(2)}, u32[]{:S(2)}) async-start(bf16[128,8,256]{2,0,1:T(8,128)(2,1)} %tile.28), calls=%async_computation.2 | async-start | bytes 1048576 | tf_op jit(solution)/shard_map/all_to_all | solution.py:176
  153.5 17.5 %copy-start.75 = (u32[32]{0:T(128)S(1)}, u32[32]{0:T(128)}, u32[]{:S(2)}) copy-start(u32[32]{0:T(128)} %constant.180) | copy-start | bytes 388
  153.5 19.4 %copy-start.71 = (bf16[12]{0:T(256)(128)(2,1)S(1)}, bf16[12]{0:T(256)(128)(2,1)}, u32[]{:S(2)}) copy-start(bf16[12]{0:T(256)(128)(2,1)} %param.21) | copy-start | bytes 76
  153.5 19.7 %copy-start.72 = (bf16[12]{0:T(256)(128)(2,1)S(1)}, bf16[12]{0:T(256)(128)(2,1)}, u32[]{:S(2)}) copy-start(bf16[12]{0:T(256)(128)(2,1)} %param.23) | copy-start | bytes 76
  153.5 19.9 %copy-start.73 = (bf16[12]{0:T(256)(128)(2,1)S(1)}, bf16[12]{0:T(256)(128)(2,1)}, u32[]{:S(2)}) copy-start(bf16[12]{0:T(256)(128)(2,1)} %param.22) | copy-start | bytes 76
  153.5 20.1 %copy-start.65 = (bf16[832]{0:T(1024)(128)(2,1)S(1)}, bf16[832]{0:T(1024)(128)(2,1)}, u32[]{:S(2)}) copy-start(bf16[832]{0:T(1024)(128)(2,1)} %param.20) | copy-start | bytes 4996
  153.5 27.6 %copy-start.62 = (bf16[4,832]{1,0:T(4,128)(2,1)S(1)}, bf16[4,832]{1,0:T(4,128)(2,1)}, u32[]{:S(2)}) copy-start(bf16[4,832]{1,0:T(4,128)(2,1)} %param.19) | copy-start | bytes 19972
  153.6 34.0 %copy-start.28 = (bf16[128,3072]{1,0:T(8,128)(2,1)S(1)}, bf16[128,3072]{1,0:T(8,128)(2,1)}, u32[]{:S(2)}) copy-start(bf16[128,3072]{1,0:T(8,128)(2,1)} %get-tuple-element.791) | copy-start | bytes 2359300
  167.4 28.5 %copy-start.23 = (bf16[128,8,256]{2,0,1:T(8,128)(2,1)}, bf16[128,8,256]{2,0,1:T(8,128)(2,1)S(1)}, u32[]{:S(2)}) copy-start(bf16[128,8,256]{2,0,1:T(8,128)(2,1)S(1)} %all-to-all-done.2) | copy-start | bytes 1572868
  167.4 24.0 %all-to-all-start.1 = ((bf16[128,8,384]{2,0,1:T(8,128)(2,1)}), bf16[128,8,384]{2,0,1:T(8,128)(2,1)S(1)}, u32[]{:S(2)}, u32[]{:S(2)}) async-start(bf16[128,8,384]{2,0,1:T(8,128)(2,1)} %bitcast.418), calls=%async_computation.1 | async-start | bytes 1572864 | tf_op jit(solution)/shard_map/all_to_all | solution.py:168
  181.1 160.4 %copy-start.68 = (f32[48]{0:T(128)}, f32[48]{0:T(128)S(1)}, u32[]{:S(2)}) copy-start(f32[48]{0:T(128)S(1)} %convert_element_type.138) | copy-start | bytes 580
  187.1 108.2 %copy-start.55 = (f32[384]{0:T(512)}, f32[384]{0:T(512)S(1)}, u32[]{:S(2)}) copy-start(f32[384]{0:T(512)S(1)} %mul.640) | copy-start | bytes 4612
  187.2 8.9 copy-start.46
  187.2 8.9 copy-start.48
  187.2 8.9 copy-start.50
  187.2 8.9 copy-start.52
  191.4 99.1 %all-to-all-start.3 = ((bf16[128,8,384]{0,2,1:T(8,128)(2,1)}), bf16[128,8,384]{0,2,1:T(8,128)(2,1)}, u32[]{:S(2)}, u32[]{:S(2)}) async-start(bf16[128,8,384]{0,2,1:T(8,128)(2,1)} %bitcast.18), calls=%async_computation.3 | async-start | bytes 1572864 | tf_op jit(solution)/shard_map/all_to_all | solution.py:167
  298.7 25.5 %all-to-all-start.4 = ((bf16[8,128,384]{2,1,0:T(8,128)(2,1)}), bf16[8,128,384]{2,1,0:T(8,128)(2,1)S(1)}, u32[]{:S(2)}, u32[]{:S(2)}) async-start(bf16[8,128,384]{2,1,0:T(8,128)(2,1)} %bitcast.580), calls=%async_computation.4 | async-start | bytes 1572864 | tf_op jit(solution)/shard_map/all_to_all | solution.py:208
  310.5 22.4 %copy-start.35 = (f32[4,1,768]{2,1,0:T(1,128)}, f32[4,1,768]{2,1,0:T(1,128)S(1)}, u32[]{:S(2)}) copy-start(f32[4,1,768]{2,1,0:T(1,128)S(1)} %convert_element_type.182) | copy-start | bytes 36868
  337.1 24.1 %all-to-all-start.5 = ((bf16[128,8,384]{0,2,1:T(8,128)(2,1)}), bf16[128,8,384]{0,2,1:T(8,128)(2,1)}, u32[]{:S(2)}, u32[]{:S(2)}) async-start(bf16[128,8,384]{0,2,1:T(8,128)(2,1)} %bitcast.583), calls=%async_computation.5 | async-start | bytes 1572864 | tf_op jit(solution)/shard_map/all_to_all | solution.py:221
  341.4 296.0 %reduce-scatter.8.cloned.1.call-start = ((), (), s32[]{:S(2)}) async-start(), calls=%async_computation.15 | async-start | bytes 589824 | tf_op jit(solution)/shard_map/reduce_scatter | solution.py:246
  399.6 12.4 copy-start.40
  441.5 12.4 copy-start.40
  483.3 12.4 copy-start.40
  525.2 12.4 copy-start.40
  563.1 278.5 %reduce-scatter.12.cloned.1.call-start = ((), (), s32[]{:S(2)}) async-start(), calls=%async_computation.18 | async-start | bytes 19464192 | tf_op jit(solution)/shard_map/reduce_scatter | solution.py:319
  585.1 22.8 %all-to-all-start.6 = ((bf16[8,128,384]{2,1,0:T(8,128)(2,1)}), bf16[8,128,384]{2,1,0:T(8,128)(2,1)S(1)}, u32[]{:S(2)}, u32[]{:S(2)}) async-start(bf16[8,128,384]{2,1,0:T(8,128)(2,1)} %bitcast.29), calls=%async_computation.6 | async-start | bytes 1572864 | tf_op jit(solution)/shard_map/all_to_all | solution.py:232
  607.9 26.4 %all-to-all-start.7 = ((bf16[8,128,384]{2,1,0:T(8,128)(2,1)}), bf16[8,128,384]{2,1,0:T(8,128)(2,1)}, u32[]{:S(2)}, u32[]{:S(2)}) async-start(bf16[8,128,384]{2,1,0:T(8,128)(2,1)} %bitcast.584), calls=%async_computation.7 | async-start | bytes 1572864 | tf_op jit(solution)/shard_map/all_to_all | solution.py:235
  612.1 593.8 %reduce-scatter.10.cloned.1.call-start = ((), (), s32[]{:S(2)}) async-start(), calls=%async_computation.16 | async-start | bytes 40550400 | tf_op jit(solution)/shard_map/reduce_scatter | solution.py:276
  613.2 22.3 %copy-start.27 = (bf16[8,16,8,384]{3,2,0,1:T(8,128)(2,1)S(1)}, bf16[8,16,8,384]{3,2,0,1:T(8,128)(2,1)}, u32[]{:S(2)}) copy-start(bf16[8,16,8,384]{3,2,0,1:T(8,128)(2,1)} %copy.389) | copy-start | bytes 2359300
  638.8 12.3 copy-start.15
  638.8 12.3 copy-start.34
  638.8 12.4 copy-start.42
  638.8 12.4 copy-start.59
  702.1 636.1 %all-reduce.33.cloned.1.call-start = ((), (), s32[]{:S(2)}) async-start(), calls=%async_computation.21 | async-start | bytes 192512
  710.0 731.3 %reduce-scatter.14.cloned.1.call-start = ((), (), s32[]{:S(2)}) async-start(), calls=%async_computation.20 | async-start | bytes 811008 | tf_op jit(solution)/shard_map/reduce_scatter | solution.py:282
  711.2 494.7 %copy-start.74 = (u32[32]{0:T(128)S(1)}, u32[32]{0:T(128)}, u32[]{:S(2)}) copy-start(u32[32]{0:T(128)} %constant.200) | copy-start | bytes 388
  711.3 497.2 %copy-start.36 = (f32[4,1,768]{2,1,0:T(1,128)S(1)}, f32[4,1,768]{2,1,0:T(1,128)}, u32[]{:S(2)}) copy-start(f32[4,1,768]{2,1,0:T(1,128)} %copy-done.35) | copy-start | bytes 36868
  711.3 497.2 %copy-start.61 = (f32[128]{0:T(128)S(1)}, f32[128]{0:T(128)}, u32[]{:S(2)}) copy-start(f32[128]{0:T(128)} %copy-done.60) | copy-start | bytes 1540
  711.3 811.6 %all-gather.15.cloned.1.call-start = ((), (), s32[]{:S(2)}) async-start(), calls=%async_computation.19 | async-start | bytes 5308416 | tf_op jit(solution)/shard_map/all_gather | solution.py:333
  841.6 824.0 %all-gather.13.cloned.1.call-start = ((), (), s32[]{:S(2)}) async-start(), calls=%async_computation.17 | async-start | bytes 11059200 | tf_op jit(solution)/shard_map/all_gather | solution.py:327
  (63 other events, 254.6 us)
Sparse Core Ops, SparseCore 0:
  9.6 127.0 all-gather.8
  138.2 64.7 all-gather.10
  563.2 63.3 reduce-scatter.7
  632.8 208.7 reduce-scatter.11
  847.9 357.9 reduce-scatter.9
  1213.3 124.8 all-reduce.32
  1343.8 97.3 reduce-scatter.13
  1443.5 79.3 all-gather.14
  1525.0 140.5 all-gather.12
where the time goes:
time: 1690 us; the launch traced here: 1680 us
  waiting for transfers between devices  1030 us (61%)
  local copies, waits for them, and re-layouts  232 us (14%)
  blocking collectives  135 us (8%)
  matrix products  133 us (8%)
  other arithmetic  96 us (6%)
  starting transfers between devices  38 us (2%)
  between operations  18.6 us (1%)
    reduce_scatter x1, waiting for transfers between devices, shards(): lax.psum_scatter(reorder(in_grad, 0, fsdp_count, seq_total), ('seq', 'fsd...  364 us
    all_gather x1, waiting for transfers between devices, shards(): lax.all_gather(blocks[0], 'seq', axis=0, tiled=True)  143 us
    reduce_scatter x1, waiting for transfers between devices, shards(): lax.psum_scatter(reorder(out_grad, 0, fsdp_count, seq_total), ('seq', 'fs...  130 us
    unnamed x10, waiting for transfers between devices  125 us
    all_gather x1, waiting for transfers between devices, shards(): lax.all_gather(in_weight, 'fsdp', axis=0, tiled=True)  108 us
    dynamic_update_slice x16, local copies, waits for them, and re-layouts, ssd_scan(): finals, outputs = lax.scan(jax.checkpoint(advance), carried, pieces)  79.5 us
    another operation x33, other arithmetic  50.7 us
    all_gather x1, waiting for transfers between devices, shards(): lax.all_gather(blocks[9], 'seq', axis=0, tiled=True)  48.8 us
  transfers between devices with their start and end apart: 17, of which 13 were waited for; matrix products, arithmetic and copies ran while one was open for 14% of the time, Pallas kernels for 0%

commit v1 on v0

v1 whole, which is shorter than its diff:
```python
import jax
import jax.numpy as jnp
from jax import lax
from jax.sharding import PartitionSpec as P

N = 128
BLOCK = 256


epsilon = 1e-05
bf16 = jnp.bfloat16
f32 = jnp.float32


def block_step(carried, pieces, decay_rate):
    x_blk, step_blk, b_blk, c_blk = pieces
    cumulative = jnp.cumsum(step_blk * decay_rate[None, :], axis=0).T
    positions = jnp.arange(step_blk.shape[0])
    triangle = positions[:, None] >= positions[None, :]
    log_gap = jnp.where(triangle[None], cumulative[:, :, None] - cumulative[:, None, :], -1e30)
    scores = jnp.dot(c_blk, b_blk.T)
    mixing = jnp.exp(log_gap) * scores[None] * step_blk.T[:, None, :]
    y_inside = jnp.einsum("hij,jhp->ihp", mixing, x_blk)
    y_carried = jnp.exp(cumulative).T[:, :, None] * jnp.einsum("in,hpn->ihp", c_blk, carried)
    weighting = jnp.exp(cumulative[:, -1:] - cumulative) * step_blk.T
    renewed = jnp.exp(cumulative[:, -1])[:, None, None] * carried + jnp.einsum(
        "hj,jhp,jn->hpn", weighting, x_blk, b_blk
    )
    return (renewed, y_inside + y_carried)


def ssd_scan(x_heads, step_size, decay_rate, b_conv, c_conv, carried):
    length = step_size.shape[0]
    extent = min(BLOCK, length)
    number = length // extent
    pieces = (
        x_heads.reshape((number, extent) + x_heads.shape[1:]),
        step_size.reshape((number, extent) + step_size.shape[1:]),
        b_conv.reshape(number, extent, -1),
        c_conv.reshape(number, extent, -1),
    )
    outs = []
    for k in range(number):
        carried, out = block_step(carried, tuple(p[k] for p in pieces), decay_rate)
        outs.append(out)
    return jnp.concatenate(outs, 0).reshape(x_heads.shape)


def prepare(extended, raw_steps, conv_kernel, conv_offset, step_bias, log_rates):
    kernel_width = conv_kernel.shape[0]
    length = extended.shape[0] - kernel_width + 1
    summed = conv_offset[None, :] + sum(
        (
            conv_kernel[offset][None, :] * extended[offset : offset + length]
            for offset in range(kernel_width)
        )
    )
    active = jax.nn.silu(summed)
    split_at = active.shape[1] - 2 * N
    step_size = jax.nn.softplus(raw_steps + step_bias[None, :])
    return (
        active[:, :split_at],
        active[:, split_at : split_at + N],
        active[:, split_at + N :],
        step_size,
        -jnp.exp(log_rates),
    )


def mix_out(x_conv, b_conv, c_conv, step_size, decay_rate, gate_in, skip_part, carried):
    length, head_count = step_size.shape
    x_heads = x_conv.reshape(length, head_count, -1)
    result = (
        ssd_scan(x_heads, step_size, decay_rate, b_conv, c_conv, carried)
        + skip_part[None, :, None] * x_heads
    )
    return result.reshape(length, -1) * jax.nn.silu(gate_in)


def contract(left, right, left_dim, right_dim):
    return lax.dot_general(
        left, right, (((left_dim,), (right_dim,)), ((), ())), preferred_element_type=f32
    )


def shards(
    tokens,
    in_weight,
    step_weight,
    conv_kernel,
    conv_bias,
    step_bias,
    log_decay,
    skip_gain,
    gate_gain,
    norm_gain,
    out_weight,
    cotangent,
):
    seqs = lax.axis_size("seq")
    fs = lax.axis_size("fsdp")
    pos = lax.axis_index("seq")
    fpos = lax.axis_index("fsdp")
    heads = step_weight.shape[1]
    inner = out_weight.shape[0] * fs
    width = tokens.shape[-1]
    hg = heads // seqs
    cols = inner // seqs
    col = pos * cols
    KW, conv_l = conv_kernel.shape

    def sl(a, start, size, axis):
        return lax.dynamic_slice_in_dim(a, start, size, axis)

    w_part = jnp.concatenate(
        [
            sl(in_weight, col, cols, 1),
            sl(in_weight, inner + col, cols, 1),
            in_weight[:, 2 * inner :],
            sl(step_weight, pos * hg, hg, 1),
        ],
        axis=1,
    )
    w_g = lax.all_gather(w_part, "fsdp", axis=0, tiled=True)
    small = jnp.concatenate(
        [
            conv_kernel.reshape(-1),
            conv_bias,
            step_bias,
            log_decay,
            skip_gain,
            gate_gain,
            norm_gain,
        ]
    )
    small = lax.all_gather(small, "fsdp", axis=0, tiled=False).astype(f32)
    at = [0]

    def take(n):
        r = small[:, at[0] : at[0] + n]
        at[0] += n
        return r

    kernel_f = take(KW * conv_l).reshape(fs, KW, conv_l).transpose(1, 0, 2).reshape(KW, -1)
    bias_f = take(conv_l).reshape(-1)
    step_bias_f = take(heads // fs).reshape(-1)
    decay_f = take(heads // fs).reshape(-1)
    skip_f = take(heads // fs).reshape(-1)
    gate_f = sl(take(inner // fs).reshape(-1), col, cols, 0)
    norm_f = take(width // fs).reshape(-1)

    tok = lax.all_gather(tokens[0], "seq", axis=0, tiled=True)
    cot = lax.all_gather(cotangent[0], "seq", axis=0, tiled=True)
    w_out = lax.all_gather(out_weight, "fsdp", axis=0, tiled=True)
    w_out_g = sl(w_out, col, cols, 0)
    length = tok.shape[0]
    own = length // seqs

    resid = tok.astype(f32)
    scale_in = lax.rsqrt(jnp.mean(resid * resid, axis=-1, keepdims=True) + epsilon)
    hidden = (resid * scale_in * norm_f[None]).astype(bf16)
    proj = contract(hidden, w_g, 1, 0).astype(bf16).astype(f32)
    gate_in = proj[:, :cols]
    body = proj[:, cols : 2 * cols + 2 * N]
    raw = proj[:, 2 * cols + 2 * N :]
    my_kernel = jnp.concatenate([sl(kernel_f, col, cols, 1), kernel_f[:, inner:]], axis=1)
    my_bias = jnp.concatenate([sl(bias_f, col, cols, 0), bias_f[inner:]], axis=0)
    my_step_bias = sl(step_bias_f, pos * hg, hg, 0)
    my_decay = sl(decay_f, pos * hg, hg, 0)
    my_skip = sl(skip_f, pos * hg, hg, 0)
    extended = jnp.concatenate([jnp.zeros((KW - 1, cols + 2 * N), f32), body], axis=0)
    prepared, pull_prepare = jax.vjp(
        prepare, extended, raw, my_kernel, my_bias, my_step_bias, my_decay
    )
    x_conv, b_conv, c_conv, step_size, decay_rate = prepared
    start = jnp.zeros((hg, cols // hg, N), f32)
    gated_f, pull_mix = jax.vjp(
        mix_out, x_conv, b_conv, c_conv, step_size, decay_rate, gate_in, my_skip, start
    )
    gated_b = gated_f.astype(bf16)
    gated = gated_b.astype(f32)
    mixed_grad = contract(cot, w_out_g, 1, 1)
    g = mixed_grad * gate_f[None]
    stats = jnp.stack([jnp.sum(gated * gated, axis=1), jnp.sum(g * gated, axis=1)])
    stats = lax.psum(stats, "seq") / inner
    scale_out = lax.rsqrt(stats[0] + epsilon)[:, None]
    mixed_norm = (gated * scale_out * gate_f[None]).astype(bf16)
    gate_gain_grad = jnp.sum(mixed_grad * gated * scale_out, axis=0)
    gated_grad = (scale_out * g - scale_out**3 * gated * stats[1][:, None]).astype(bf16)

    mixed_all = lax.all_to_all(mixed_norm, "seq", split_axis=0, concat_axis=1, tiled=True)
    my_tok = tokens[0].astype(f32)
    block_out = (my_tok + contract(mixed_all, w_out, 1, 0)).astype(bf16)
    out_part = contract(mixed_norm, cot, 0, 0)
    x_grad, b_grad, c_grad, step_grad, rate_grad, gate_grad, skip_grad, _ = pull_mix(
        gated_grad.astype(f32)
    )
    ext_grad, raw_grad, kernel_grad, bias_grad, step_bias_grad, decay_grad = pull_prepare(
        (x_grad, b_grad, c_grad, step_grad, rate_grad)
    )
    proj_grad = jnp.concatenate([gate_grad, ext_grad[KW - 1 :], raw_grad], axis=1).astype(bf16)
    hid_part = contract(proj_grad, w_g, 1, 1)
    hidden_grad = lax.psum_scatter(
        hid_part.astype(bf16), "seq", scatter_dimension=0, tiled=True
    ).astype(f32)
    in_part = contract(hidden, proj_grad, 0, 0)
    in_red = lax.psum_scatter(in_part.astype(bf16), "fsdp", scatter_dimension=0, tiled=True)
    in_all = lax.all_gather(in_red, "seq", axis=0, tiled=False).astype(f32)
    in_grad = jnp.concatenate(
        [
            jnp.moveaxis(in_all[:, :, :cols], 0, 1).reshape(-1, inner),
            jnp.moveaxis(in_all[:, :, cols : 2 * cols], 0, 1).reshape(-1, inner),
            jnp.sum(in_all[:, :, 2 * cols : 2 * cols + 2 * N], axis=0),
        ],
        axis=1,
    )
    step_w_grad = jnp.moveaxis(in_all[:, :, 2 * cols + 2 * N :], 0, 1).reshape(-1, heads)
    out_red = lax.psum_scatter(out_part.astype(bf16), "fsdp", scatter_dimension=0, tiled=True)
    out_all = lax.all_gather(out_red, ("seq", "fsdp"), axis=0, tiled=True)
    out_rows = inner // fs
    out_grad = sl(out_all, fpos * out_rows, out_rows, 0).astype(f32)

    own_scale = lax.rsqrt(jnp.mean(my_tok * my_tok, axis=-1, keepdims=True) + epsilon)
    norm_gain_grad = jnp.sum(hidden_grad * my_tok * own_scale, axis=0)
    e = hidden_grad * norm_f[None]
    inner_mean = jnp.mean(e * my_tok, axis=-1, keepdims=True)
    input_grad = cotangent[0].astype(f32) + own_scale * e - own_scale**3 * my_tok * inner_mean

    def put(a, total, start, axis):
        shape = list(a.shape)
        shape[axis] = total
        idx = [0] * a.ndim
        idx[axis] = start
        return lax.dynamic_update_slice(jnp.zeros(shape, f32), a, tuple(idx))

    conv = inner + 2 * N
    kg = jnp.concatenate([put(kernel_grad[:, :cols], inner, col, 1), kernel_grad[:, cols:]], 1)
    bg = jnp.concatenate([put(bias_grad[:cols], inner, col, 0), bias_grad[cols:]], 0)
    packed = jnp.concatenate(
        [
            kg.reshape(-1),
            bg,
            put(step_bias_grad, heads, pos * hg, 0),
            put(decay_grad, heads, pos * hg, 0),
            put(skip_grad, heads, pos * hg, 0),
            put(gate_gain_grad, inner, col, 0),
            norm_gain_grad,
        ]
    )
    packed = lax.psum(packed, ("seq", "fsdp"))
    at[0] = 0

    def grab(n, size, rows=None):
        r = packed[at[0] : at[0] + n]
        at[0] += n
        if rows:
            return sl(r.reshape(rows, -1), fpos * size, size, 1)
        return sl(r, fpos * size, size, 0)

    kernel_out = grab(KW * conv, conv_l, KW)
    bias_out = grab(conv, conv_l)
    sb_out = grab(heads, heads // fs)
    ld_out = grab(heads, heads // fs)
    sk_out = grab(heads, heads // fs)
    gg_out = grab(inner, inner // fs)
    ng_out = grab(width, width // fs)
    return (
        block_out[None],
        input_grad[None],
        in_grad,
        step_w_grad,
        kernel_out,
        bias_out,
        sb_out,
        ld_out,
        sk_out,
        gg_out,
        ng_out,
        out_grad,
    )


def solution(mesh):
    row = P("fsdp", None)
    tok = P("fsdp", "seq", None)
    one = P("fsdp")
    return jax.shard_map(
        shards,
        mesh=mesh,
        in_specs=(tok, row, row, P(None, "fsdp"), one, one, one, one, one, one, row, tok),
        out_specs=(tok, tok, row, row, P(None, "fsdp"), one, one, one, one, one, one, row),
        check_vma=False,
    )
```

time: 1690 us -> 870 us (0.51)
  waiting for transfers between devices: 1030 us -> 511 us
  local copies, waits for them, and re-layouts: 232 us -> 100 us
  blocking collectives: 135 us -> 35.9 us
  matrix products: 133 us -> 75.5 us
  starting transfers between devices: 38 us -> 6.17 us
  other arithmetic: 96 us -> 116 us
    reduce_scatter x4 -> x2, waiting for transfers between devices: 527 us -> 78.5 us  [the longest x1 52.5 us: shards(): lax.psum_scatter(hid_part.astype(bf16), 'seq', scatter_dimension=0, tiled...]
    psum x0 -> x1, waiting for transfers between devices: none -> 95.1 us  [shards(): packed = lax.psum(packed, ('seq', 'fsdp'))]
    unnamed x10 -> x11, waiting for transfers between devices: 125 us -> 42.5 us
    all_gather x6 -> x0, blocking collectives: 82.3 us -> none  [the longest x1 32.1 us: shards(): lax.all_gather(blocks[1], 'seq', axis=0, tiled=True)]
    dynamic_update_slice x20 -> x5, local copies, waits for them, and re-layouts: 80.2 us -> 1.03 us  [put(): return lax.dynamic_update_slice(jnp.zeros(shape, f32), a, tuple(idx))]
    all_to_all x8 -> x1, waiting for transfers between devices: 78.1 us -> 20.4 us  [shards(): lax.all_to_all(mixed_norm, 'seq', split_axis=0, concat_axis=1, tiled=True)]
    dot_general x59 -> x44, matrix products: 89.3 us -> 41.1 us  [the longest x12 22.6 us: block_step(): y_inside = jnp.einsum('hij,jhp->ihp', mixing, x_blk)]
    all_to_all x8 -> x1, starting transfers between devices: 37.6 us -> 5.77 us  [shards(): lax.all_to_all(mixed_norm, 'seq', split_axis=0, concat_axis=1, tiled=True)]
  transfers between devices with their start and end apart: 17 -> 11, of which waited for: 13 -> 11; matrix products, arithmetic and copies ran while one was open for 14% -> 17% of each run, Pallas kernels for 0% -> 0%
where the time goes in v1:
time: 870 us; the launch traced here: 862 us
  waiting for transfers between devices  511 us (59%)
  other arithmetic  116 us (13%)
  local copies, waits for them, and re-layouts  100 us (11%)
  matrix products  75.5 us (9%)
  blocking collectives  35.9 us (4%)
  between operations  17.3 us (2%)
    all_gather x1, waiting for transfers between devices, shards(): in_all = lax.all_gather(in_red, 'seq', axis=0, tiled=False).astype(f32)  96.4 us
    psum x1, waiting for transfers between devices, shards(): packed = lax.psum(packed, ('seq', 'fsdp'))  95.1 us
    all_gather x1, waiting for transfers between devices, shards(): w_out = lax.all_gather(out_weight, 'fsdp', axis=0, tiled=True)  64.3 us
    reduce_scatter x1, waiting for transfers between devices, shards(): lax.psum_scatter(hid_part.astype(bf16), 'seq', scatter_dimension=0, tiled...  52.5 us
    another operation x17, other arithmetic  49.7 us
    unnamed x11, waiting for transfers between devices  42.5 us
    all_gather x1, waiting for transfers between devices, shards(): tok = lax.all_gather(tokens[0], 'seq', axis=0, tiled=True)  42.3 us
    unnamed x312, local copies, waits for them, and re-layouts  41.4 us
  transfers between devices with their start and end apart: 11, of which 11 were waited for; matrix products, arithmetic and copies ran while one was open for 17% of the time, Pallas kernels for 0%

profile of v1, /device:TPU:0, one launch (start us, length us, event | category | flops | bytes accessed | tf_op | source)
XLA Modules:
  0.0 861.9 jit_solution(4475649698283908109)
XLA Ops:
  13.7 13.6 %all-reduce.34 = bf16[21392]{0:T(1024)(128)(2,1)S(1)} all-reduce(bf16[21392]{0:T(1024)(128)(2,1)S(1)} %dynamic-update-slice), channel_id=2, replica_groups=mesh['seq'=8,'fsdp'=4] {'fsdp'}, use_global_device_ids=true, to_apply=%add.34 | all-reduce | flops 21392 | bytes 85568
  30.7 42.3 %all-gather.17.cloned.1.call-done = bf16[1,1024,1536]{2,1,0:T(8,128)(2,1)} async-done(((bf16[1,128,1536]{2,1,0:T(8,128)(2,1)}), bf16[1,1024,1536]{2,1,0:T(8,128)(2,1)}) %all-gather.17.cloned.1.call-update) | async-done | bytes 3145744 | tf_op jit(solution)/shard_map/all_gather | solution.py:152
  73.1 2.7 fusion
  75.8 28.8 %all-gather.11.cloned.1.call-done = bf16[1536,1030]{1,0:T(8,128)(2,1)} async-done(((bf16[384,1030]{1,0:T(8,128)(2,1)}), bf16[1536,1030]{1,0:T(8,128)(2,1)}) %all-gather.11.cloned.1.call-update) | async-done | bytes 3164176 | tf_op jit(solution)/shard_map/all_gather | solution.py:124
  104.6 5.9 fusion.3
  110.8 3.9 fusion.14
  116.2 1.8 reduce-window.64
  118.3 1.8 reduce-window.54
  122.6 2.0 reduce-window.56
  134.5 32.4 %all-gather.19.cloned.1.call-done = bf16[1,1024,1536]{2,1,0:T(8,128)(2,1)} async-done(((bf16[1,128,1536]{2,1,0:T(8,128)(2,1)}), bf16[1,1024,1536]{2,1,0:T(8,128)(2,1)}) %all-gather.19.cloned.1.call-update) | async-done | bytes 3145744 | tf_op jit(solution)/shard_map/all_gather | solution.py:153
  166.9 64.3 %all-gather.13.cloned.1.call-done = bf16[3072,1536]{1,0:T(8,128)(2,1)} async-done(((bf16[768,1536]{1,0:T(8,128)(2,1)}), bf16[3072,1536]{1,0:T(8,128)(2,1)}) %all-gather.13.cloned.1.call-update) | async-done | bytes 9437200 | tf_op jit(solution)/shard_map/all_gather | solution.py:154
  231.3 6.0 fusion.20
  237.9 22.3 %psum.14 = f32[2,1024]{1,0:T(2,128)} all-reduce(f32[2,1024]{1,0:T(2,128)} %pad_maximum_fusion.6), channel_id=1, replica_groups=mesh['seq'=8,'fsdp'=4] {'seq'}, use_global_device_ids=true, to_apply=%region_11.12 | all-reduce | flops 2048 | bytes 16384 | tf_op jit(solution)/shard_map/psum | solution.py:185
  260.9 5.3 multiply_reduce_fusion.4
  291.9 2.6 fusion.75
  294.6 6.8 fusion.118
  302.8 7.5 reduce-window.70
  313.3 8.2 reduce-window.76
  330.9 7.6 reduce-window.74
  340.1 15.3 %reduce-window.66 = f32[6,2,128]{2,1,0:T(2,128)S(1)} reduce-window(f32[6,2,128]{2,1,0:T(2,128)S(1)} %reshape.527, f32[]{:T(128)} %constant.35.clone.1), window={size=1x1x128 pad=0_0x0_0x0_127}, to_apply=%region_21.22 | reduce-window | flops 195072 | bytes 12292 | tf_op jit(solution)/shard_map/reduce-window.8
  359.2 1.8 fusion.102
  373.8 8.0 multiply_reduce_fusion.2
  382.6 2.1 fusion.13
  385.8 6.0 convolution_convert_fusion.2
  392.5 6.2 convolution_convert_fusion
  398.7 3.7 copy.246
  403.5 4.4 fusion.8
  410.0 52.5 %reduce-scatter.6.cloned.1.call-done = bf16[128,1536]{1,0:T(8,128)(2,1)} async-done(((bf16[1024,1536]{1,0:T(8,128)(2,1)}), bf16[128,1536]{1,0:T(8,128)(2,1)}) %reduce-scatter.6.cloned.1.call-update) | async-done | bytes 393232 | tf_op jit(solution)/shard_map/reduce_scatter | solution.py:203
  464.6 40.5 %reduce-scatter.10.cloned.1.call-done = bf16[384,1030]{1,0:T(8,128)(2,1)} async-done(((bf16[1536,1030]{1,0:T(8,128)(2,1)}), bf16[384,1030]{1,0:T(8,128)(2,1)}) %reduce-scatter.10.cloned.1.call-update) | async-done | bytes 791056
  505.1 2.2 copy.247
  507.3 26.0 %reduce-scatter.8.cloned.1.call-done = bf16[96,1536]{1,0:T(8,128)(2,1)} async-done(((bf16[384,1536]{1,0:T(8,128)(2,1)}), bf16[96,1536]{1,0:T(8,128)(2,1)}) %reduce-scatter.8.cloned.1.call-update) | async-done | bytes 294928 | tf_op jit(solution)/shard_map/reduce_scatter | solution.py:218
  534.4 5.8 all-to-all-start
  540.1 20.4 %all-to-all-done = bf16[8,128,384]{1,2,0:T(8,128)(2,1)S(1)} async-done(((bf16[8,128,384]{1,2,0:T(8,128)(2,1)}), bf16[8,128,384]{1,2,0:T(8,128)(2,1)S(1)}, u32[]{:S(2)}, u32[]{:S(2)}) %all-to-all-start) | async-done | bytes 786464 | tf_op jit(solution)/shard_map/all_to_all | solution.py:191
  560.6 6.0 fusion.16
  567.8 95.1 %all-reduce.37.cloned.1.call-done = f32[21392]{0:T(1024)} async-done(((f32[21392]{0:T(1024)}), f32[21392]{0:T(1024)}) %all-reduce.37.cloned.1.call-update) | async-done | bytes 85584 | tf_op jit(solution)/shard_map/psum | solution.py:250
  671.3 96.4 %all-gather.21.cloned.1.call-done = bf16[3072,1030]{0,1:T(8,128)(2,1)} async-done(((bf16[384,1030]{0,1:T(8,128)(2,1)}), bf16[3072,1030]{0,1:T(8,128)(2,1)}) %all-gather.21.cloned.1.call-update) | async-done | bytes 6328336 | tf_op jit(solution)/shard_map/all_gather | solution.py:208
  767.7 9.0 %convert_element_type.81 = f32[3072,1030]{0,1:T(8,128)} convert(bf16[3072,1030]{0,1:T(8,128)(2,1)} %all-gather.21.cloned.1.call-done) | non-fusion elementwise | flops 3164160 | bytes 18984960 | tf_op jit(solution)/shard_map/convert_element_type | solution.py:208
  776.7 12.2 %copy.259 = f32[129,8,8,384]{3,2,1,0:T(8,128)} copy(f32[129,8,8,384]{3,1,2,0:T(8,128)} %bitcast.562) | data formatting | bytes 25362432
  789.0 5.2 slice_bitcast_fusion
  794.2 4.6 copy-done.2
  799.7 8.1 slice_bitcast_fusion.2
  807.8 6.1 copy.197
  813.9 5.7 copy.261
  819.6 6.1 copy.196
  825.7 5.5 copy.260
  831.9 8.4 pad_maximum_fusion
  840.3 9.8 %all-gather.15.cloned.1.call-done = bf16[3072,1536]{1,0:T(8,128)(2,1)} async-done(((bf16[96,1536]{1,0:T(8,128)(2,1)}), bf16[3072,1536]{1,0:T(8,128)(2,1)}) %all-gather.15.cloned.1.call-update) | async-done | bytes 9437200 | tf_op jit(solution)/shard_map/all_gather | solution.py:219
  850.1 4.5 dynamic-slice_convert_fusion
  (554 shorter events, 101.1 us)
Async XLA Ops:
  7.2 65.8 %all-gather.17.cloned.1.call-start = ((), (), s32[]{:S(2)}) async-start(), calls=%async_computation.10 | async-start | bytes 3538944 | tf_op jit(solution)/shard_map/all_gather | solution.py:152
  7.9 96.7 %all-gather.11.cloned.1.call-start = ((), (), s32[]{:S(2)}) async-start(), calls=%async_computation.4 | async-start | bytes 4423680 | tf_op jit(solution)/shard_map/all_gather | solution.py:124
  10.5 156.5 %all-gather.19.cloned.1.call-start = ((), (), s32[]{:S(2)}) async-start(), calls=%async_computation.11 | async-start | bytes 3538944 | tf_op jit(solution)/shard_map/all_gather | solution.py:153
  11.2 220.1 %all-gather.13.cloned.1.call-start = ((), (), s32[]{:S(2)}) async-start(), calls=%async_computation.5 | async-start | bytes 11796480 | tf_op jit(solution)/shard_map/all_gather | solution.py:154
  11.8 450.7 %reduce-scatter.6.cloned.1.call-start = ((), (), s32[]{:S(2)}) async-start(), calls=%async_computation.6 | async-start | bytes 3538944 | tf_op jit(solution)/shard_map/reduce_scatter | solution.py:203
  27.6 77.0 %copy-start.64 = (f32[1536]{0:T(1024)}, f32[1536]{0:T(1024)S(1)}, u32[]{:S(2)}) copy-start(f32[1536]{0:T(1024)S(1)} %mul.709) | copy-start | bytes 18436
  29.2 86.2 %copy-start.143 = (f32[6]{0:T(128)}, f32[6]{0:T(128)S(1)}, u32[]{:S(2)}) copy-start(f32[6]{0:T(128)S(1)} %dynamic_slice.59) | copy-start | bytes 76
  29.3 46.5 %copy-start.139 = (f32[48]{0:T(128)}, f32[48]{0:T(128)S(1)}, u32[]{:S(2)}) copy-start(f32[48]{0:T(128)S(1)} %reshape.513) | copy-start | bytes 580
  30.0 80.8 %copy-start.83 = (f32[640]{0:T(1024)}, f32[640]{0:T(1024)S(1)}, u32[]{:S(2)}) copy-start(f32[640]{0:T(1024)S(1)} %get-tuple-element.58) | copy-start | bytes 7684
  30.0 80.8 %copy-start.85 = (f32[640]{0:T(1024)}, f32[640]{0:T(1024)S(1)}, u32[]{:S(2)}) copy-start(f32[640]{0:T(1024)S(1)} %get-tuple-element.59) | copy-start | bytes 7684
  30.1 85.5 %copy-start.127 = (f32[6]{0:T(128)}, f32[6]{0:T(128)S(1)}, u32[]{:S(2)}) copy-start(f32[6]{0:T(128)S(1)} %fusion.310) | copy-start | bytes 76
  73.1 31.6 %copy-start.22 = (bf16[1,1024,1536]{2,1,0:T(8,128)(2,1)S(1)}, bf16[1,1024,1536]{2,1,0:T(8,128)(2,1)}, u32[]{:S(2)}) copy-start(bf16[1,1024,1536]{2,1,0:T(8,128)(2,1)} %all-gather.17.cloned.1.call-done) | copy-start | bytes 9437188
  75.8 34.7 %copy-start.128 = (f32[1024]{0:T(1024)}, f32[1024]{0:T(1024)S(1)}, u32[]{:S(2)}) copy-start(f32[1024]{0:T(1024)S(1)} %add_rsqrt_fusion) | copy-start | bytes 12292
  125.1 6.6 copy-start.100
  125.7 7.4 copy-start.95
  126.2 6.9 copy-start.90
  127.1 6.0 copy-start.55
  127.3 5.8 copy-start.24
  127.4 5.7 copy-start.7
  237.3 28.9 %copy-start.35 = (bf16[1024,384]{0,1:T(8,128)(2,1)}, bf16[1024,384]{0,1:T(8,128)(2,1)S(1)}, u32[]{:S(2)}) copy-start(bf16[1024,384]{0,1:T(8,128)(2,1)S(1)} %get-tuple-element.65) | copy-start | bytes 2359300
  267.4 9.9 %copy-start.15 = (f32[256,384]{0,1:T(8,128)}, f32[256,384]{0,1:T(8,128)S(1)}, u32[]{:S(2)}) copy-start(f32[256,384]{0,1:T(8,128)S(1)} %get-tuple-element.84) | copy-start | bytes 1179652
  267.4 13.9 %copy-start.14 = (f32[256,384]{0,1:T(8,128)}, f32[256,384]{0,1:T(8,128)S(1)}, u32[]{:S(2)}) copy-start(f32[256,384]{0,1:T(8,128)S(1)} %get-tuple-element.81) | copy-start | bytes 1179652
  283.9 7.8 copy-start.96
  283.9 8.0 copy-start.123
  284.0 7.9 copy-start.125
  294.5 6.9 copy-start.92
  294.5 6.9 copy-start.93
  294.5 6.9 copy-start.103
  294.6 6.8 copy-start.104
  294.6 6.8 copy-start.105
  294.6 6.8 copy-start.110
  294.6 6.8 copy-start.113
  294.6 35.5 %copy-start.94 = (f32[256,6]{0,1:T(8,128)S(1)}, f32[256,6]{0,1:T(8,128)}, u32[]{:S(2)}) copy-start(f32[256,6]{0,1:T(8,128)} %multiply_reduce_fusion.17) | copy-start | bytes 18436
  294.6 44.8 %copy-start.63 = (f32[1,6,2,128]{3,2,1,0:T(2,128)S(1)}, f32[1,6,2,128]{3,2,1,0:T(2,128)}, u32[]{:S(2)}) copy-start(f32[1,6,2,128]{3,2,1,0:T(2,128)} %copy-done.62) | copy-start | bytes 18436
  294.6 44.8 %copy-start.89 = (f32[256,6]{0,1:T(8,128)S(1)}, f32[256,6]{0,1:T(8,128)}, u32[]{:S(2)}) copy-start(f32[256,6]{0,1:T(8,128)} %multiply_reduce_fusion.19) | copy-start | bytes 18436
  373.8 8.0 copy-start.84
  373.8 8.0 copy-start.86
  391.8 113.3 %reduce-scatter.10.cloned.1.call-start = ((), (), s32[]{:S(2)}) async-start(), calls=%async_computation.13 | async-start | bytes 4423680
  402.4 5.6 copy-start.13
  402.4 130.9 %reduce-scatter.8.cloned.1.call-start = ((), (), s32[]{:S(2)}) async-start(), calls=%async_computation.8 | async-start | bytes 1474560 | tf_op jit(solution)/shard_map/reduce_scatter | solution.py:218
  407.9 255.0 %all-reduce.37.cloned.1.call-start = ((), (), s32[]{:S(2)}) async-start(), calls=%async_computation.7 | async-start | bytes 172032 | tf_op jit(solution)/shard_map/psum | solution.py:250
  463.8 69.5 %copy-start.21 = (bf16[48,8,8,128]{3,2,1,0:T(8,128)(2,1)S(1)}, bf16[48,8,8,128]{3,2,1,0:T(8,128)(2,1)}, u32[]{:S(2)}) copy-start(bf16[48,8,8,128]{3,2,1,0:T(8,128)(2,1)} %get-tuple-element.85) | copy-start | bytes 2359300
  464.5 303.2 %all-gather.21.cloned.1.call-start = ((), (), s32[]{:S(2)}) async-start(), calls=%async_computation.12 | async-start | bytes 7133184 | tf_op jit(solution)/shard_map/all_gather | solution.py:208
  507.3 342.8 %all-gather.15.cloned.1.call-start = ((), (), s32[]{:S(2)}) async-start(), calls=%async_computation.9 | async-start | bytes 9732096 | tf_op jit(solution)/shard_map/all_gather | solution.py:219
  534.4 26.2 %all-to-all-start = ((bf16[8,128,384]{1,2,0:T(8,128)(2,1)}), bf16[8,128,384]{1,2,0:T(8,128)(2,1)S(1)}, u32[]{:S(2)}, u32[]{:S(2)}) async-start(bf16[8,128,384]{1,2,0:T(8,128)(2,1)} %bitcast.553), calls=%async_computation | async-start | bytes 1572864 | tf_op jit(solution)/shard_map/all_to_all | solution.py:191
  560.5 6.0 copy-start.32
  560.6 6.0 copy-start.33
  825.7 5.5 slice-start
  (115 other events, 280.4 us)
Sparse Core Ops, SparseCore 0:
  10.2 62.8 all-gather.16
  75.2 29.3 all-gather.10
  106.8 60.0 all-gather.18
  168.3 62.8 all-gather.12
  391.9 70.5 reduce-scatter.5
  465.5 39.5 reduce-scatter.9
  507.6 25.6 reduce-scatter.7
  539.4 123.3 all-reduce.36
  665.5 102.1 all-gather.20
  770.5 79.6 all-gather.14

commit v2 on v1

v2 whole, which is shorter than its diff:
```python
from types import SimpleNamespace

import jax
import jax.numpy as jnp
from jax import lax
from jax.experimental import pallas as pl
from jax.experimental.pallas import tpu as pltpu
from jax.sharding import PartitionSpec as P

N = 128
HEAD = 64
Q = 128
epsilon = 1e-05
bf16 = jnp.bfloat16
f32 = jnp.float32
MESH = pl.DeviceIdType.MESH
HI = lax.Precision.HIGHEST
VMEM_LIMIT = 64 * 1024 * 1024 - 65536


def mm(a, b, da=1, db=0, precision=None):
    return lax.dot_general(
        a, b, (((da,), (db,)), ((), ())), preferred_element_type=f32, precision=precision
    )


def rcopy(src, dst, ss, rs, **dev):
    return pltpu.make_async_remote_copy(
        src_ref=src, dst_ref=dst, send_sem=ss, recv_sem=rs, device_id=dev, device_id_type=MESH
    )


class Place:
    def __init__(self, S, F):
        self.S, self.F = S, F
        self.Z = 4
        self.X = S // 4
        self.s = lax.axis_index("seq")
        self.f = lax.axis_index("fsdp")
        self.z = self.s // self.X
        self.x = lax.rem(self.s, self.X)

    def zz(self, k):
        return lax.rem(self.z + k + (k // 2) * (1 - 2 * (k % 2)), self.Z)

    def blk(self, k, q):
        return self.zz(k) * self.X + lax.rem(self.x + q, self.X)

    def barrier(self):
        bar = pltpu.get_barrier_semaphore()
        n = 0
        for k in range(1, self.S):
            pl.semaphore_signal(
                bar, inc=1, device_id={"seq": lax.rem(self.s + k, self.S)}, device_id_type=MESH
            )
            n += 1
        for k in range(1, self.F):
            pl.semaphore_signal(
                bar, inc=1, device_id={"fsdp": lax.rem(self.f + k, self.F)}, device_id_type=MESH
            )
            n += 1
        pl.semaphore_wait(bar, n)


class Gather:
    def __init__(self, pc, src, buf, ss, rs):
        self.pc, self.src, self.buf, self.ss, self.rs = pc, src, buf, ss, rs

    def start(self):
        pc = self.pc
        for k in range(1, pc.Z):
            rcopy(
                self.src, self.buf.at[pc.s], self.ss.at[k - 1], self.rs.at[pc.s],
                seq=pc.zz(k) * pc.X + pc.x,
            ).start()
        self.across(self.src, pc.s, 0)

    def across(self, src, b, k):
        pc = self.pc
        for q in range(1, pc.X):
            rcopy(
                src, self.buf.at[b], self.ss.at[pc.Z - 1 + k * (pc.X - 1) + q - 1], self.rs.at[b],
                seq=pc.z * pc.X + lax.rem(pc.x + q, pc.X),
            ).start()

    def wait(self, b):
        r = self.buf.at[b]
        rcopy(r, r, self.ss.at[0], self.rs.at[b], seq=self.pc.s).wait_recv()

    def drain(self):
        for i in range(self.pc.Z - 1 + self.pc.Z * (self.pc.X - 1)):
            rcopy(self.src, self.src, self.ss.at[i], self.rs.at[0], seq=self.pc.s).wait_send()


def gather_sems(S):
    Z, X = 4, S // 4
    return [pltpu.SemaphoreType.DMA((Z - 1 + Z * (X - 1),)), pltpu.SemaphoreType.DMA((S,))]


def pair(col, p):
    lane = lax.broadcasted_iota(jnp.int32, (col.shape[0], 128), 1)
    return jnp.where(lane < HEAD, col[:, 2 * p : 2 * p + 1], col[:, 2 * p + 1 : 2 * p + 2])


def spread(col, cp):
    return jnp.concatenate([pair(col, p) for p in range(cp // 128)], axis=1)


def sigmoid(v):
    return 1.0 / (1.0 + jnp.exp(-v))


def softplus(v):
    return jnp.maximum(v, 0.0) + jnp.log1p(jnp.exp(-jnp.abs(v)))


def tri(shape, flip=False):
    i = lax.broadcasted_iota(jnp.int32, shape, 0)
    j = lax.broadcasted_iota(jnp.int32, shape, 1)
    return j >= i if flip else i >= j


def split(x2):
    lane = lax.broadcasted_iota(jnp.int32, x2.shape, 1)
    return jnp.concatenate([jnp.where(lane < HEAD, x2, 0), jnp.where(lane >= HEAD, x2, 0)], axis=0)


def chunk_inputs(c, ext, rawb, small, cp):
    r0 = pl.multiple_of(c * Q, Q)
    v = ext[pl.ds(r0, Q + 16), :].astype(f32)
    C = cp + 2 * N
    taps = [pltpu.roll(v, 3 - k, 0)[16:] if k < 3 else v[16:] for k in range(4)]
    summed = small[4:5, :C]
    for k in range(4):
        summed = summed + small[k : k + 1, :C] * taps[k]
    sig = sigmoid(summed)
    raw = rawb[pl.ds(r0, Q), :].astype(f32) + small[7:8, 0:128]
    dt = softplus(raw)
    rate = -jnp.exp(small[7:8, 128:256])
    cum = mm(tri((Q, Q)).astype(f32), dt * rate, precision=HI)
    return taps, summed, sig, raw, dt, rate, cum


def skip_row(small, cp):
    return spread(small[7:8, 256:384], cp)


def body_fwd(cfg, tok, cot, wp, wo, sm, R):
    S, F, T, D, cp, WC = cfg
    L = S * T
    C = cp + 2 * N
    pc = Place(S, F)
    nh = cp // HEAD
    pc.barrier()
    tg = Gather(pc, tok, R.tok_all, R.ss_t, R.rs_t)
    cg = Gather(pc, cot, R.cot_all, R.ss_c, R.rs_c)
    ssw, rsw = R.ss_w, R.rs_w
    owner = pc.s // (S // F)
    tg.start()
    for k in range(1, F):
        to = lax.rem(pc.f + k, F)
        rcopy(sm, R.sm_all.at[pc.f], ssw.at[0, k], rsw.at[0, pc.f], fsdp=to).start()
        rcopy(wp, R.w_all.at[pc.f], ssw.at[1, k], rsw.at[1, pc.f], fsdp=to).start()

    @pl.when(pc.f == owner)
    def _():
        for k in range(1, F):
            to = lax.rem(pc.f + k, F)
            rcopy(wo, R.wo_g, ssw.at[2, k], rsw.at[2, 0], fsdp=to).start()
        pltpu.make_async_copy(wo, R.wo_g, R.wsem.at[1]).start()

    cg.start()
    R.tok_all[pc.s] = tok[...]
    R.cot_all[pc.s] = cot[...]
    pltpu.make_async_copy(wp, R.w_all.at[pc.f], R.wsem.at[0]).start()
    R.sm_all[pc.f] = sm[...]

    for i, (src, dst) in enumerate(((sm, R.sm_all), (wp, R.w_all))):
        for k in range(1, F):
            o = lax.rem(pc.f + k, F)
            rcopy(src, dst.at[o], ssw.at[i, 0], rsw.at[i, o], fsdp=pc.f).wait_recv()
        if i == 0:
            total = R.sm_all[0]
            for k in range(1, F):
                total = total + R.sm_all[k]
            R.small[...] = total
    pltpu.make_async_copy(wp, R.w_all.at[pc.f], R.wsem.at[0]).wait()
    small = R.small
    R.ext[0:16, :] = jnp.zeros((16, C), bf16)

    def project(j, carry):
        k, q = j // pc.X, lax.rem(j, pc.X)
        b = pc.blk(k, q)

        @pl.when(j > 0)
        def _():
            tg.wait(b)

        @pl.when(jnp.logical_and(q == 0, k > 0))
        def _():
            tg.across(R.tok_all.at[b], b, k)

        r = R.tok_all[b].astype(f32)
        scale = lax.rsqrt(jnp.mean(r * r, axis=1, keepdims=True) + epsilon)
        h = r * scale * small[6:7, :]
        r0 = pl.multiple_of(b * T, T)
        R.hid_t[:, pl.ds(r0, T)] = h.T.astype(bf16)
        out = mm(h.astype(bf16), R.w_all[...].reshape(D, WC)).astype(bf16)
        R.zb[pl.ds(r0, T), :] = out[:, :cp]
        R.rawb[pl.ds(r0, T), :] = out[:, 2 * cp + 2 * N :]
        R.ext[pl.ds(r0 + 16, T), :] = out[:, cp : 2 * cp + 2 * N]
        return carry

    lax.fori_loop(0, S, project, 0)
    R.state[...] = jnp.zeros((N, cp), f32)
    ones = jnp.ones((8, cp), f32)

    def forward(c, carry):
        @pl.when(c < pc.Z - 1)
        def _():
            b = pc.blk(c + 1, 0)
            cg.wait(b)
            cg.across(R.cot_all.at[b], b, c + 1)

        r0 = pl.multiple_of(c * Q, Q)
        taps, summed, sig, raw, dt, rate, cum = chunk_inputs(c, R.ext, R.rawb, small, cp)
        act = summed * sig
        x = act[:, :cp]
        bb = act[:, cp : cp + N].astype(bf16)
        cb = act[:, cp + N :].astype(bf16)
        cum_t = cum.T
        dt_t = dt.T
        scores = mm(cb, bb, 1, 1)
        causal = tri((Q, Q))
        parts = []
        for p in range(cp // 128):
            mix = []
            for h in (2 * p, 2 * p + 1):
                gap = jnp.where(causal, cum[:, h : h + 1] - cum_t[h : h + 1, :], -1e30)
                mix.append((jnp.exp(gap) * scores * dt_t[h : h + 1, :]).astype(bf16))
            parts.append(
                mm(jnp.concatenate(mix, axis=1), split(x[:, 128 * p : 128 * p + 128]).astype(bf16))
            )
        state = R.state[...]
        R.states[c] = state
        last = cum[Q - 1 : Q, :]
        y = jnp.concatenate(parts, axis=1) + mm(cb, state.astype(bf16)) * spread(jnp.exp(cum), cp)
        y = y + skip_row(small, cp) * x
        wx = (spread(jnp.exp(last - cum) * dt, cp) * x).astype(bf16)
        R.state[...] = spread(jnp.exp(last), cp) * state + mm(bb, wx, 0, 0)
        R.y[pl.ds(r0, Q), :] = y
        z = R.zb[pl.ds(r0, Q), :].astype(f32)
        gated = (y * (z * sigmoid(z))).astype(bf16)
        R.dpx[pl.ds(r0, Q), :cp] = gated
        g32 = gated.astype(f32)
        R.st[0:1, pl.ds(r0, Q)] = mm(ones, g32 * g32, 1, 1, HI)[0:1]
        return carry

    lax.fori_loop(0, L // Q, forward, 0)

    @pl.when(pc.f != owner)
    def _():
        rcopy(wo, R.wo_g, ssw.at[2, 0], rsw.at[2, 0], fsdp=pc.f).wait_recv()

    @pl.when(pc.f == owner)
    def _():
        pltpu.make_async_copy(wo, R.wo_g, R.wsem.at[1]).wait()

    def mixed(j, carry):
        k, q = j // pc.X, lax.rem(j, pc.X)
        b = pc.blk(k, q)

        @pl.when(q > 0)
        def _():
            cg.wait(b)

        r0 = pl.multiple_of(b * T, T)
        mg = mm(R.cot_all[b], R.wo_g[...], 1, 1)
        R.mg[pl.ds(r0, T), :] = mg
        g = mg * small[5:6, :cp] * R.dpx[pl.ds(r0, T), :cp].astype(f32)
        R.st[1:2, pl.ds(r0, T)] = mm(ones, g, 1, 1, HI)[0:1]
        return carry

    lax.fori_loop(0, S, mixed, 0)
    for k in range(1, S):
        rcopy(
            R.st, R.st_all.at[pc.s], R.ss_s.at[k], R.rs_s.at[pc.s],
            seq=lax.rem(pc.s + k, S),
        ).start()
    R.st_all[pc.s] = R.st[...]
    for k in range(1, S):
        o = lax.rem(pc.s + k, S)
        rcopy(R.st, R.st_all.at[o], R.ss_s.at[0], R.rs_s.at[o], seq=pc.s).wait_recv()
    total = R.st_all[0]
    for k in range(1, S):
        total = total + R.st_all[k]
    R.stats[...] = total

    tg.drain()
    cg.drain()
    for k in range(1, S):
        rcopy(R.st, R.st, R.ss_s.at[k], R.rs_s.at[0], seq=pc.s).wait_send()
    for k in range(1, F):
        rcopy(sm, sm, ssw.at[0, k], rsw.at[0, 0], fsdp=pc.f).wait_send()
        rcopy(wp, wp, ssw.at[1, k], rsw.at[1, 0], fsdp=pc.f).wait_send()

    @pl.when(pc.f == owner)
    def _():
        for k in range(1, F):
            rcopy(wo, wo, ssw.at[2, k], rsw.at[2, 0], fsdp=pc.f).wait_send()


def fwd_scratch(cfg):
    S, F, T, D, cp, WC = cfg
    L = S * T
    Dl = D // F
    C = cp + 2 * N
    V = pltpu.VMEM
    sem = pltpu.SemaphoreType.DMA
    n_ag = 3 + 4 * (S // 4 - 1)
    return SimpleNamespace(
        tok_all=V((S, T, D), bf16),
        cot_all=V((S, T, D), bf16),
        w_all=V((F, Dl, WC), bf16),
        wo_g=V((cp, D), bf16),
        sm_all=V((F, 8, D), f32),
        small=V((8, D), f32),
        hid_t=V((D, L), bf16),
        zb=V((L, cp), bf16),
        rawb=V((L, 128), bf16),
        ext=V((16 + L, C), bf16),
        state=V((N, cp), f32),
        states=V((L // Q, N, cp), f32),
        y=V((L, cp), f32),
        mg=V((L, cp), f32),
        st=V((2, L), f32),
        st_all=V((S, 2, L), f32),
        stats=V((2, L), f32),
        ss_t=sem((n_ag,)),
        rs_t=sem((S,)),
        ss_c=sem((n_ag,)),
        rs_c=sem((S,)),
        ss_w=sem((3, F)),
        rs_w=sem((3, F)),
        wsem=sem((2,)),
        ss_s=sem((S,)),
        rs_s=sem((S,)),
    )


def prep(cfg, in_weight, step_weight, conv_kernel, conv_bias, step_bias, log_decay, skip_gain,
         gate_gain, norm_gain, out_weight):
    S, F, T, D, cp, WC = cfg
    s = lax.axis_index("seq")
    f = lax.axis_index("fsdp")
    heads = step_weight.shape[1]
    hg = heads // S
    inner = out_weight.shape[0] * F
    cols = inner // S
    col = s * cols

    def sl(a, start, size, axis):
        return lax.dynamic_slice_in_dim(a, start, size, axis)

    def padc(a, to):
        return jnp.pad(a, [(0, 0)] * (a.ndim - 1) + [(0, to - a.shape[-1])])

    wp = jnp.concatenate(
        [
            padc(sl(in_weight, col, cols, 1), cp),
            padc(sl(in_weight, inner + col, cols, 1), cp),
            in_weight[:, 2 * inner :],
            padc(sl(step_weight, s * hg, hg, 1), 128),
        ],
        axis=1,
    )
    per = out_weight.shape[0] // cols
    wo = jnp.pad(sl(out_weight, lax.rem(s, per) * cols, cols, 0), [(0, cp - cols), (0, 0)])

    def window(a, start, size, out):
        n = a.shape[-1]
        pad = jnp.pad(a, [(0, 0)] * (a.ndim - 1) + [(size, size)])
        return padc(sl(pad, jnp.clip(start - n * f + size, 0, n + size), size, a.ndim - 1), out)

    def conv_rows(a):
        return jnp.concatenate(
            [window(a, col, cols, cp), window(a, inner, 2 * N, 2 * N)], axis=-1
        )

    def row(a):
        return padc(a.astype(f32), D).reshape(-1, D)

    def head(a):
        return window(a[None], s * hg, hg, 128)

    sm = jnp.concatenate(
        [
            row(conv_rows(conv_kernel)),
            row(conv_rows(conv_bias[None])),
            row(window(gate_gain[None], col, cols, cp)),
            row(window(norm_gain[None], 0, D, D)),
            row(jnp.concatenate([head(step_bias), head(log_decay), head(skip_gain)], axis=-1)),
        ],
        axis=0,
    )
    return wp, wo, sm


class Scatter:
    def __init__(self, pc, part, rx, rz, sems):
        self.pc, self.part, self.rx, self.rz = pc, part, rx, rz
        self.ssx, self.rsx, self.ssz, self.rsz = sems

    def across(self, b):
        pc = self.pc
        zb, xb = b // pc.X, lax.rem(b, pc.X)

        @pl.when(xb != pc.x)
        def _():
            slot = lax.rem(pc.x - xb - 1 + pc.X, pc.X)
            rcopy(
                self.part.at[b], self.rx.at[zb, slot], self.ssx.at[b], self.rsx.at[zb, slot],
                seq=pc.z * pc.X + xb,
            ).start()

    def column(self, zb):
        pc = self.pc
        b = zb * pc.X + pc.x
        total = self.part[b].astype(f32)
        for q in range(pc.X - 1):
            r = self.rx.at[zb, q]
            rcopy(r, r, self.ssx.at[0], self.rsx.at[zb, q], seq=pc.s).wait_recv()
            total = total + self.rx[zb, q].astype(f32)
        self.part[b] = total.astype(bf16)

        @pl.when(zb != pc.z)
        def _():
            slot = lax.rem(pc.z - zb - 1 + pc.Z, pc.Z)
            rcopy(
                self.part.at[b], self.rz.at[slot], self.ssz.at[zb], self.rsz.at[slot], seq=b
            ).start()

    def total(self):
        pc = self.pc
        out = self.part[pc.s].astype(f32)
        for q in range(pc.Z - 1):
            r = self.rz.at[q]
            rcopy(r, r, self.ssz.at[0], self.rsz.at[q], seq=pc.s).wait_recv()
            out = out + self.rz[q].astype(f32)
        return out

    def drain(self):
        pc = self.pc
        r = self.rz.at[0]
        for b in range(pc.S):

            @pl.when(b % pc.X != pc.x)
            def _():
                rcopy(r, r, self.ssx.at[b], self.rsz.at[0], seq=pc.s).wait_send()

        for zb in range(pc.Z):

            @pl.when(zb != pc.z)
            def _():
                rcopy(r, r, self.ssz.at[zb], self.rsz.at[0], seq=pc.s).wait_send()


class Shared:
    def __init__(self, pc, part, recv, ss, rs):
        self.pc, self.part, self.recv, self.ss, self.rs = pc, part, recv, ss, rs

    def send(self, k):
        pc = self.pc
        to = lax.rem(pc.f + k, pc.F)
        rcopy(
            self.part.at[to], self.recv.at[k - 1], self.ss.at[k - 1], self.rs.at[k - 1], fsdp=to
        ).start()

    def total(self):
        pc = self.pc
        out = self.part[pc.f].astype(f32)
        for k in range(1, pc.F):
            r = self.recv.at[k - 1]
            rcopy(r, r, self.ss.at[k - 1], self.rs.at[k - 1], fsdp=pc.f).wait_recv()
            out = out + self.recv[k - 1].astype(f32)
        return out

    def drain(self):
        for k in range(1, self.pc.F):
            r = self.recv.at[k - 1]
            rcopy(r, r, self.ss.at[k - 1], self.rs.at[k - 1], fsdp=self.pc.f).wait_send()


def body_bwd(cfg, inner, tok, cot, R, O):
    S, F, T, D, cp, WC = cfg
    L = S * T
    C = cp + 2 * N
    Dl = D // F
    nc = L // Q
    cr = cp // F
    per = S // F
    pc = Place(S, F)
    small = R.small
    blk = Scatter(pc, R.bp, R.brx, R.brz, (R.bs0, R.bs1, R.bs2, R.bs3))
    hid = Scatter(pc, R.tok_all, R.hrx, R.hrz, (R.hs0, R.hs1, R.hs2, R.hs3))
    zs = Shared(pc, R.zp, R.zr, R.zs0, R.zs1)
    os_ = Shared(pc, R.op, R.orecv, R.os0, R.os1)
    xs = Shared(pc, R.xp, R.xr, R.xs0, R.xs1)
    zg = Gather(pc, R.zred, O.gz, R.gz0, R.gz1)
    og = Gather(pc, R.ored, O.go_s, R.go0, R.go1)
    xg = Gather(pc, R.xred, O.gx, R.gx0, R.gx1)

    def own(src, dst, i):
        return pltpu.make_async_copy(src, dst, R.lsem.at[i])

    gate = small[5:6, :cp]
    R.acc[...] = jnp.zeros((8, D), f32)
    R.hacc[...] = jnp.zeros((2, 8, 128), f32)
    R.dstate[...] = jnp.zeros((N, cp), f32)
    R.head[...] = jnp.zeros((8, C), f32)

    def first(i, carry):
        c = nc - 1 - i
        r0 = pl.multiple_of(c * Q, Q)
        rows = pl.ds(r0, Q)
        st = jnp.concatenate([R.stats[:, rows], jnp.zeros((6, Q), f32)], axis=0).T
        scale = lax.rsqrt(st[:, 0:1] / inner + epsilon)
        mean = st[:, 1:2] / inner
        gated = R.dpx[rows, :cp].astype(f32)
        mg = R.mg[rows, :]
        ng = gated * scale
        mn = ng * gate
        R.acc[5:6, :cp] += jnp.sum(mg * ng, axis=0, keepdims=True)
        gg = (scale * (mg * gate) - scale * scale * scale * gated * mean).astype(bf16).astype(f32)
        z = R.zb[rows, :].astype(f32)
        sz = sigmoid(z)
        R.zb[rows, :] = (gg * R.y[rows, :] * (sz * (1.0 + z * (1.0 - sz)))).astype(bf16)
        R.mg[rows, :] = gg * (z * sz)
        R.mn_t[:, rows] = mn.T.astype(bf16)
        R.dpx[rows, :cp] = mn.astype(bf16)
        return carry

    def block(i, carry):
        c = nc - 1 - i
        rows = pl.ds(pl.multiple_of(c * Q, Q), Q)
        R.bp[c] = mm(R.dpx[rows, :cp], R.wo_g[...]).astype(bf16)
        blk.across(c)
        return carry

    lax.fori_loop(0, nc, first, 0)
    if not tight(cfg):
        lax.fori_loop(0, nc, block, 0)

    def zpart(k, carry):
        to = lax.rem(pc.f + k, F)
        rows = pl.ds(pl.multiple_of(to * Dl, Dl), Dl)
        R.zp[to] = mm(R.hid_t[rows, :], R.zb[...]).astype(bf16)

        @pl.when(k < F)
        def _():
            rcopy(
                R.zp.at[to], R.zr.at[k - 1], R.zs0.at[k - 1], R.zs1.at[k - 1], fsdp=to
            ).start()
        return carry

    lax.fori_loop(1, F + 1, zpart, 0)
    W = 384

    def opart(j, carry):
        cols = pl.ds(pl.multiple_of(j * W, W), W)
        a = R.cot_all[:, :, cols].reshape(L, W)
        R.op[:, :, cols] = mm(R.mn_t[...], a).reshape(F, cr, W).astype(bf16)
        return carry

    lax.fori_loop(0, D // W, opart, 0)
    for k in range(1, F):
        os_.send(k)
    if tight(cfg):
        lax.fori_loop(0, nc, block, 0)

    sel = (
        lax.broadcasted_iota(jnp.int32, (8, cp), 1) // HEAD
        == lax.broadcasted_iota(jnp.int32, (8, cp), 0)
    ).astype(f32)
    sub = lax.broadcasted_iota(jnp.int32, (8, Q), 0)

    def scan(i, carry):
        c = nc - 1 - i
        r0 = pl.multiple_of(c * Q, Q)
        rows = pl.ds(r0, Q)

        @pl.when(i < pc.Z)
        def _():
            blk.column(pc.Z - 1 - i)

        @pl.when(i == 2)
        def _():
            R.zred[...] = zs.total().astype(bf16)
            zg.start()
            own(R.zred, O.gz.at[pc.s], 0).start()

        @pl.when(i == 3)
        def _():
            R.ored[...] = os_.total().astype(bf16)
            og.start()
            own(R.ored, O.go_s.at[pc.s], 4).start()

        @pl.when(jnp.logical_and(i >= 5, i < 5 + pc.Z - 1))
        def _():
            k = i - 4
            b = pc.blk(k, 0)
            zg.wait(b)
            zg.across(O.gz.at[b], b, k)
            og.wait(b)
            og.across(O.go_s.at[b], b, k)

        taps, summed, sig, raw, dt, rate, cum = chunk_inputs(c, R.ext, R.rawb, small, cp)
        act = summed * sig
        x = act[:, :cp]
        xb = x.astype(bf16)
        bb = act[:, cp : cp + N].astype(bf16)
        cb = act[:, cp + N :].astype(bf16)
        cum_t = cum.T
        dt_t = dt.T
        dy = R.mg[rows, :]
        dyb = dy.astype(bf16)
        last = cum[Q - 1 : Q, :]
        edy = spread(jnp.exp(cum), cp) * dy
        edyb = edy.astype(bf16)
        wdec = jnp.exp(last - cum)
        w = wdec * dt
        state = R.states[c]
        sb = state.astype(bf16)
        ds = R.dstate[...]
        dsb = ds.astype(bf16)
        ws = spread(w, cp)
        v = mm(bb, dsb)
        carr = mm(sel, edy * mm(cb, sb), 1, 1, HI)
        dw = mm(sel, x * v, 1, 1, HI)
        db = mm((ws * x).astype(bf16), dsb, 1, 1)
        dc = mm(edyb, sb, 1, 1)
        dlast = mm(sel, jnp.sum(state * ds, axis=0, keepdims=True), 1, 1, HI)
        R.dstate[...] = spread(jnp.exp(last), cp) * ds + mm(cb, edyb, 0, 0)
        scores = mm(bb, cb, 1, 1)
        seen = tri((Q, Q), True)
        dtb = dt_t[0:8].astype(bf16)
        dsc = jnp.zeros((Q, Q), f32)
        direct = jnp.zeros((8, Q), f32)
        onto = jnp.zeros((8, Q), f32)
        parts = []
        for p in range(cp // 128):
            cols = slice(128 * p, 128 * p + 128)
            g2 = mm(split(x[:, cols]).astype(bf16), dyb[:, cols], 1, 1)
            mix = []
            for h in (2 * p, 2 * p + 1):
                g = g2[:Q] if h % 2 == 0 else g2[Q:]
                decay = jnp.exp(jnp.where(seen, cum_t[h : h + 1, :] - cum[:, h : h + 1], -1e30))
                ls = decay * scores
                mix.append((ls * dt[:, h : h + 1]).astype(bf16))
                e = (g * ls).astype(bf16)
                dsc = dsc + g * decay * dt[:, h : h + 1]
                direct = direct + mm(jnp.where(sub == h, 1.0, 0.0).astype(bf16), e, 1, 1)
                onto = onto + mm(jnp.where(sub == h, dtb.astype(f32), 0.0).astype(bf16), e)
            parts.append(mm(jnp.concatenate(mix, axis=1), split(dy[:, cols]).astype(bf16)))
        dscb = dsc.astype(bf16)
        db = db + mm(dscb, cb)
        dc = dc + mm(dscb, bb, 0, 0)
        dx = skip_row(small, cp) * dy + ws * v + jnp.concatenate(parts, axis=1)
        R.acc[7:8, :cp] += jnp.sum(dy * x, axis=0, keepdims=True)
        dt_r = dt_t[0:8]
        wdec_r = wdec.T[0:8]
        w_r = wdec_r * dt_r
        rate_r = jnp.broadcast_to(rate, (128, 128)).T[0:8, 0:1]
        last_r = jnp.exp(cum_t[0:8, Q - 1 : Q])
        dcum = carr + onto - dtb.astype(f32) * direct - w_r * dw
        end = jnp.sum(w_r * dw, axis=1, keepdims=True) + last_r * dlast
        da = mm(dcum, tri((Q, Q)).astype(f32), precision=HI) + end
        ddt = direct + wdec_r * dw + rate_r * da
        draw = ddt * sigmoid(raw).T[0:8]
        R.hacc[0] += draw
        R.hacc[1] += da * dt_r * rate_r
        dact = jnp.concatenate([dx, db, dc], axis=1)
        dsum = dact * (sig * (1.0 + summed * (1.0 - sig)))
        full = jnp.concatenate([dsum, R.head[...]], axis=0)
        dxbc = jnp.zeros((Q, C), f32)
        for k in range(4):
            R.acc[k : k + 1, :C] += jnp.sum(dsum * taps[k], axis=0, keepdims=True)
            moved = pltpu.roll(full, Q + 8 - (3 - k), 0)[:Q] if k < 3 else dsum
            dxbc = dxbc + small[k : k + 1, :C] * moved
        R.acc[4:5, :C] += jnp.sum(dsum, axis=0, keepdims=True)
        R.head[...] = dsum[:8]
        R.dpx[rows, :C] = dxbc.astype(bf16)
        pad = jnp.concatenate([draw, jnp.zeros((120, Q), f32)], axis=0).T
        R.dpx[rows, C:] = pad.astype(bf16)
        grad = jnp.concatenate([R.zb[rows, :], R.dpx[rows, :]], axis=1)
        hp = mm(grad, R.w_all[...].reshape(D, WC), 1, 1)
        r = R.tok_all[c].astype(f32)
        scale = lax.rsqrt(jnp.mean(r * r, axis=1, keepdims=True) + epsilon)
        R.acc[6:7, :] += jnp.sum(hp * r * scale, axis=0, keepdims=True)
        R.tok_all[c] = hp.astype(bf16)
        hid.across(c)
        return carry

    lax.fori_loop(0, nc, scan, 0)

    def xpart(k, carry):
        to = lax.rem(pc.f + k, F)
        rows = pl.ds(pl.multiple_of(to * Dl, Dl), Dl)
        R.xp[to] = mm(R.hid_t[rows, :], R.dpx[...]).astype(bf16)

        @pl.when(k < F)
        def _():
            rcopy(
                R.xp.at[to], R.xr.at[k - 1], R.xs0.at[k - 1], R.xs1.at[k - 1], fsdp=to
            ).start()
        return carry

    lax.fori_loop(1, F + 1, xpart, 0)
    diag = lax.broadcasted_iota(jnp.int32, (8, 128), 0) == lax.broadcasted_iota(
        jnp.int32, (8, 128), 1
    )

    def along(v):
        return jnp.sum(jnp.where(diag, jnp.sum(v, axis=1, keepdims=True), 0.0), axis=0, keepdims=True)

    dskip = jnp.sum(
        jnp.where(diag, mm(sel, R.acc[7:8, :cp], 1, 1, HI), 0.0), axis=0, keepdims=True
    )
    R.acc[7:8, :] = jnp.concatenate(
        [along(R.hacc[0]), along(R.hacc[1]), dskip, jnp.zeros((1, D - 384), f32)], axis=1
    )
    for k in range(1, F):
        to = lax.rem(pc.f + k, F)
        rcopy(
            R.acc, R.ar.at[k - 1], R.as0.at[k - 1], R.as1.at[k - 1], fsdp=to
        ).start()

    def hid_column(i, carry):
        hid.column(pc.Z - 1 - i)
        return carry

    lax.fori_loop(0, pc.Z, hid_column, 0)
    total = R.acc[...]
    for k in range(1, F):
        r = R.ar.at[k - 1]
        rcopy(r, r, R.as0.at[k - 1], R.as1.at[k - 1], fsdp=pc.f).wait_recv()
        total = total + R.ar[k - 1]
    R.asum[...] = total
    for k in range(1, S):
        rcopy(
            R.asum, O.sm.at[pc.s], R.as2.at[k], R.as3.at[pc.s], seq=lax.rem(pc.s + k, S)
        ).start()
    own(R.asum, O.sm.at[pc.s], 1).start()
    R.xred[...] = xs.total().astype(bf16)
    xg.start()
    own(R.xred, O.gx.at[pc.s], 2).start()

    mine = tok[...].astype(f32)
    O.block[...] = (mine + blk.total()).astype(bf16)
    for k in range(pc.Z):
        for q in range(1, pc.X):
            og.wait(pc.blk(k, q))
    own(R.ored, O.go_s.at[pc.s], 4).wait()
    for k in range(1, F):
        to = lax.rem(pc.f + k, F)
        rcopy(
            O.go_s.at[pl.ds(to * per, per)], O.go.at[pc.f], R.gs0.at[k], R.gs1.at[pc.f],
            fsdp=to,
        ).start()
    own(O.go_s.at[pl.ds(pc.f * per, per)], O.go.at[pc.f], 3).start()
    scale = lax.rsqrt(jnp.mean(mine * mine, axis=1, keepdims=True) + epsilon)
    e = hid.total() * small[6:7, :]
    mean = jnp.mean(e * mine, axis=1, keepdims=True)
    O.input[...] = cot[...].astype(f32) + scale * e - scale * scale * scale * mine * mean

    for k in range(1, pc.Z):
        b = pc.blk(k, 0)
        xg.wait(b)
        xg.across(O.gx.at[b], b, k)
    for k in range(pc.Z):
        for q in range(1, pc.X):
            zg.wait(pc.blk(k, q))
    for k in range(1, F):
        o = lax.rem(pc.f + k, F)
        r = O.go.at[o]
        rcopy(r, r, R.gs0.at[0], R.gs1.at[o], fsdp=pc.f).wait_recv()
    for k in range(1, S):
        o = lax.rem(pc.s + k, S)
        r = O.sm.at[o]
        rcopy(r, r, R.as2.at[0], R.as3.at[o], seq=pc.s).wait_recv()
    for k in range(pc.Z):
        for q in range(1, pc.X):
            xg.wait(pc.blk(k, q))
    own(R.zred, O.gz.at[pc.s], 0).wait()
    own(R.asum, O.sm.at[pc.s], 1).wait()
    own(R.xred, O.gx.at[pc.s], 2).wait()
    own(O.go_s.at[pl.ds(pc.f * per, per)], O.go.at[pc.f], 3).wait()
    for a in (blk, hid, zs, os_, xs, zg, og, xg):
        a.drain()
    for k in range(1, F):
        r = R.ar.at[k - 1]
        rcopy(r, r, R.as0.at[k - 1], R.as1.at[0], fsdp=pc.f).wait_send()
        r = O.go.at[0]
        rcopy(r, r, R.gs0.at[k], R.gs1.at[0], fsdp=pc.f).wait_send()
    for k in range(1, S):
        rcopy(R.asum, R.asum, R.as2.at[k], R.as3.at[0], seq=pc.s).wait_send()


def tight(cfg):
    S, F, T, D, cp, WC = cfg
    return S * T * D * 2 > 2**22


def bwd_scratch(cfg):
    S, F, T, D, cp, WC = cfg
    L = S * T
    Dl = D // F
    C = cp + 2 * N
    Z, X = 4, S // 4
    WX = WC - cp
    cr = cp // F
    V = pltpu.VMEM
    sem = pltpu.SemaphoreType.DMA
    n_ag = Z - 1 + Z * (X - 1)
    out = SimpleNamespace(
        acc=V((8, D), f32),
        asum=V((8, D), f32),
        ar=V((F - 1, 8, D), f32),
        hacc=V((2, 8, 128), f32),
        dstate=V((N, cp), f32),
        head=V((8, C), f32),
        mn_t=V((cp, L), bf16),
        dpx=V((L, WX), bf16),
        brx=V((Z, X - 1, T, D), bf16),
        brz=V((Z - 1, T, D), bf16),
        hrx=V((Z, X - 1, T, D), bf16),
        hrz=V((Z - 1, T, D), bf16),
        zp=V((F, Dl, cp), bf16),
        zr=V((F - 1, Dl, cp), bf16),
        zred=V((Dl, cp), bf16),
        op=V((F, cr, D), bf16),
        orecv=V((F - 1, cr, D), bf16),
        ored=V((cr, D), bf16),
        xp=V((F, Dl, WX), bf16),
        xr=V((F - 1, Dl, WX), bf16),
        xred=V((Dl, WX), bf16),
        lsem=sem((5,)),
        as0=sem((F,)), as1=sem((F,)), as2=sem((S,)), as3=sem((S,)),
        gs0=sem((F,)), gs1=sem((F,)),
    )
    if not tight(cfg):
        out.bp = V((S, T, D), bf16)

    def both():
        return sem((S,)), sem((Z, X - 1)), sem((Z,)), sem((Z - 1,))

    out.bs0, out.bs1, out.bs2, out.bs3 = both()
    out.hs0, out.hs1, out.hs2, out.hs3 = both()
    out.zs0, out.zs1, out.gz0, out.gz1 = sem((F,)), sem((F,)), sem((n_ag,)), sem((S,))
    out.os0, out.os1, out.go0, out.go1 = sem((F,)), sem((F,)), sem((n_ag,)), sem((S,))
    out.xs0, out.xs1, out.gx0, out.gx1 = sem((F,)), sem((F,)), sem((n_ag,)), sem((S,))
    return out


def shards(tokens, in_weight, step_weight, conv_kernel, conv_bias, step_bias, log_decay,
           skip_gain, gate_gain, norm_gain, out_weight, cotangent):
    S = lax.axis_size("seq")
    F = lax.axis_size("fsdp")
    _, T, D = tokens.shape
    inner = out_weight.shape[0] * F
    heads = step_weight.shape[1]
    cols = inner // S
    cp = -(-cols // 128) * 128
    C = cp + 2 * N
    WC = 2 * cp + 2 * N + 128
    WX = WC - cp
    Dl = D // F
    cr = cp // F
    per = S // F
    cfg = (S, F, T, D, cp, WC)
    wp, wo, sm = prep(cfg, in_weight, step_weight, conv_kernel, conv_bias, step_bias, log_decay,
                      skip_gain, gate_gain, norm_gain, out_weight)
    scratch = {**vars(fwd_scratch(cfg)), **vars(bwd_scratch(cfg))}
    names = list(scratch)
    outs = dict(
        block=jax.ShapeDtypeStruct((T, D), bf16),
        input=jax.ShapeDtypeStruct((T, D), f32),
        gz=jax.ShapeDtypeStruct((S, Dl, cp), bf16),
        gx=jax.ShapeDtypeStruct((S, Dl, WX), bf16),
        go=jax.ShapeDtypeStruct((F, per, cr, D), bf16),
        go_s=jax.ShapeDtypeStruct((S, cr, D), bf16),
        sm=jax.ShapeDtypeStruct((S, 8, D), f32),
    )
    on = list(outs)

    def kern(tok, cot, wp, wo, sm, *rest):
        O = SimpleNamespace(**dict(zip(on, rest[: len(on)])))
        R = SimpleNamespace(**dict(zip(names, rest[len(on) :])))
        if tight(cfg):
            R.bp = R.cot_all
        body_fwd(cfg, tok, cot, wp, wo, sm, R)
        body_bwd(cfg, float(inner), tok, cot, R, O)

    v = pl.BlockSpec(memory_space=pltpu.VMEM)
    hbm = pl.BlockSpec(memory_space=pl.ANY)
    res = pl.pallas_call(
        kern,
        out_shape=[outs[n] for n in on],
        in_specs=[v, v, hbm, hbm, v],
        out_specs=[v, v, hbm, hbm, hbm, hbm, hbm],
        scratch_shapes=[scratch[n] for n in names],
        compiler_params=pltpu.CompilerParams(
            collective_id=0, has_side_effects=True, vmem_limit_bytes=VMEM_LIMIT
        ),
    )(tokens[0], cotangent[0], wp, wo, sm)
    G = SimpleNamespace(**dict(zip(on, res)))
    gz, gx, go, gs = G.gz, G.gx, G.go, G.sm
    fpos = lax.axis_index("fsdp")

    def join(a, n):
        return jnp.moveaxis(a[..., :n], 0, -2).reshape(a.shape[1:-1] + (-1,))

    hg = heads // S
    in_grad = jnp.concatenate(
        [
            join(gz, cols),
            join(gx, cols),
            jnp.sum(gx[:, :, cp:C].astype(f32), axis=0).astype(bf16),
        ],
        axis=1,
    ).astype(f32)
    step_grad = join(gx[:, :, C:], hg).astype(f32)
    out_grad = (
        jnp.moveaxis(go, 0, 1).reshape(per, cp, D)[:, :cols].reshape(per * cols, D).astype(f32)
    )

    def mine(a, axis):
        n = a.shape[axis] // F
        return lax.dynamic_slice_in_dim(a, fpos * n, n, axis)

    conv = jnp.concatenate(
        [join(gs[:, 0:5], cols), jnp.sum(gs[:, 0:5, cp:C], axis=0)], axis=1
    )
    conv = mine(conv, 1)
    return (
        G.block[None],
        G.input[None],
        in_grad,
        step_grad,
        conv[0:4],
        conv[4],
        mine(join(gs[:, 7], hg), 0),
        mine(join(gs[:, 7, 128:], hg), 0),
        mine(join(gs[:, 7, 256:], hg), 0),
        mine(join(gs[:, 5], cols), 0),
        mine(jnp.sum(gs[:, 6], axis=0), 0),
        out_grad,
    )


def solution(mesh):
    row = P("fsdp", None)
    tok = P("fsdp", "seq", None)
    one = P("fsdp")
    return jax.shard_map(
        shards,
        mesh=mesh,
        in_specs=(tok, row, row, P(None, "fsdp"), one, one, one, one, one, one, row, tok),
        out_specs=(tok, tok, row, row, P(None, "fsdp"), one, one, one, one, one, one, row),
        check_vma=False,
    )
```

time: 870 us -> 399 us (0.46)
  the two profiles are of different devices: /device:TPU:0 before, /device:TPU:14 now
where the time goes in v2:
time: 399 us; the launch traced here: 398 us
  Pallas kernels  339 us (85%)
  local copies, waits for them, and re-layouts  43.7 us (11%)
  other arithmetic  13.8 us (3%)
    pallas_call x1, Pallas kernels, shards(): pl.pallas_call(kern, out_shape=[outs[n] for n in on], in_specs=[v, v, hbm...  339 us
    unnamed x16, local copies, waits for them, and re-layouts  12.4 us
    transpose x3, local copies, waits for them, and re-layouts, join(): return jnp.moveaxis(a[..., :n], 0, -2).reshape(a.shape[1:-1] + (-1,))  10.6 us

profile of v2, /device:TPU:14, one launch (start us, length us, event | category | flops | bytes accessed | tf_op | source)
XLA Modules:
  0.0 397.7 jit_solution(10967017219899759145)
XLA Ops:
  0.7 0.9 constant_dynamic-slice_fusion.2
  1.6 0.7 constant_dynamic-slice_fusion
  2.3 0.7 broadcast_in_dim.26
  3.0 0.8 pad_dynamic-slice_fusion.4
  3.8 0.7 broadcast_in_dim.25
  4.5 0.1 pad_dynamic-slice_fusion.6
  4.6 0.8 pad_dynamic-slice_fusion.3
  5.3 0.7 broadcast_in_dim.24
  6.0 0.1 pad_dynamic-slice_fusion.7
  6.1 0.1 pad_dynamic-slice_fusion.5
  6.2 0.7 constant_dynamic-slice_fusion.4
  6.9 0.1 pad_dynamic-slice_fusion.2
  7.1 0.6 concatenate.44.sm
  7.7 0.2 copy.42
  7.9 0.9 slice.55
  8.9 1.1 constant_dynamic-slice_fusion.6
  10.0 1.0 fusion.1.wp
  11.0 1.1 constant_dynamic-slice_fusion.3.wo
  12.1 339.4 %shard_map.211 = (bf16[128,1536]{1,0:T(8,128)(2,1)}, f32[128,1536]{1,0:T(8,128)}, bf16[8,384,384]{2,1,0:T(8,128)(2,1)}, bf16[8,384,768]{2,1,0:T(8,128)(2,1)}, bf...) custom-call(bf16[128,1536]{1,0:T(8,128)(2,1)} %bitcast.41, ...), custom_call_target="tpu_custom_call" | custom-call | tf_op jit(solution)/shard_map/pallas_call | solution.py:906
  351.4 0.9 slice_reduce_fusion.1
  352.3 1.0 slice.67
  353.4 0.6 dynamic_slice.73
  354.0 1.0 slice.65
  355.0 0.1 reshape.122
  355.1 0.6 dynamic_slice.72
  355.7 0.9 slice.59
  356.6 1.5 slice_reduce_fusion.2
  358.1 0.7 dynamic_slice.75
  358.8 0.1 fusion.2
  358.9 0.6 slice_reduce_fusion.3
  359.5 0.6 slice.72
  360.1 0.7 dynamic_slice.74
  360.8 0.1 reshape.121
  360.9 0.6 dynamic_slice.71
  361.5 1.6 slice_reduce_fusion
  363.1 0.2 copy.34
  363.2 1.2 convert_bitcast_fusion.1
  364.5 3.3 slice_bitcast_fusion
  367.8 0.5 copy.35
  368.3 0.7 reshape.125
  368.9 3.0 copy.33
  371.9 4.3 %copy.32 = bf16[384,8,384]{0,2,1:T(8,128)(2,1)} copy(bf16[384,8,384]{2,0,1:T(8,128)(2,1)} %bitcast.37) | data formatting | bytes 4718592 | tf_op jit(solution)/shard_map/transpose | solution.py:921
  376.2 2.3 convert_bitcast_fusion
  378.5 2.5 copy.36
  381.1 4.4 %maximum_convert_fusion = f32[384,6400]{0,1:T(8,128)} fusion(bf16[384,256]{0,1:T(8,128)(2,1)S(1)} %copy.34, bf16[384,3072]{0,1:T(8,128)(2,1)S(1)} %bitcast.34, bf16[384,3072]{0,1:T(8,128)(2,1)S(1)} %bitcast.35), kind=kLoop, calls=%fused_computation | loop fusion | flops 14745600 | bytes 14745600 | tf_op jit(solution)/shard_map/convert_element_type | solution.py:931
  385.5 10.5 %copy.37 = f32[384,6400]{1,0:T(8,128)} copy(f32[384,6400]{0,1:T(8,128)} %maximum_convert_fusion) | data formatting | bytes 19660800
  396.0 0.7 copy.53
  396.8 0.9 copy.54
  (23 shorter events, 0.3 us)
Async XLA Ops:
  0.6 10.3 %copy-start.2 = (bf16[768,1536]{1,0:T(8,128)(2,1)S(1)}, bf16[768,1536]{1,0:T(8,128)(2,1)}, u32[]{:S(2)}) copy-start(bf16[768,1536]{1,0:T(8,128)(2,1)} %param.22) | copy-start | bytes 7077892
  378.5 2.6 copy-start
  385.5 10.5 %copy-start.3 = (bf16[128,1536]{1,0:T(8,128)(2,1)S(1)}, bf16[128,1536]{1,0:T(8,128)(2,1)}, u32[]{:S(2)}) copy-start(bf16[128,1536]{1,0:T(8,128)(2,1)} %get-tuple-element.18) | copy-start | bytes 1179652
  385.5 11.3 %copy-start.1 = (f32[128,1536]{1,0:T(8,128)S(1)}, f32[128,1536]{1,0:T(8,128)}, u32[]{:S(2)}) copy-start(f32[128,1536]{1,0:T(8,128)} %get-tuple-element.19) | copy-start | bytes 2359300

commit v3 on v2

--- a/solution.py
+++ b/solution.py
@@ -30,21 +30,36 @@
     )
 
 
+class Axis:
+    def __init__(self, name, outer, inner):
+        self.name, self.outer, self.inner = name, outer, inner
+        self.me = lax.axis_index(name)
+        self.o = self.me // inner
+        self.i = lax.rem(self.me, inner)
+
+    def near(self, k):
+        half = self.outer // 2
+        side = self.o // half
+        m = self.o + side * (self.outer - 1 - 2 * self.o)
+        at = jnp.where(k == 0, m, k - m * ((3 - k) // 2))
+        return at + side * (self.outer - 1 - 2 * at)
+
+    def blk(self, k, q):
+        return self.near(k) * self.inner + lax.rem(self.i + q, self.inner)
+
+    def to(self, d):
+        return {self.name: d}
+
+
 class Place:
     def __init__(self, S, F):
         self.S, self.F = S, F
-        self.Z = 4
-        self.X = S // 4
-        self.s = lax.axis_index("seq")
-        self.f = lax.axis_index("fsdp")
-        self.z = self.s // self.X
-        self.x = lax.rem(self.s, self.X)
-
-    def zz(self, k):
-        return lax.rem(self.z + k + (k // 2) * (1 - 2 * (k % 2)), self.Z)
-
-    def blk(self, k, q):
-        return self.zz(k) * self.X + lax.rem(self.x + q, self.X)
+        self.seq = Axis("seq", 4, S // 4)
+        self.fsdp = Axis("fsdp", F // 2, 2)
+        self.Z, self.X = 4, S // 4
+        self.s, self.z, self.x = self.seq.me, self.seq.o, self.seq.i
+        self.f = self.fsdp.me
+        self.blk = self.seq.blk
 
     def barrier(self):
         bar = pltpu.get_barrier_semaphore()
@@ -63,38 +78,82 @@
 
 
 class Gather:
-    def __init__(self, pc, src, buf, ss, rs):
-        self.pc, self.src, self.buf, self.ss, self.rs = pc, src, buf, ss, rs
+    def __init__(self, ax, src, buf, sems):
+        self.ax, self.src, self.buf = ax, src, buf
+        self.ss, self.rs = sems
+
+    def send(self, src, b, sem, dst):
+        rcopy(src, self.buf.at[b], self.ss.at[sem], self.rs.at[b], **self.ax.to(dst)).start()
 
     def start(self):
-        pc = self.pc
-        for k in range(1, pc.Z):
-            rcopy(
-                self.src, self.buf.at[pc.s], self.ss.at[k - 1], self.rs.at[pc.s],
-                seq=pc.zz(k) * pc.X + pc.x,
-            ).start()
-        self.across(self.src, pc.s, 0)
+        ax = self.ax
+        for sem, d in ((0, 1), (1, -1)):
+
+            @pl.when(jnp.logical_and(ax.o + d >= 0, ax.o + d < ax.outer))
+            def _():
+                self.send(self.src, ax.me, sem, ax.me + d * ax.inner)
+
+        self.across(self.src, ax.me, 0)
 
     def across(self, src, b, k):
-        pc = self.pc
-        for q in range(1, pc.X):
-            rcopy(
-                src, self.buf.at[b], self.ss.at[pc.Z - 1 + k * (pc.X - 1) + q - 1], self.rs.at[b],
-                seq=pc.z * pc.X + lax.rem(pc.x + q, pc.X),
-            ).start()
+        ax = self.ax
+        for q in range(1, ax.inner):
+            sem = ax.outer + 1 + k * (ax.inner - 1) + q - 1
+            self.send(src, b, sem, ax.o * ax.inner + lax.rem(ax.i + q, ax.inner))
+
+    def onward(self, k):
+        ax = self.ax
+        return ax.o + jnp.where(ax.o > ax.near(k), 1, -1)
+
+    def relay(self, k):
+        ax = self.ax
+        b = ax.blk(k, 0)
+        self.wait(b)
+        nxt = self.onward(k)
+
+        @pl.when(jnp.logical_and(nxt >= 0, nxt < ax.outer))
+        def _():
+            self.send(self.buf.at[b], b, 1 + k, nxt * ax.inner + ax.i)
+
+        self.across(self.buf.at[b], b, k)
 
     def wait(self, b):
         r = self.buf.at[b]
-        rcopy(r, r, self.ss.at[0], self.rs.at[b], seq=self.pc.s).wait_recv()
+        rcopy(r, r, self.ss.at[0], self.rs.at[b], **self.ax.to(self.ax.me)).wait_recv()
+
+    def wait_across(self):
+        for k in range(self.ax.outer):
+            for q in range(1, self.ax.inner):
+                self.wait(self.ax.blk(k, q))
 
     def drain(self):
-        for i in range(self.pc.Z - 1 + self.pc.Z * (self.pc.X - 1)):
-            rcopy(self.src, self.src, self.ss.at[i], self.rs.at[0], seq=self.pc.s).wait_send()
-
-
-def gather_sems(S):
-    Z, X = 4, S // 4
-    return [pltpu.SemaphoreType.DMA((Z - 1 + Z * (X - 1),)), pltpu.SemaphoreType.DMA((S,))]
+        ax = self.ax
+
+        def done(sem):
+            rcopy(
+                self.src, self.src, self.ss.at[sem], self.rs.at[0], **ax.to(ax.me)
+            ).wait_send()
+
+        for sem, d in ((0, 1), (1, -1)):
+
+            @pl.when(jnp.logical_and(ax.o + d >= 0, ax.o + d < ax.outer))
+            def _():
+                done(sem)
+
+        for k in range(1, ax.outer):
+            nxt = self.onward(k)
+
+            @pl.when(jnp.logical_and(nxt >= 0, nxt < ax.outer))
+            def _():
+                done(1 + k)
+
+        for sem in range(ax.outer * (ax.inner - 1)):
+            done(ax.outer + 1 + sem)
+
+
+def gather_sems(outer, inner):
+    sem = pltpu.SemaphoreType.DMA
+    return sem((outer + 1 + outer * (inner - 1),)), sem((outer * inner,))
 
 
 def pair(col, p):
@@ -145,60 +204,151 @@
     return spread(small[7:8, 256:384], cp)
 
 
-def body_fwd(cfg, tok, cot, wp, wo, sm, R):
+def tight(cfg):
     S, F, T, D, cp, WC = cfg
+    return S * T * D * 2 > 2**22
+
+
+def lanes_from(row, shift, width, size):
+    n = row.shape[1]
+    if n < width:
+        row = jnp.concatenate([row, jnp.zeros((row.shape[0], width - n), f32)], axis=1)
+    row = pltpu.roll(row, lax.rem(shift + width, width), 1)
+    return row[:, :size]
+
+
+def small_rows(cfg, dims, flat, pc):
+    S, F, T, D, cp, WC = cfg
+    inner, heads, cols = dims
+    conv = inner + 2 * N
+    cl, gl, nl, hl = conv // F, inner // F, D // F, heads // F
+    up = lambda n: -(-n // 128) * 128
+    at = 0
+    parts = []
+    for n in [cl] * 5 + [gl, nl, hl, hl, hl]:
+        parts.append(flat[:, at : at + up(n)])
+        at += up(n)
+    rows = jnp.concatenate(parts[:5] + [jnp.zeros((3, up(cl)), f32)], axis=0)
+    lane = lax.broadcasted_iota(jnp.int32, (8, cp), 1)
+    xs = lanes_from(rows, cl * pc.f - cols * pc.s, conv, cp)
+    bc = lanes_from(rows, cl * pc.f - inner, conv, 2 * N)
+    gate = lanes_from(parts[5], gl * pc.f - cols * pc.s, inner, cp)
+    if cols < cp:
+        xs = jnp.where(lane < cols, xs, 0.0)
+        gate = jnp.where(lane[0:1] < cols, gate, 0.0)
+    norm = lanes_from(parts[6], nl * pc.f, D, D)
+    hg = heads // S
+    hv = jnp.concatenate(parts[7:10] + [jnp.zeros((5, 128), f32)], axis=0)
+    hv = lanes_from(hv, hl * pc.f - hg * pc.s, 128, 128)
+    hv = jnp.where(lane[:, :128] < hg, hv, 0.0)
+
+    def wide(v):
+        return jnp.concatenate([v, jnp.zeros((v.shape[0], D - v.shape[1]), f32)], axis=1)
+
+    return jnp.concatenate(
+        [
+            wide(jnp.concatenate([xs, bc], axis=1)[0:5]),
+            wide(gate),
+            norm,
+            wide(jnp.concatenate([hv[0:1], hv[1:2], hv[2:3]], axis=1)),
+        ],
+        axis=0,
+    )
+
+
+def body_fwd(cfg, dims, tok, cot, wsrc, wo, flat, R):
+    S, F, T, D, cp, WC = cfg
+    inner, heads, cols = dims
     L = S * T
     C = cp + 2 * N
+    per = S // F
     pc = Place(S, F)
-    nh = cp // HEAD
+    own = R.w_all.at[pc.f]
+    if len(wsrc) == 1:
+        parts = [(wsrc[0], own)]
+    else:
+        win, step = wsrc
+        col = pl.multiple_of(pc.s * cols, cols)
+        parts = [
+            (win.at[:, pl.ds(col, cols)], own.at[:, pl.ds(0, cols)]),
+            (win.at[:, pl.ds(inner + col, cols)], own.at[:, pl.ds(cols, cols)]),
+            (win.at[:, pl.ds(2 * inner, 2 * N)], own.at[:, pl.ds(2 * cols, 2 * N)]),
+            (step, own.at[:, pl.ds(2 * cols + 2 * N, 128)]),
+        ]
+    parts = [pltpu.make_async_copy(a, b, R.wsem.at[i]) for i, (a, b) in enumerate(parts)]
+    for c in parts:
+        c.start()
+    R.sm_own[...] = small_rows(cfg, dims, flat[...].astype(f32), pc)
     pc.barrier()
-    tg = Gather(pc, tok, R.tok_all, R.ss_t, R.rs_t)
-    cg = Gather(pc, cot, R.cot_all, R.ss_c, R.rs_c)
-    ssw, rsw = R.ss_w, R.rs_w
-    owner = pc.s // (S // F)
+    tg = Gather(pc.seq, tok, R.tok_all, (R.ss_t, R.rs_t))
+    cg = Gather(pc.seq, cot, R.cot_all, (R.ss_c, R.rs_c))
+    wg = Gather(pc.fsdp, own, R.w_all, (R.ss_w, R.rs_w))
+    first = lax.rem(pc.s, per)
+    owner = pc.s // per
+    wogs = []
+    if not tight(cfg):
+        for p in range(per):
+            at = lax.rem(first + p, per)
+            wogs.append(
+                Gather(pc.fsdp, wo.at[at], R.w_out.at[at], (R.ss_o.at[p], R.rs_o.at[p]))
+            )
+    sm = R.sm_own
     tg.start()
     for k in range(1, F):
         to = lax.rem(pc.f + k, F)
-        rcopy(sm, R.sm_all.at[pc.f], ssw.at[0, k], rsw.at[0, pc.f], fsdp=to).start()
-        rcopy(wp, R.w_all.at[pc.f], ssw.at[1, k], rsw.at[1, pc.f], fsdp=to).start()
-
-    @pl.when(pc.f == owner)
-    def _():
-        for k in range(1, F):
-            to = lax.rem(pc.f + k, F)
-            rcopy(wo, R.wo_g, ssw.at[2, k], rsw.at[2, 0], fsdp=to).start()
-        pltpu.make_async_copy(wo, R.wo_g, R.wsem.at[1]).start()
-
+        rcopy(sm, R.sm_all.at[pc.f], R.ss_m.at[k], R.rs_m.at[pc.f], fsdp=to).start()
+    for c in parts:
+        c.wait()
+    wg.start()
     cg.start()
+    keep = []
+    for p in range(len(wogs)):
+        wogs[p].start()
+        at = lax.rem(first + p, per)
+        keep.append(pltpu.make_async_copy(wo.at[at], R.w_out.at[at, pc.f], R.osem.at[p]))
+    if tight(cfg):
+        keep.append(pltpu.make_async_copy(wo, R.wo_g, R.osem.at[0]))
+
+        @pl.when(pc.f == owner)
+        def _():
+            keep[0].start()
+            for k in range(1, F):
+                to = lax.rem(pc.f + k, F)
+                rcopy(wo, R.wo_g, R.ss_o.at[k], R.rs_o.at[0], fsdp=to).start()
+    else:
+        for c in keep:
+            c.start()
     R.tok_all[pc.s] = tok[...]
     R.cot_all[pc.s] = cot[...]
-    pltpu.make_async_copy(wp, R.w_all.at[pc.f], R.wsem.at[0]).start()
     R.sm_all[pc.f] = sm[...]
-
-    for i, (src, dst) in enumerate(((sm, R.sm_all), (wp, R.w_all))):
-        for k in range(1, F):
-            o = lax.rem(pc.f + k, F)
-            rcopy(src, dst.at[o], ssw.at[i, 0], rsw.at[i, o], fsdp=pc.f).wait_recv()
-        if i == 0:
-            total = R.sm_all[0]
-            for k in range(1, F):
-                total = total + R.sm_all[k]
-            R.small[...] = total
-    pltpu.make_async_copy(wp, R.w_all.at[pc.f], R.wsem.at[0]).wait()
+    R.ext[0:16, :] = jnp.zeros((16, C), bf16)
+    for k in range(1, F):
+        o = lax.rem(pc.f + k, F)
+        rcopy(sm, R.sm_all.at[o], R.ss_m.at[0], R.rs_m.at[o], fsdp=pc.f).wait_recv()
+    total = R.sm_all[0]
+    for k in range(1, F):
+        total = total + R.sm_all[k]
+    R.small[...] = total
     small = R.small
-    R.ext[0:16, :] = jnp.zeros((16, C), bf16)
+    for k in range(1, F // 2):
+        wg.relay(k)
+    wg.wait_across()
 
     def project(j, carry):
         k, q = j // pc.X, lax.rem(j, pc.X)
         b = pc.blk(k, q)
 
-        @pl.when(j > 0)
+        @pl.when(q > 0)
         def _():
             tg.wait(b)
 
         @pl.when(jnp.logical_and(q == 0, k > 0))
         def _():
-            tg.across(R.tok_all.at[b], b, k)
+            tg.relay(k)
+
+        @pl.when(j == S - 1)
+        def _():
+            cg.relay(1)
 
         r = R.tok_all[b].astype(f32)
         scale = lax.rsqrt(jnp.mean(r * r, axis=1, keepdims=True) + epsilon)
@@ -216,11 +366,9 @@
     ones = jnp.ones((8, cp), f32)
 
     def forward(c, carry):
-        @pl.when(c < pc.Z - 1)
-        def _():
-            b = pc.blk(c + 1, 0)
-            cg.wait(b)
-            cg.across(R.cot_all.at[b], b, c + 1)
+        @pl.when(jnp.logical_or(c == 2, c == 4))
+        def _():
+            cg.relay(c // 2 + 1)
 
         r0 = pl.multiple_of(c * Q, Q)
         taps, summed, sig, raw, dt, rate, cum = chunk_inputs(c, R.ext, R.rawb, small, cp)
@@ -258,13 +406,23 @@
 
     lax.fori_loop(0, L // Q, forward, 0)
 
-    @pl.when(pc.f != owner)
-    def _():
-        rcopy(wo, R.wo_g, ssw.at[2, 0], rsw.at[2, 0], fsdp=pc.f).wait_recv()
-
-    @pl.when(pc.f == owner)
-    def _():
-        pltpu.make_async_copy(wo, R.wo_g, R.wsem.at[1]).wait()
+    if tight(cfg):
+        group = R.wo_g
+
+        @pl.when(pc.f != owner)
+        def _():
+            rcopy(wo, R.wo_g, R.ss_o.at[0], R.rs_o.at[0], fsdp=pc.f).wait_recv()
+
+        @pl.when(pc.f == owner)
+        def _():
+            keep[0].wait()
+    else:
+        group = R.w_out.at[first, owner]
+        for c in keep:
+            c.wait()
+        for k in range(1, F // 2):
+            wogs[0].relay(k)
+        wogs[0].wait_across()
 
     def mixed(j, carry):
         k, q = j // pc.X, lax.rem(j, pc.X)
@@ -275,7 +433,7 @@
             cg.wait(b)
 
         r0 = pl.multiple_of(b * T, T)
-        mg = mm(R.cot_all[b], R.wo_g[...], 1, 1)
+        mg = mm(R.cot_all[b], group[...], 1, 1)
         R.mg[pl.ds(r0, T), :] = mg
         g = mg * small[5:6, :cp] * R.dpx[pl.ds(r0, T), :cp].astype(f32)
         R.st[1:2, pl.ds(r0, T)] = mm(ones, g, 1, 1, HI)[0:1]
@@ -296,18 +454,23 @@
         total = total + R.st_all[k]
     R.stats[...] = total
 
-    tg.drain()
-    cg.drain()
+    if not tight(cfg):
+        for g in wogs[1:]:
+            for k in range(1, F // 2):
+                g.relay(k)
+            g.wait_across()
+    for g in [tg, cg, wg] + wogs:
+        g.drain()
     for k in range(1, S):
         rcopy(R.st, R.st, R.ss_s.at[k], R.rs_s.at[0], seq=pc.s).wait_send()
     for k in range(1, F):
-        rcopy(sm, sm, ssw.at[0, k], rsw.at[0, 0], fsdp=pc.f).wait_send()
-        rcopy(wp, wp, ssw.at[1, k], rsw.at[1, 0], fsdp=pc.f).wait_send()
-
-    @pl.when(pc.f == owner)
-    def _():
-        for k in range(1, F):
-            rcopy(wo, wo, ssw.at[2, k], rsw.at[2, 0], fsdp=pc.f).wait_send()
+        rcopy(sm, sm, R.ss_m.at[k], R.rs_m.at[0], fsdp=pc.f).wait_send()
+    if tight(cfg):
+
+        @pl.when(pc.f == owner)
+        def _():
+            for k in range(1, F):
+                rcopy(wo, wo, R.ss_o.at[k], R.rs_o.at[0], fsdp=pc.f).wait_send()
 
 
 def fwd_scratch(cfg):
@@ -317,12 +480,14 @@
     C = cp + 2 * N
     V = pltpu.VMEM
     sem = pltpu.SemaphoreType.DMA
-    n_ag = 3 + 4 * (S // 4 - 1)
-    return SimpleNamespace(
+    per = S // F
+    seq = gather_sems(4, S // 4)
+    fsdp = gather_sems(F // 2, 2)
+    out = SimpleNamespace(
         tok_all=V((S, T, D), bf16),
         cot_all=V((S, T, D), bf16),
         w_all=V((F, Dl, WC), bf16),
-        wo_g=V((cp, D), bf16),
+        sm_own=V((8, D), f32),
         sm_all=V((F, 8, D), f32),
         small=V((8, D), f32),
         hid_t=V((D, L), bf16),
@@ -336,74 +501,27 @@
         st=V((2, L), f32),
         st_all=V((S, 2, L), f32),
         stats=V((2, L), f32),
-        ss_t=sem((n_ag,)),
-        rs_t=sem((S,)),
-        ss_c=sem((n_ag,)),
-        rs_c=sem((S,)),
-        ss_w=sem((3, F)),
-        rs_w=sem((3, F)),
-        wsem=sem((2,)),
+        ss_t=seq[0],
+        rs_t=seq[1],
+        ss_c=seq[0],
+        rs_c=seq[1],
+        ss_w=fsdp[0],
+        rs_w=fsdp[1],
+        ss_m=sem((F,)),
+        rs_m=sem((F,)),
+        wsem=sem((4,)),
+        osem=sem((per,)),
         ss_s=sem((S,)),
         rs_s=sem((S,)),
     )
-
-
-def prep(cfg, in_weight, step_weight, conv_kernel, conv_bias, step_bias, log_decay, skip_gain,
-         gate_gain, norm_gain, out_weight):
-    S, F, T, D, cp, WC = cfg
-    s = lax.axis_index("seq")
-    f = lax.axis_index("fsdp")
-    heads = step_weight.shape[1]
-    hg = heads // S
-    inner = out_weight.shape[0] * F
-    cols = inner // S
-    col = s * cols
-
-    def sl(a, start, size, axis):
-        return lax.dynamic_slice_in_dim(a, start, size, axis)
-
-    def padc(a, to):
-        return jnp.pad(a, [(0, 0)] * (a.ndim - 1) + [(0, to - a.shape[-1])])
-
-    wp = jnp.concatenate(
-        [
-            padc(sl(in_weight, col, cols, 1), cp),
-            padc(sl(in_weight, inner + col, cols, 1), cp),
-            in_weight[:, 2 * inner :],
-            padc(sl(step_weight, s * hg, hg, 1), 128),
-        ],
-        axis=1,
-    )
-    per = out_weight.shape[0] // cols
-    wo = jnp.pad(sl(out_weight, lax.rem(s, per) * cols, cols, 0), [(0, cp - cols), (0, 0)])
-
-    def window(a, start, size, out):
-        n = a.shape[-1]
-        pad = jnp.pad(a, [(0, 0)] * (a.ndim - 1) + [(size, size)])
-        return padc(sl(pad, jnp.clip(start - n * f + size, 0, n + size), size, a.ndim - 1), out)
-
-    def conv_rows(a):
-        return jnp.concatenate(
-            [window(a, col, cols, cp), window(a, inner, 2 * N, 2 * N)], axis=-1
-        )
-
-    def row(a):
-        return padc(a.astype(f32), D).reshape(-1, D)
-
-    def head(a):
-        return window(a[None], s * hg, hg, 128)
-
-    sm = jnp.concatenate(
-        [
-            row(conv_rows(conv_kernel)),
-            row(conv_rows(conv_bias[None])),
-            row(window(gate_gain[None], col, cols, cp)),
-            row(window(norm_gain[None], 0, D, D)),
-            row(jnp.concatenate([head(step_bias), head(log_decay), head(skip_gain)], axis=-1)),
-        ],
-        axis=0,
-    )
-    return wp, wo, sm
+    if tight(cfg):
+        out.wo_g = V((cp, D), bf16)
+        out.ss_o = out.rs_o = sem((F,))
+    else:
+        out.w_out = V((per, F, cp, D), bf16)
+        out.ss_o = sem((per,) + fsdp[0].shape)
+        out.rs_o = sem((per,) + fsdp[1].shape)
+    return out
 
 
 class Scatter:
@@ -491,36 +609,54 @@
             rcopy(r, r, self.ss.at[k - 1], self.rs.at[k - 1], fsdp=self.pc.f).wait_send()
 
 
-def body_bwd(cfg, inner, tok, cot, R, O):
+def body_bwd(cfg, dims, tok, cot, R, O):
     S, F, T, D, cp, WC = cfg
+    inner = float(dims[0])
     L = S * T
     C = cp + 2 * N
     Dl = D // F
     nc = L // Q
     cr = cp // F
     per = S // F
+    bh = Dl // S
     pc = Place(S, F)
     small = R.small
-    blk = Scatter(pc, R.bp, R.brx, R.brz, (R.bs0, R.bs1, R.bs2, R.bs3))
+    if tight(cfg):
+        blk = Scatter(pc, R.bp, R.brx, R.brz, (R.bs0, R.bs1, R.bs2, R.bs3))
     hid = Scatter(pc, R.tok_all, R.hrx, R.hrz, (R.hs0, R.hs1, R.hs2, R.hs3))
     zs = Shared(pc, R.zp, R.zr, R.zs0, R.zs1)
     os_ = Shared(pc, R.op, R.orecv, R.os0, R.os1)
     xs = Shared(pc, R.xp, R.xr, R.xs0, R.xs1)
-    zg = Gather(pc, R.zred, O.gz, R.gz0, R.gz1)
-    og = Gather(pc, R.ored, O.go_s, R.go0, R.go1)
-    xg = Gather(pc, R.xred, O.gx, R.gx0, R.gx1)
+    bs = Shared(pc, R.cp_, R.cr_, R.cs0, R.cs1)
+    zg = Gather(pc.seq, R.zred, O.gz, (R.gz0, R.gz1))
+    og = Gather(pc.seq, R.ored, O.go_s, (R.go0, R.go1))
+    xg = Gather(pc.seq, R.xred, O.gx, (R.gx0, R.gx1))
+    sg = Gather(pc.seq, R.asum, O.sm, (R.as2, R.as3))
+
+    def direct(src, dst, ss, rs, to):
+        rcopy(src, dst.at[pc.s], ss.at[to], rs.at[pc.s], seq=to).start()
+
+    def arrived(dst, ss, rs):
+        for k in range(1, S):
+            o = lax.rem(pc.s + k, S)
+            r = dst.at[o]
+            rcopy(r, r, ss.at[0], rs.at[o], seq=pc.s).wait_recv()
+
+    def sent(src, ss, rs):
+        for k in range(1, S):
+            rcopy(src, src, ss.at[lax.rem(pc.s + k, S)], rs.at[0], seq=pc.s).wait_send()
 
     def own(src, dst, i):
         return pltpu.make_async_copy(src, dst, R.lsem.at[i])
 
     gate = small[5:6, :cp]
-    R.acc[...] = jnp.zeros((8, D), f32)
+    R.acc[...] = jnp.zeros((16, D), f32)
     R.hacc[...] = jnp.zeros((2, 8, 128), f32)
     R.dstate[...] = jnp.zeros((N, cp), f32)
     R.head[...] = jnp.zeros((8, C), f32)
 
     def first(i, carry):
-        c = nc - 1 - i
+        c = lax.rem(pc.s + 1 + i, nc)
         r0 = pl.multiple_of(c * Q, Q)
         rows = pl.ds(r0, Q)
         st = jnp.concatenate([R.stats[:, rows], jnp.zeros((6, Q), f32)], axis=0).T
@@ -537,7 +673,15 @@
         R.zb[rows, :] = (gg * R.y[rows, :] * (sz * (1.0 + z * (1.0 - sz)))).astype(bf16)
         R.mg[rows, :] = gg * (z * sz)
         R.mn_t[:, rows] = mn.T.astype(bf16)
-        R.dpx[rows, :cp] = mn.astype(bf16)
+        if tight(cfg):
+            R.dpx[rows, :cp] = mn.astype(bf16)
+        else:
+            R.mn[c] = mn.astype(bf16)
+
+            @pl.when(c != pc.s)
+            def _():
+                direct(R.mn.at[c], R.mall, R.ms0, R.ms1, c)
+
         return carry
 
     def block(i, carry):
@@ -548,8 +692,6 @@
         return carry
 
     lax.fori_loop(0, nc, first, 0)
-    if not tight(cfg):
-        lax.fori_loop(0, nc, block, 0)
 
     def zpart(k, carry):
         to = lax.rem(pc.f + k, F)
@@ -589,30 +731,31 @@
         r0 = pl.multiple_of(c * Q, Q)
         rows = pl.ds(r0, Q)
 
-        @pl.when(i < pc.Z)
-        def _():
-            blk.column(pc.Z - 1 - i)
-
-        @pl.when(i == 2)
+        if tight(cfg):
+
+            @pl.when(i < pc.Z)
+            def _():
+                blk.column(pc.Z - 1 - i)
+
+        @pl.when(i == 1)
         def _():
             R.zred[...] = zs.total().astype(bf16)
             zg.start()
             own(R.zred, O.gz.at[pc.s], 0).start()
 
-        @pl.when(i == 3)
+        @pl.when(i == 2)
         def _():
             R.ored[...] = os_.total().astype(bf16)
             og.start()
-            own(R.ored, O.go_s.at[pc.s], 4).start()
-
-        @pl.when(jnp.logical_and(i >= 5, i < 5 + pc.Z - 1))
-        def _():
-            k = i - 4
-            b = pc.blk(k, 0)
-            zg.wait(b)
-            zg.across(O.gz.at[b], b, k)
-            og.wait(b)
-            og.across(O.go_s.at[b], b, k)
+            own(R.ored, O.go_s.at[pc.s], 5).start()
+
+        @pl.when(jnp.logical_and(i >= 3, i < 3 + pc.Z - 1))
+        def _():
+            zg.relay(i - 2)
+
+        @pl.when(jnp.logical_and(i >= 4, i < 4 + pc.Z - 1))
+        def _():
+            og.relay(i - 3)
 
         taps, summed, sig, raw, dt, rate, cum = chunk_inputs(c, R.ext, R.rawb, small, cp)
         act = summed * sig
@@ -690,6 +833,7 @@
         R.acc[4:5, :C] += jnp.sum(dsum, axis=0, keepdims=True)
         R.head[...] = dsum[:8]
         R.dpx[rows, :C] = dxbc.astype(bf16)
+        R.acc[8:16, :] += mm(draw.astype(bf16), R.hid_t[:, rows], 1, 1)
         pad = jnp.concatenate([draw, jnp.zeros((120, Q), f32)], axis=0).T
         R.dpx[rows, C:] = pad.astype(bf16)
         grad = jnp.concatenate([R.zb[rows, :], R.dpx[rows, :]], axis=1)
@@ -703,10 +847,24 @@
 
     lax.fori_loop(0, nc, scan, 0)
 
+    def lower(k, carry):
+        to = lax.rem(pc.f + k, F)
+        rows = pl.ds(pl.multiple_of(to * Dl, Dl), Dl)
+        R.cp_[to] = mm(R.hid_t[rows, :], R.dpx[:, cp:C]).astype(bf16)
+
+        @pl.when(k < F)
+        def _():
+            rcopy(
+                R.cp_.at[to], R.cr_.at[k - 1], R.cs0.at[k - 1], R.cs1.at[k - 1], fsdp=to
+            ).start()
+        return carry
+
+    lax.fori_loop(1, F + 1, lower, 0)
+
     def xpart(k, carry):
         to = lax.rem(pc.f + k, F)
         rows = pl.ds(pl.multiple_of(to * Dl, Dl), Dl)
-        R.xp[to] = mm(R.hid_t[rows, :], R.dpx[...]).astype(bf16)
+        R.xp[to] = mm(R.hid_t[rows, :], R.dpx[:, :cp]).astype(bf16)
 
         @pl.when(k < F)
         def _():
@@ -735,32 +893,41 @@
             R.acc, R.ar.at[k - 1], R.as0.at[k - 1], R.as1.at[k - 1], fsdp=to
         ).start()
 
+    low = bs.total()
+    for g in range(S):
+        R.cb[g] = low[g * bh : (g + 1) * bh].astype(bf16)
+    for k in range(1, S):
+        to = lax.rem(pc.s + k, S)
+        direct(R.cb.at[to], R.cbr, R.cb0, R.cb1, to)
+
     def hid_column(i, carry):
         hid.column(pc.Z - 1 - i)
         return carry
 
-    lax.fori_loop(0, pc.Z, hid_column, 0)
+    lax.fori_loop(0, pc.Z - 2, hid_column, 0)
+    R.xred[...] = xs.total().astype(bf16)
+    xg.start()
+    own(R.xred, O.gx.at[pc.s], 2).start()
+    lax.fori_loop(pc.Z - 2, pc.Z, hid_column, 0)
     total = R.acc[...]
     for k in range(1, F):
         r = R.ar.at[k - 1]
         rcopy(r, r, R.as0.at[k - 1], R.as1.at[k - 1], fsdp=pc.f).wait_recv()
         total = total + R.ar[k - 1]
-    R.asum[...] = total
+    R.asum[...] = total.astype(bf16)
+    sg.start()
+    own(R.asum, O.sm.at[pc.s], 1).start()
+    arrived(R.cbr, R.cb0, R.cb1)
+    R.cbr[pc.s] = R.cb[pc.s]
+    low = R.cbr[0].astype(f32)
+    for g in range(1, S):
+        low = low + R.cbr[g].astype(f32)
+    R.cbd[...] = low.astype(bf16)
     for k in range(1, S):
-        rcopy(
-            R.asum, O.sm.at[pc.s], R.as2.at[k], R.as3.at[pc.s], seq=lax.rem(pc.s + k, S)
-        ).start()
-    own(R.asum, O.sm.at[pc.s], 1).start()
-    R.xred[...] = xs.total().astype(bf16)
-    xg.start()
-    own(R.xred, O.gx.at[pc.s], 2).start()
-
-    mine = tok[...].astype(f32)
-    O.block[...] = (mine + blk.total()).astype(bf16)
-    for k in range(pc.Z):
-        for q in range(1, pc.X):
-            og.wait(pc.blk(k, q))
-    own(R.ored, O.go_s.at[pc.s], 4).wait()
+        direct(R.cbd, O.gbc, R.cd0, R.cd1, lax.rem(pc.s + k, S))
+    own(R.cbd, O.gbc.at[pc.s], 4).start()
+    own(R.ored, O.go_s.at[pc.s], 5).wait()
+    og.wait_across()
     for k in range(1, F):
         to = lax.rem(pc.f + k, F)
         rcopy(
@@ -768,47 +935,59 @@
             fsdp=to,
         ).start()
     own(O.go_s.at[pl.ds(pc.f * per, per)], O.go.at[pc.f], 3).start()
+    xg.relay(1)
+    sg.relay(1)
+
+    mine = tok[...].astype(f32)
+    if tight(cfg):
+        O.block[...] = (mine + blk.total()).astype(bf16)
+    else:
+        arrived(R.mall, R.ms0, R.ms1)
+        R.mall[pc.s] = R.mn[pc.s]
+        R.total[...] = mine
+
+        def add(g, carry):
+            w = R.w_out[lax.rem(g, per), g // per]
+            R.total[...] += mm(R.mall[g], w)
+            return carry
+
+        lax.fori_loop(0, S, add, 0)
+        O.block[...] = R.total[...].astype(bf16)
+    xg.relay(2)
+    sg.relay(2)
     scale = lax.rsqrt(jnp.mean(mine * mine, axis=1, keepdims=True) + epsilon)
     e = hid.total() * small[6:7, :]
     mean = jnp.mean(e * mine, axis=1, keepdims=True)
     O.input[...] = cot[...].astype(f32) + scale * e - scale * scale * scale * mine * mean
-
-    for k in range(1, pc.Z):
-        b = pc.blk(k, 0)
-        xg.wait(b)
-        xg.across(O.gx.at[b], b, k)
-    for k in range(pc.Z):
-        for q in range(1, pc.X):
-            zg.wait(pc.blk(k, q))
+    xg.relay(3)
+    sg.relay(3)
+
+    zg.wait_across()
     for k in range(1, F):
         o = lax.rem(pc.f + k, F)
         r = O.go.at[o]
         rcopy(r, r, R.gs0.at[0], R.gs1.at[o], fsdp=pc.f).wait_recv()
-    for k in range(1, S):
-        o = lax.rem(pc.s + k, S)
-        r = O.sm.at[o]
-        rcopy(r, r, R.as2.at[0], R.as3.at[o], seq=pc.s).wait_recv()
-    for k in range(pc.Z):
-        for q in range(1, pc.X):
-            xg.wait(pc.blk(k, q))
+    arrived(O.gbc, R.cd0, R.cd1)
+    sg.wait_across()
+    xg.wait_across()
     own(R.zred, O.gz.at[pc.s], 0).wait()
     own(R.asum, O.sm.at[pc.s], 1).wait()
     own(R.xred, O.gx.at[pc.s], 2).wait()
     own(O.go_s.at[pl.ds(pc.f * per, per)], O.go.at[pc.f], 3).wait()
-    for a in (blk, hid, zs, os_, xs, zg, og, xg):
+    own(R.cbd, O.gbc.at[pc.s], 4).wait()
+    if tight(cfg):
+        blk.drain()
+    else:
+        sent(R.mn.at[0], R.ms0, R.ms1)
+    sent(R.cb.at[0], R.cb0, R.cb1)
+    sent(R.cbd, R.cd0, R.cd1)
+    for a in (hid, zs, os_, xs, bs, zg, og, xg, sg):
         a.drain()
     for k in range(1, F):
         r = R.ar.at[k - 1]
         rcopy(r, r, R.as0.at[k - 1], R.as1.at[0], fsdp=pc.f).wait_send()
         r = O.go.at[0]
         rcopy(r, r, R.gs0.at[k], R.gs1.at[0], fsdp=pc.f).wait_send()
-    for k in range(1, S):
-        rcopy(R.asum, R.asum, R.as2.at[k], R.as3.at[0], seq=pc.s).wait_send()
-
-
-def tight(cfg):
-    S, F, T, D, cp, WC = cfg
-    return S * T * D * 2 > 2**22
 
 
 def bwd_scratch(cfg):
@@ -817,22 +996,20 @@
     Dl = D // F
     C = cp + 2 * N
     Z, X = 4, S // 4
-    WX = WC - cp
     cr = cp // F
+    bh = Dl // S
     V = pltpu.VMEM
     sem = pltpu.SemaphoreType.DMA
-    n_ag = Z - 1 + Z * (X - 1)
+    seq = gather_sems(4, S // 4)
     out = SimpleNamespace(
-        acc=V((8, D), f32),
-        asum=V((8, D), f32),
-        ar=V((F - 1, 8, D), f32),
+        acc=V((16, D), f32),
+        asum=V((16, D), bf16),
+        ar=V((F - 1, 16, D), f32),
         hacc=V((2, 8, 128), f32),
         dstate=V((N, cp), f32),
         head=V((8, C), f32),
         mn_t=V((cp, L), bf16),
-        dpx=V((L, WX), bf16),
-        brx=V((Z, X - 1, T, D), bf16),
-        brz=V((Z - 1, T, D), bf16),
+        dpx=V((L, WC - cp), bf16),
         hrx=V((Z, X - 1, T, D), bf16),
         hrz=V((Z - 1, T, D), bf16),
         zp=V((F, Dl, cp), bf16),
@@ -841,25 +1018,72 @@
         op=V((F, cr, D), bf16),
         orecv=V((F - 1, cr, D), bf16),
         ored=V((cr, D), bf16),
-        xp=V((F, Dl, WX), bf16),
-        xr=V((F - 1, Dl, WX), bf16),
-        xred=V((Dl, WX), bf16),
-        lsem=sem((5,)),
-        as0=sem((F,)), as1=sem((F,)), as2=sem((S,)), as3=sem((S,)),
-        gs0=sem((F,)), gs1=sem((F,)),
+        xp=V((F, Dl, cp), bf16),
+        xr=V((F - 1, Dl, cp), bf16),
+        xred=V((Dl, cp), bf16),
+        cp_=V((F, Dl, 2 * N), bf16),
+        cr_=V((F - 1, Dl, 2 * N), bf16),
+        cb=V((S, bh, 2 * N), bf16),
+        cbr=V((S, bh, 2 * N), bf16),
+        cbd=V((bh, 2 * N), bf16),
+        lsem=sem((6,)),
+        as0=sem((F,)), as1=sem((F,)), as2=seq[0], as3=seq[1],
+        gs0=sem((F,)), gs1=sem((F,)), cs0=sem((F,)), cs1=sem((F,)),
+        cb0=sem((S,)), cb1=sem((S,)), cd0=sem((S,)), cd1=sem((S,)),
+        zs0=sem((F,)), zs1=sem((F,)), gz0=seq[0], gz1=seq[1],
+        os0=sem((F,)), os1=sem((F,)), go0=seq[0], go1=seq[1],
+        xs0=sem((F,)), xs1=sem((F,)), gx0=seq[0], gx1=seq[1],
+        hs0=sem((S,)), hs1=sem((Z, X - 1)), hs2=sem((Z,)), hs3=sem((Z - 1,)),
     )
-    if not tight(cfg):
-        out.bp = V((S, T, D), bf16)
-
-    def both():
-        return sem((S,)), sem((Z, X - 1)), sem((Z,)), sem((Z - 1,))
-
-    out.bs0, out.bs1, out.bs2, out.bs3 = both()
-    out.hs0, out.hs1, out.hs2, out.hs3 = both()
-    out.zs0, out.zs1, out.gz0, out.gz1 = sem((F,)), sem((F,)), sem((n_ag,)), sem((S,))
-    out.os0, out.os1, out.go0, out.go1 = sem((F,)), sem((F,)), sem((n_ag,)), sem((S,))
-    out.xs0, out.xs1, out.gx0, out.gx1 = sem((F,)), sem((F,)), sem((n_ag,)), sem((S,))
+    if tight(cfg):
+        out.brx = V((Z, X - 1, T, D), bf16)
+        out.brz = V((Z - 1, T, D), bf16)
+        out.bs0, out.bs1, out.bs2, out.bs3 = out.hs0, out.hs1, out.hs2, out.hs3
+    else:
+        out.mn = V((S, T, cp), bf16)
+        out.mall = V((S, T, cp), bf16)
+        out.total = V((T, D), f32)
+        out.ms0 = out.ms1 = sem((S,))
     return out
+
+
+def assemble(cfg, dims, gz, gx, gbc, go, sm, win, step, conv, bias, gate, norm, heads, wout):
+    S, F, T, D, cp, WC = cfg
+    inner, nheads, cols = dims
+    for g in range(S):
+        win[:, g * cols : (g + 1) * cols] = gz[g, :, :cols].astype(f32)
+        win[:, inner + g * cols : inner + (g + 1) * cols] = gx[g, :, :cols].astype(f32)
+    wout[...] = go[0, 0].astype(f32)
+    C = cp + 2 * N
+    hg = nheads // S
+    Dl = D // F
+    win[:, 2 * inner :] = gbc[...].astype(f32)
+
+    @pl.when(pl.program_id(0) == 0)
+    def _():
+        f = lax.axis_index("fsdp")
+
+        def mine(v, size):
+            n = v.shape[1]
+            return pltpu.roll(v, lax.rem(n - size * f, n), 1)[:, :size]
+
+        v = [sm[g].astype(f32) for g in range(S)]
+        total = v[0]
+        for g in range(1, S):
+            total = total + v[g]
+        xs = jnp.concatenate([a[0:8, :cols] for a in v] + [total[0:8, cp:C]], axis=1)
+        xs = mine(xs, (inner + 2 * N) // F)
+        conv[...] = xs[0:4]
+        bias[...] = xs[4:5]
+        gate[...] = mine(jnp.concatenate([a[0:8, :cols] for a in v], axis=1), inner // F)[5:6]
+        norm[...] = mine(total[0:8], Dl)[6:7]
+        n = nheads // F
+        zero = jnp.zeros((8, 128 - nheads), f32)
+        for i in range(3):
+            hs = [a[0:8, 128 * i : 128 * i + hg] for a in v]
+            heads[i : i + 1, :] = mine(jnp.concatenate(hs + [zero], axis=1), n)[7:8]
+        cols_t = [mine(a[8:16], Dl).T[:, :hg] for a in v]
+        step[...] = jnp.concatenate(cols_t, axis=1)
 
 
 def shards(tokens, in_weight, step_weight, conv_kernel, conv_bias, step_bias, log_decay,
@@ -871,90 +1095,128 @@
     heads = step_weight.shape[1]
     cols = inner // S
     cp = -(-cols // 128) * 128
-    C = cp + 2 * N
     WC = 2 * cp + 2 * N + 128
-    WX = WC - cp
     Dl = D // F
     cr = cp // F
     per = S // F
+    bh = Dl // S
     cfg = (S, F, T, D, cp, WC)
-    wp, wo, sm = prep(cfg, in_weight, step_weight, conv_kernel, conv_bias, step_bias, log_decay,
-                      skip_gain, gate_gain, norm_gain, out_weight)
+    dims = (inner, heads, cols)
+    s = lax.axis_index("seq")
+
+    def padc(a, to):
+        return jnp.pad(a, [(0, 0)] * (a.ndim - 1) + [(0, to - a.shape[-1])])
+
+    def part(a, start, size, axis):
+        return lax.dynamic_slice_in_dim(a, start, size, axis)
+
+    step = padc(part(step_weight, s * (heads // S), heads // S, 1), 128)
+    if cols % 128 == 0:
+        wsrc = (in_weight, step)
+    else:
+        wsrc = (
+            jnp.concatenate(
+                [
+                    padc(part(in_weight, s * cols, cols, 1), cp),
+                    padc(part(in_weight, inner + s * cols, cols, 1), cp),
+                    in_weight[:, 2 * inner :],
+                    step,
+                ],
+                axis=1,
+            ),
+        )
+    if tight(cfg):
+        wo = jnp.pad(
+            part(out_weight, lax.rem(s, per) * cols, cols, 0), [(0, cp - cols), (0, 0)]
+        )
+    else:
+        wo = out_weight.reshape(per, cols, D)
+    vectors = list(conv_kernel) + [
+        conv_bias, gate_gain, norm_gain, step_bias, log_decay, skip_gain,
+    ]
+    flat = jnp.concatenate([padc(a, -(-a.shape[0] // 128) * 128) for a in vectors])[None]
     scratch = {**vars(fwd_scratch(cfg)), **vars(bwd_scratch(cfg))}
     names = list(scratch)
     outs = dict(
         block=jax.ShapeDtypeStruct((T, D), bf16),
         input=jax.ShapeDtypeStruct((T, D), f32),
         gz=jax.ShapeDtypeStruct((S, Dl, cp), bf16),
-        gx=jax.ShapeDtypeStruct((S, Dl, WX), bf16),
+        gx=jax.ShapeDtypeStruct((S, Dl, cp), bf16),
+        gbc=jax.ShapeDtypeStruct((S, bh, 2 * N), bf16),
         go=jax.ShapeDtypeStruct((F, per, cr, D), bf16),
         go_s=jax.ShapeDtypeStruct((S, cr, D), bf16),
-        sm=jax.ShapeDtypeStruct((S, 8, D), f32),
+        sm=jax.ShapeDtypeStruct((S, 16, D), bf16),
     )
     on = list(outs)
-
-    def kern(tok, cot, wp, wo, sm, *rest):
-        O = SimpleNamespace(**dict(zip(on, rest[: len(on)])))
-        R = SimpleNamespace(**dict(zip(names, rest[len(on) :])))
+    nw = len(wsrc)
+
+    def kern(tok, cot, wo, flat, *rest):
+        O = SimpleNamespace(**dict(zip(on, rest[nw : nw + len(on)])))
+        R = SimpleNamespace(**dict(zip(names, rest[nw + len(on) :])))
         if tight(cfg):
             R.bp = R.cot_all
-        body_fwd(cfg, tok, cot, wp, wo, sm, R)
-        body_bwd(cfg, float(inner), tok, cot, R, O)
+        body_fwd(cfg, dims, tok, cot, rest[:nw], wo, flat, R)
+        body_bwd(cfg, dims, tok, cot, R, O)
 
     v = pl.BlockSpec(memory_space=pltpu.VMEM)
     hbm = pl.BlockSpec(memory_space=pl.ANY)
     res = pl.pallas_call(
         kern,
         out_shape=[outs[n] for n in on],
-        in_specs=[v, v, hbm, hbm, v],
-        out_specs=[v, v, hbm, hbm, hbm, hbm, hbm],
+        in_specs=[v, v, hbm, v] + [hbm] * nw,
+        out_specs=[v, v] + [hbm] * (len(on) - 2),
         scratch_shapes=[scratch[n] for n in names],
         compiler_params=pltpu.CompilerParams(
             collective_id=0, has_side_effects=True, vmem_limit_bytes=VMEM_LIMIT
         ),
-    )(tokens[0], cotangent[0], wp, wo, sm)
+    )(tokens[0], cotangent[0], wo, flat, *wsrc)
     G = SimpleNamespace(**dict(zip(on, res)))
-    gz, gx, go, gs = G.gz, G.gx, G.go, G.sm
-    fpos = lax.axis_index("fsdp")
-
-    def join(a, n):
-        return jnp.moveaxis(a[..., :n], 0, -2).reshape(a.shape[1:-1] + (-1,))
-
-    hg = heads // S
-    in_grad = jnp.concatenate(
-        [
-            join(gz, cols),
-            join(gx, cols),
-            jnp.sum(gx[:, :, cp:C].astype(f32), axis=0).astype(bf16),
+    pieces = cols // cr
+    steps = per * pieces
+    rows = Dl // steps
+    cl, gl, hl = (inner + 2 * N) // F, inner // F, heads // F
+
+    def whole(*shape):
+        return pl.BlockSpec(shape, lambda i: (0,) * len(shape))
+
+    def out(*shape):
+        return jax.ShapeDtypeStruct(shape, f32)
+
+    joined = pl.pallas_call(
+        lambda *refs: assemble(cfg, dims, *refs),
+        grid=(steps,),
+        out_shape=[
+            out(Dl, 2 * inner + 2 * N), out(Dl, heads), out(4, cl), out(1, cl), out(1, gl),
+            out(1, Dl), out(3, hl), out(per * cols, D),
         ],
-        axis=1,
-    ).astype(f32)
-    step_grad = join(gx[:, :, C:], hg).astype(f32)
-    out_grad = (
-        jnp.moveaxis(go, 0, 1).reshape(per, cp, D)[:, :cols].reshape(per * cols, D).astype(f32)
-    )
-
-    def mine(a, axis):
-        n = a.shape[axis] // F
-        return lax.dynamic_slice_in_dim(a, fpos * n, n, axis)
-
-    conv = jnp.concatenate(
-        [join(gs[:, 0:5], cols), jnp.sum(gs[:, 0:5, cp:C], axis=0)], axis=1
-    )
-    conv = mine(conv, 1)
+        in_specs=[
+            pl.BlockSpec((S, rows, cp), lambda i: (0, i, 0)),
+            pl.BlockSpec((S, rows, cp), lambda i: (0, i, 0)),
+            pl.BlockSpec((rows, 2 * N), lambda i: (i, 0)),
+            pl.BlockSpec((1, 1, cr, D), lambda i: (lax.rem(i, pieces), i // pieces, 0, 0)),
+            whole(S, 16, D),
+        ],
+        out_specs=[
+            pl.BlockSpec((rows, 2 * inner + 2 * N), lambda i: (i, 0)),
+            whole(Dl, heads), whole(4, cl), whole(1, cl), whole(1, gl), whole(1, Dl),
+            whole(3, hl),
+            pl.BlockSpec((cr, D), lambda i: (i, 0)),
+        ],
+    )(G.gz, G.gx, G.gbc.reshape(Dl, 2 * N), G.go, G.sm)
+    win, stepg, conv, bias, gate, norm, hd, wout = joined
     return (
         G.block[None],
         G.input[None],
-        in_grad,
-        step_grad,
-        conv[0:4],
-        conv[4],
-        mine(join(gs[:, 7], hg), 0),
-        mine(join(gs[:, 7, 128:], hg), 0),
-        mine(join(gs[:, 7, 256:], hg), 0),
-        mine(join(gs[:, 5], cols), 0),
-        mine(jnp.sum(gs[:, 6], axis=0), 0),
-        out_grad,
+        win,
+        stepg,
+        conv,
+        bias[0],
+        hd[0],
+        hd[1],
+        hd[2],
+        gate[0],
+        norm[0],
+        wout,
     )
 
 

time: 399 us -> 297 us (0.74)
  the two profiles are of different devices: /device:TPU:14 before, /device:TPU:0 now
where the time goes in v3:
time: 297 us; the launch traced here: 296 us
  Pallas kernels  278 us (94%)
  local copies, waits for them, and re-layouts  13.7 us (5%)
  other arithmetic  3.85 us (1%)
    pallas_call x1, Pallas kernels, shards(): pl.pallas_call(kern, out_shape=[outs[n] for n in on], in_specs=[v, v, hbm...  267 us
    pallas_call x1, Pallas kernels, shards(): pl.pallas_call(lambda *refs: assemble(cfg, dims, *refs), grid=(steps,), o...  10.6 us
    unnamed x17, local copies, waits for them, and re-layouts  6.61 us

profile of v3, /device:TPU:0, one launch (start us, length us, event | category | flops | bytes accessed | tf_op | source)
XLA Modules:
  0.0 296.0 jit_solution(9490761030367264808)
XLA Ops:
  0.6 0.7 pad.35
  1.3 0.7 pad.36
  2.0 0.7 pad.37
  2.6 0.7 pad.34
  3.3 0.7 constant_dynamic-slice_fusion
  4.0 0.9 slice_reduce_fusion
  5.0 0.2 dynamic-update-slice
  5.2 0.2 dynamic-update-slice.1
  5.4 0.2 dynamic-update-slice.2
  5.6 0.2 dynamic-update-slice.3
  5.8 0.2 dynamic-update-slice.4
  6.0 0.9 dynamic-update-slice.5
  6.9 0.9 dynamic-update-slice.6
  7.7 0.2 dynamic-update-slice.7
  7.9 0.2 dynamic-update-slice.8
  8.1 0.2 dynamic-update-slice.9
  8.3 0.6 broadcast_in_dim.9.flat
  8.9 0.2 copy.26
  9.1 0.7 pad.38.rest_1_
  9.8 267.1 %shard_map.211 = (bf16[128,1536]{1,0:T(8,128)(2,1)}, f32[128,1536]{1,0:T(8,128)}, bf16[8,384,384]{2,1,0:T(8,128)(2,1)}, bf16[8,384,384]{2,1,0:T(8,128)(2,1)}, bf...) custom-call(bf16[128,1536]{1,0:T(8,128)(2,1)} %bitcast.14, ...), custom_call_target="tpu_custom_call" | custom-call | tf_op jit(solution)/shard_map/pallas_call | solution.py:1163
  276.9 0.0 copy-start.1
  276.9 0.0 copy-start
  277.0 10.6 %shard_map.212 = (f32[384,6400]{1,0:T(8,128)}, f32[384,48]{1,0:T(8,128)}, f32[4,832]{1,0:T(4,128)}, f32[1,832]{1,0:T(1,128)}, f32[1,768]{1,0:T(1,128)}, /*index=...) custom-call(bf16[8,384,384]{2,1,0:T(8,128)(2,1)} %get-tuple-element.29.refs_0_, ...), custom_call_target="tpu_custom_call" | custom-call | tf_op jit(solution)/shard_map/pallas_call | solution.py:1185
  287.6 1.3 slice_bitcast_fusion
  288.9 1.3 reduce.6
  290.1 1.3 reduce.4
  291.4 1.3 reduce.5
  292.7 1.7 copy.25
  294.4 0.0 copy-done.1
  294.4 0.7 copy.39
  295.1 0.0 copy-done
  295.1 0.9 copy.40
  (5 shorter events, 0.0 us)
Async XLA Ops:
  276.9 17.5 %copy-start.1 = (bf16[128,1536]{1,0:T(8,128)(2,1)S(1)}, bf16[128,1536]{1,0:T(8,128)(2,1)}, u32[]{:S(2)}) copy-start(bf16[128,1536]{1,0:T(8,128)(2,1)} %get-tuple-element.27) | copy-start | bytes 1179652
  276.9 18.2 %copy-start = (f32[128,1536]{1,0:T(8,128)S(1)}, f32[128,1536]{1,0:T(8,128)}, u32[]{:S(2)}) copy-start(f32[128,1536]{1,0:T(8,128)} %get-tuple-element.28) | copy-start | bytes 2359300

commit v4 on v3

--- a/solution.py
+++ b/solution.py
@@ -300,7 +300,6 @@
     for c in parts:
         c.wait()
     wg.start()
-    cg.start()
     keep = []
     for p in range(len(wogs)):
         wogs[p].start()
@@ -330,8 +329,12 @@
         total = total + R.sm_all[k]
     R.small[...] = total
     small = R.small
+    tg.relay(1)
+    tg.relay(2)
     for k in range(1, F // 2):
         wg.relay(k)
+    tg.relay(3)
+    cg.start()
     wg.wait_across()
 
     def project(j, carry):
@@ -342,11 +345,7 @@
         def _():
             tg.wait(b)
 
-        @pl.when(jnp.logical_and(q == 0, k > 0))
-        def _():
-            tg.relay(k)
-
-        @pl.when(j == S - 1)
+        @pl.when(j == S // 2)
         def _():
             cg.relay(1)
 
@@ -366,9 +365,9 @@
     ones = jnp.ones((8, cp), f32)
 
     def forward(c, carry):
-        @pl.when(jnp.logical_or(c == 2, c == 4))
-        def _():
-            cg.relay(c // 2 + 1)
+        @pl.when(jnp.logical_or(c == 0, c == 5))
+        def _():
+            cg.relay(2 + c // 5)
 
         r0 = pl.multiple_of(c * Q, Q)
         taps, summed, sig, raw, dt, rate, cum = chunk_inputs(c, R.ext, R.rawb, small, cp)
@@ -454,12 +453,7 @@
         total = total + R.st_all[k]
     R.stats[...] = total
 
-    if not tight(cfg):
-        for g in wogs[1:]:
-            for k in range(1, F // 2):
-                g.relay(k)
-            g.wait_across()
-    for g in [tg, cg, wg] + wogs:
+    for g in [tg, cg, wg]:
         g.drain()
     for k in range(1, S):
         rcopy(R.st, R.st, R.ss_s.at[k], R.rs_s.at[0], seq=pc.s).wait_send()
@@ -471,6 +465,8 @@
         def _():
             for k in range(1, F):
                 rcopy(wo, wo, R.ss_o.at[k], R.rs_o.at[0], fsdp=pc.f).wait_send()
+
+    return wogs
 
 
 def fwd_scratch(cfg):
@@ -609,7 +605,7 @@
             rcopy(r, r, self.ss.at[k - 1], self.rs.at[k - 1], fsdp=self.pc.f).wait_send()
 
 
-def body_bwd(cfg, dims, tok, cot, R, O):
+def body_bwd(cfg, dims, tok, cot, wogs, R, O):
     S, F, T, D, cp, WC = cfg
     inner = float(dims[0])
     L = S * T
@@ -715,6 +711,9 @@
         return carry
 
     lax.fori_loop(0, D // W, opart, 0)
+    for g in wogs[1:]:
+        for k in range(1, F // 2):
+            g.relay(k)
     for k in range(1, F):
         os_.send(k)
     if tight(cfg):
@@ -942,6 +941,8 @@
     if tight(cfg):
         O.block[...] = (mine + blk.total()).astype(bf16)
     else:
+        for g in wogs[1:]:
+            g.wait_across()
         arrived(R.mall, R.ms0, R.ms1)
         R.mall[pc.s] = R.mn[pc.s]
         R.total[...] = mine
@@ -981,7 +982,7 @@
         sent(R.mn.at[0], R.ms0, R.ms1)
     sent(R.cb.at[0], R.cb0, R.cb1)
     sent(R.cbd, R.cd0, R.cd1)
-    for a in (hid, zs, os_, xs, bs, zg, og, xg, sg):
+    for a in [hid, zs, os_, xs, bs, zg, og, xg, sg] + wogs:
         a.drain()
     for k in range(1, F):
         r = R.ar.at[k - 1]
@@ -1155,8 +1156,8 @@
         R = SimpleNamespace(**dict(zip(names, rest[nw + len(on) :])))
         if tight(cfg):
             R.bp = R.cot_all
-        body_fwd(cfg, dims, tok, cot, rest[:nw], wo, flat, R)
-        body_bwd(cfg, dims, tok, cot, R, O)
+        wogs = body_fwd(cfg, dims, tok, cot, rest[:nw], wo, flat, R)
+        body_bwd(cfg, dims, tok, cot, wogs, R, O)
 
     v = pl.BlockSpec(memory_space=pltpu.VMEM)
     hbm = pl.BlockSpec(memory_space=pl.ANY)

time: 297 us -> 272 us (0.916)
  Pallas kernels: 278 us -> 253 us
    pallas_call x1, Pallas kernels: 267 us -> 242 us  [shards(): pl.pallas_call(kern, out_shape=[outs[n] for n in on], in_specs=[v, v, hbm...]
where the time goes in v4:
time: 272 us; the launch traced here: 271 us
  Pallas kernels  253 us (93%)
  local copies, waits for them, and re-layouts  13.7 us (5%)
  other arithmetic  3.85 us (1%)
    pallas_call x1, Pallas kernels, shards(): pl.pallas_call(kern, out_shape=[outs[n] for n in on], in_specs=[v, v, hbm...  242 us
    pallas_call x1, Pallas kernels, shards(): pl.pallas_call(lambda *refs: assemble(cfg, dims, *refs), grid=(steps,), o...  10.6 us
    unnamed x17, local copies, waits for them, and re-layouts  6.61 us

profile of v4, /device:TPU:0, one launch (start us, length us, event | category | flops | bytes accessed | tf_op | source)
XLA Modules:
  0.0 271.4 jit_solution(360152942032290693)
XLA Ops:
  0.6 0.7 pad.35
  1.3 0.7 pad.36
  2.0 0.7 pad.37
  2.6 0.7 pad.34
  3.3 0.7 constant_dynamic-slice_fusion
  4.0 0.9 slice_reduce_fusion
  5.0 0.2 dynamic-update-slice
  5.2 0.2 dynamic-update-slice.1
  5.4 0.2 dynamic-update-slice.2
  5.6 0.2 dynamic-update-slice.3
  5.8 0.2 dynamic-update-slice.4
  6.0 0.9 dynamic-update-slice.5
  6.9 0.9 dynamic-update-slice.6
  7.7 0.2 dynamic-update-slice.7
  7.9 0.2 dynamic-update-slice.8
  8.1 0.2 dynamic-update-slice.9
  8.3 0.6 broadcast_in_dim.9.flat
  8.9 0.2 copy.26
  9.1 0.7 pad.38.rest_1_
  9.8 242.5 %shard_map.211 = (bf16[128,1536]{1,0:T(8,128)(2,1)}, f32[128,1536]{1,0:T(8,128)}, bf16[8,384,384]{2,1,0:T(8,128)(2,1)}, bf16[8,384,384]{2,1,0:T(8,128)(2,1)}, bf...) custom-call(bf16[128,1536]{1,0:T(8,128)(2,1)} %bitcast.14, ...), custom_call_target="tpu_custom_call" | custom-call | tf_op jit(solution)/shard_map/pallas_call | solution.py:1164
  252.3 0.0 copy-start.1
  252.3 0.0 copy-start
  252.3 10.6 %shard_map.212 = (f32[384,6400]{1,0:T(8,128)}, f32[384,48]{1,0:T(8,128)}, f32[4,832]{1,0:T(4,128)}, f32[1,832]{1,0:T(1,128)}, f32[1,768]{1,0:T(1,128)}, /*index=...) custom-call(bf16[8,384,384]{2,1,0:T(8,128)(2,1)} %get-tuple-element.29.refs_0_, ...), custom_call_target="tpu_custom_call" | custom-call | tf_op jit(solution)/shard_map/pallas_call | solution.py:1186
  262.9 1.3 slice_bitcast_fusion
  264.2 1.3 reduce.6
  265.5 1.3 reduce.4
  266.8 1.3 reduce.5
  268.0 1.7 copy.25
  269.7 0.0 copy-done.1
  269.7 0.7 copy.39
  270.5 0.0 copy-done
  270.5 0.9 copy.40
  (5 shorter events, 0.0 us)
Async XLA Ops:
  252.3 17.5 %copy-start.1 = (bf16[128,1536]{1,0:T(8,128)(2,1)S(1)}, bf16[128,1536]{1,0:T(8,128)(2,1)}, u32[]{:S(2)}) copy-start(bf16[128,1536]{1,0:T(8,128)(2,1)} %get-tuple-element.27) | copy-start | bytes 1179652
  252.3 18.2 %copy-start = (f32[128,1536]{1,0:T(8,128)S(1)}, f32[128,1536]{1,0:T(8,128)}, u32[]{:S(2)}) copy-start(f32[128,1536]{1,0:T(8,128)} %get-tuple-element.28) | copy-start | bytes 2359300

commit v5 on v4

--- a/solution.py
+++ b/solution.py
@@ -78,12 +78,15 @@
 
 
 class Gather:
-    def __init__(self, ax, src, buf, sems):
-        self.ax, self.src, self.buf = ax, src, buf
+    def __init__(self, ax, src, buf, sems, cut=None):
+        self.ax, self.src, self.buf, self.cut = ax, src, buf, cut
         self.ss, self.rs = sems
 
+    def at(self, b):
+        return self.buf.at[b] if self.cut is None else self.buf.at[b, self.cut]
+
     def send(self, src, b, sem, dst):
-        rcopy(src, self.buf.at[b], self.ss.at[sem], self.rs.at[b], **self.ax.to(dst)).start()
+        rcopy(src, self.at(b), self.ss.at[sem], self.rs.at[b], **self.ax.to(dst)).start()
 
     def start(self):
         ax = self.ax
@@ -113,12 +116,12 @@
 
         @pl.when(jnp.logical_and(nxt >= 0, nxt < ax.outer))
         def _():
-            self.send(self.buf.at[b], b, 1 + k, nxt * ax.inner + ax.i)
-
-        self.across(self.buf.at[b], b, k)
+            self.send(self.at(b), b, 1 + k, nxt * ax.inner + ax.i)
+
+        self.across(self.at(b), b, k)
 
     def wait(self, b):
-        r = self.buf.at[b]
+        r = self.at(b)
         rcopy(r, r, self.ss.at[0], self.rs.at[b], **self.ax.to(self.ax.me)).wait_recv()
 
     def wait_across(self):
@@ -151,6 +154,40 @@
             done(ax.outer + 1 + sem)
 
 
+class Halves:
+    def __init__(self, ax, src, buf, sems):
+        n = src.shape[0] // 2
+        self.parts = []
+        for h in range(2):
+            cut = pl.ds(n * h, n)
+            self.parts.append(
+                Gather(ax, src.at[cut], buf, (sems[0].at[h], sems[1].at[h]), cut)
+            )
+
+    def start(self):
+        for g in self.parts:
+            g.start()
+
+    def relay(self, k, ends=None):
+        for g in self.parts:
+            if ends is None:
+                g.relay(k)
+                continue
+            last = jnp.logical_or(g.ax.o == 0, g.ax.o == g.ax.outer - 1)
+
+            @pl.when(last if ends else jnp.logical_not(last))
+            def _():
+                g.relay(k)
+
+    def wait(self, b):
+        for g in self.parts:
+            g.wait(b)
+
+    def drain(self):
+        for g in self.parts:
+            g.drain()
+
+
 def gather_sems(outer, inner):
     sem = pltpu.SemaphoreType.DMA
     return sem((outer + 1 + outer * (inner - 1),)), sem((outer * inner,))
@@ -163,6 +200,13 @@
 
 def spread(col, cp):
     return jnp.concatenate([pair(col, p) for p in range(cp // 128)], axis=1)
+
+
+def row_sums(v):
+    part = v[:, :128]
+    for p in range(1, v.shape[1] // 128):
+        part = part + v[:, 128 * p : 128 * p + 128]
+    return jnp.sum(part.T, axis=0, keepdims=True)
 
 
 def sigmoid(v):
@@ -222,23 +266,24 @@
     inner, heads, cols = dims
     conv = inner + 2 * N
     cl, gl, nl, hl = conv // F, inner // F, D // F, heads // F
-    up = lambda n: -(-n // 128) * 128
-    at = 0
-    parts = []
-    for n in [cl] * 5 + [gl, nl, hl, hl, hl]:
-        parts.append(flat[:, at : at + up(n)])
-        at += up(n)
-    rows = jnp.concatenate(parts[:5] + [jnp.zeros((3, up(cl)), f32)], axis=0)
+    def line(v):
+        v = v[...].astype(f32)
+        v = v if v.ndim == 2 else v[None]
+        n = -v.shape[1] % 128
+        return jnp.concatenate([v, jnp.zeros((v.shape[0], n), f32)], axis=1) if n else v
+
+    parts = [line(v) for v in flat]
+    rows = jnp.concatenate(parts[:2] + [jnp.zeros((3, parts[0].shape[1]), f32)], axis=0)
     lane = lax.broadcasted_iota(jnp.int32, (8, cp), 1)
     xs = lanes_from(rows, cl * pc.f - cols * pc.s, conv, cp)
     bc = lanes_from(rows, cl * pc.f - inner, conv, 2 * N)
-    gate = lanes_from(parts[5], gl * pc.f - cols * pc.s, inner, cp)
+    gate = lanes_from(parts[2], gl * pc.f - cols * pc.s, inner, cp)
     if cols < cp:
         xs = jnp.where(lane < cols, xs, 0.0)
         gate = jnp.where(lane[0:1] < cols, gate, 0.0)
-    norm = lanes_from(parts[6], nl * pc.f, D, D)
+    norm = lanes_from(parts[3], nl * pc.f, D, D)
     hg = heads // S
-    hv = jnp.concatenate(parts[7:10] + [jnp.zeros((5, 128), f32)], axis=0)
+    hv = jnp.concatenate(parts[4:7] + [jnp.zeros((5, 128), f32)], axis=0)
     hv = lanes_from(hv, hl * pc.f - hg * pc.s, 128, 128)
     hv = jnp.where(lane[:, :128] < hg, hv, 0.0)
 
@@ -256,7 +301,7 @@
     )
 
 
-def body_fwd(cfg, dims, tok, cot, wsrc, wo, flat, R):
+def body_fwd(cfg, dims, tok, cot, wsrc, wo, step, flat, R):
     S, F, T, D, cp, WC = cfg
     inner, heads, cols = dims
     L = S * T
@@ -264,24 +309,33 @@
     per = S // F
     pc = Place(S, F)
     own = R.w_all.at[pc.f]
-    if len(wsrc) == 1:
-        parts = [(wsrc[0], own)]
+    hg = heads // S
+    up = -(-heads // 8) * 8
+    st = step[...].astype(f32)
+    if up > heads:
+        st = jnp.concatenate([st, jnp.zeros((up - heads, st.shape[1]), f32)], axis=0)
+    st = pltpu.roll(st, lax.rem(up - hg * pc.s, up), 0)[:8].T
+    lane = lax.broadcasted_iota(jnp.int32, st.shape, 1)
+    st = jnp.where(lane < hg, st, 0.0)
+    st = jnp.concatenate([st, jnp.zeros((st.shape[0], 120), f32)], axis=1).astype(bf16)
+    R.w_all[pc.f, :, 2 * cp + 2 * N :] = st
+    if cols < cp:
+        parts = [(wsrc[0], own.at[:, pl.ds(0, 2 * cp + 2 * N)])]
     else:
-        win, step = wsrc
+        (win,) = wsrc
         col = pl.multiple_of(pc.s * cols, cols)
         parts = [
             (win.at[:, pl.ds(col, cols)], own.at[:, pl.ds(0, cols)]),
             (win.at[:, pl.ds(inner + col, cols)], own.at[:, pl.ds(cols, cols)]),
             (win.at[:, pl.ds(2 * inner, 2 * N)], own.at[:, pl.ds(2 * cols, 2 * N)]),
-            (step, own.at[:, pl.ds(2 * cols + 2 * N, 128)]),
         ]
     parts = [pltpu.make_async_copy(a, b, R.wsem.at[i]) for i, (a, b) in enumerate(parts)]
     for c in parts:
         c.start()
-    R.sm_own[...] = small_rows(cfg, dims, flat[...].astype(f32), pc)
+    R.sm_own[...] = small_rows(cfg, dims, flat, pc)
     pc.barrier()
-    tg = Gather(pc.seq, tok, R.tok_all, (R.ss_t, R.rs_t))
-    cg = Gather(pc.seq, cot, R.cot_all, (R.ss_c, R.rs_c))
+    tg = Halves(pc.seq, tok, R.tok_all, (R.ss_t, R.rs_t))
+    cg = Halves(pc.seq, cot, R.cot_all, (R.ss_c, R.rs_c))
     wg = Gather(pc.fsdp, own, R.w_all, (R.ss_w, R.rs_w))
     first = lax.rem(pc.s, per)
     owner = pc.s // per
@@ -331,9 +385,10 @@
     small = R.small
     tg.relay(1)
     tg.relay(2)
+    tg.relay(3, False)
     for k in range(1, F // 2):
         wg.relay(k)
-    tg.relay(3)
+    tg.relay(3, True)
     cg.start()
     wg.wait_across()
 
@@ -362,7 +417,6 @@
 
     lax.fori_loop(0, S, project, 0)
     R.state[...] = jnp.zeros((N, cp), f32)
-    ones = jnp.ones((8, cp), f32)
 
     def forward(c, carry):
         @pl.when(jnp.logical_or(c == 0, c == 5))
@@ -400,7 +454,7 @@
         gated = (y * (z * sigmoid(z))).astype(bf16)
         R.dpx[pl.ds(r0, Q), :cp] = gated
         g32 = gated.astype(f32)
-        R.st[0:1, pl.ds(r0, Q)] = mm(ones, g32 * g32, 1, 1, HI)[0:1]
+        R.st[0:1, pl.ds(r0, Q)] = row_sums(g32 * g32)
         return carry
 
     lax.fori_loop(0, L // Q, forward, 0)
@@ -435,7 +489,7 @@
         mg = mm(R.cot_all[b], group[...], 1, 1)
         R.mg[pl.ds(r0, T), :] = mg
         g = mg * small[5:6, :cp] * R.dpx[pl.ds(r0, T), :cp].astype(f32)
-        R.st[1:2, pl.ds(r0, T)] = mm(ones, g, 1, 1, HI)[0:1]
+        R.st[1:2, pl.ds(r0, T)] = row_sums(g)
         return carry
 
     lax.fori_loop(0, S, mixed, 0)
@@ -497,10 +551,10 @@
         st=V((2, L), f32),
         st_all=V((S, 2, L), f32),
         stats=V((2, L), f32),
-        ss_t=seq[0],
-        rs_t=seq[1],
-        ss_c=seq[0],
-        rs_c=seq[1],
+        ss_t=sem((2,) + seq[0].shape),
+        rs_t=sem((2,) + seq[1].shape),
+        ss_c=sem((2,) + seq[0].shape),
+        rs_c=sem((2,) + seq[1].shape),
         ss_w=fsdp[0],
         rs_w=fsdp[1],
         ss_m=sem((F,)),
@@ -622,11 +676,24 @@
     hid = Scatter(pc, R.tok_all, R.hrx, R.hrz, (R.hs0, R.hs1, R.hs2, R.hs3))
     zs = Shared(pc, R.zp, R.zr, R.zs0, R.zs1)
     os_ = Shared(pc, R.op, R.orecv, R.os0, R.os1)
-    xs = Shared(pc, R.xp, R.xr, R.xs0, R.xs1)
+    nt = cp // 128
+
+    def xs(t):
+        return Shared(pc, R.xp.at[t], R.xr.at[t], R.xs0.at[t], R.xs1.at[t])
+
+    def xg(t):
+        return Gather(pc.seq, R.xred.at[t], O.gx.at[t], (R.gx0.at[t], R.gx1.at[t]))
+
+    def own_x(t):
+        return pltpu.make_async_copy(R.xred.at[t], O.gx.at[t, pc.s], R.xsem.at[t])
+
+    def settle(t):
+        R.xred[t] = xs(t).total().astype(bf16)
+        xg(t).start()
+        own_x(t).start()
     bs = Shared(pc, R.cp_, R.cr_, R.cs0, R.cs1)
     zg = Gather(pc.seq, R.zred, O.gz, (R.gz0, R.gz1))
     og = Gather(pc.seq, R.ored, O.go_s, (R.go0, R.go1))
-    xg = Gather(pc.seq, R.xred, O.gx, (R.gx0, R.gx1))
     sg = Gather(pc.seq, R.asum, O.sm, (R.as2, R.as3))
 
     def direct(src, dst, ss, rs, to):
@@ -748,13 +815,13 @@
             og.start()
             own(R.ored, O.go_s.at[pc.s], 5).start()
 
-        @pl.when(jnp.logical_and(i >= 3, i < 3 + pc.Z - 1))
-        def _():
-            zg.relay(i - 2)
-
         @pl.when(jnp.logical_and(i >= 4, i < 4 + pc.Z - 1))
         def _():
-            og.relay(i - 3)
+            zg.relay(i - 3)
+
+        @pl.when(jnp.logical_and(i >= 6, i < 6 + pc.Z - 2))
+        def _():
+            og.relay(i - 5)
 
         taps, summed, sig, raw, dt, rate, cum = chunk_inputs(c, R.ext, R.rawb, small, cp)
         act = summed * sig
@@ -846,33 +913,6 @@
 
     lax.fori_loop(0, nc, scan, 0)
 
-    def lower(k, carry):
-        to = lax.rem(pc.f + k, F)
-        rows = pl.ds(pl.multiple_of(to * Dl, Dl), Dl)
-        R.cp_[to] = mm(R.hid_t[rows, :], R.dpx[:, cp:C]).astype(bf16)
-
-        @pl.when(k < F)
-        def _():
-            rcopy(
-                R.cp_.at[to], R.cr_.at[k - 1], R.cs0.at[k - 1], R.cs1.at[k - 1], fsdp=to
-            ).start()
-        return carry
-
-    lax.fori_loop(1, F + 1, lower, 0)
-
-    def xpart(k, carry):
-        to = lax.rem(pc.f + k, F)
-        rows = pl.ds(pl.multiple_of(to * Dl, Dl), Dl)
-        R.xp[to] = mm(R.hid_t[rows, :], R.dpx[:, :cp]).astype(bf16)
-
-        @pl.when(k < F)
-        def _():
-            rcopy(
-                R.xp.at[to], R.xr.at[k - 1], R.xs0.at[k - 1], R.xs1.at[k - 1], fsdp=to
-            ).start()
-        return carry
-
-    lax.fori_loop(1, F + 1, xpart, 0)
     diag = lax.broadcasted_iota(jnp.int32, (8, 128), 0) == lax.broadcasted_iota(
         jnp.int32, (8, 128), 1
     )
@@ -886,36 +926,72 @@
     R.acc[7:8, :] = jnp.concatenate(
         [along(R.hacc[0]), along(R.hacc[1]), dskip, jnp.zeros((1, D - 384), f32)], axis=1
     )
+    R.accb[...] = R.acc[...].astype(bf16)
     for k in range(1, F):
         to = lax.rem(pc.f + k, F)
         rcopy(
-            R.acc, R.ar.at[k - 1], R.as0.at[k - 1], R.as1.at[k - 1], fsdp=to
+            R.accb, R.ar.at[k - 1], R.as0.at[k - 1], R.as1.at[k - 1], fsdp=to
         ).start()
 
+    for t in range(nt):
+
+        def xpart(k, carry):
+            to = lax.rem(pc.f + k, F)
+            rows = pl.ds(pl.multiple_of(to * Dl, Dl), Dl)
+            R.xp[t, to] = mm(R.hid_t[rows, :], R.dpx[:, 128 * t : 128 * t + 128]).astype(bf16)
+
+            @pl.when(k < F)
+            def _():
+                rcopy(
+                    R.xp.at[t, to], R.xr.at[t, k - 1], R.xs0.at[t, k - 1], R.xs1.at[t, k - 1],
+                    fsdp=to,
+                ).start()
+            return carry
+
+        lax.fori_loop(1, F + 1, xpart, 0)
+
+    def lower(k, carry):
+        to = lax.rem(pc.f + k, F)
+        rows = pl.ds(pl.multiple_of(to * Dl, Dl), Dl)
+        R.cp_[to] = mm(R.hid_t[rows, :], R.dpx[:, cp:C]).astype(bf16)
+
+        @pl.when(k < F)
+        def _():
+            rcopy(
+                R.cp_.at[to], R.cr_.at[k - 1], R.cs0.at[k - 1], R.cs1.at[k - 1], fsdp=to
+            ).start()
+        return carry
+
+    lax.fori_loop(1, F + 1, lower, 0)
+    def hid_column(i, carry):
+        hid.column(pc.Z - 1 - i)
+        return carry
+
+    total = R.acc[...]
+    for k in range(1, F):
+        r = R.ar.at[k - 1]
+        rcopy(r, r, R.as0.at[k - 1], R.as1.at[k - 1], fsdp=pc.f).wait_recv()
+        total = total + R.ar[k - 1].astype(f32)
+    R.asum[...] = total.astype(bf16)
+    sg.start()
+    own(R.asum, O.sm.at[pc.s], 1).start()
+    og.relay(3)
+    settle(0)
+    for t in range(1, nt):
+        settle(t)
     low = bs.total()
     for g in range(S):
         R.cb[g] = low[g * bh : (g + 1) * bh].astype(bf16)
     for k in range(1, S):
         to = lax.rem(pc.s + k, S)
         direct(R.cb.at[to], R.cbr, R.cb0, R.cb1, to)
-
-    def hid_column(i, carry):
-        hid.column(pc.Z - 1 - i)
-        return carry
-
-    lax.fori_loop(0, pc.Z - 2, hid_column, 0)
-    R.xred[...] = xs.total().astype(bf16)
-    xg.start()
-    own(R.xred, O.gx.at[pc.s], 2).start()
-    lax.fori_loop(pc.Z - 2, pc.Z, hid_column, 0)
-    total = R.acc[...]
-    for k in range(1, F):
-        r = R.ar.at[k - 1]
-        rcopy(r, r, R.as0.at[k - 1], R.as1.at[k - 1], fsdp=pc.f).wait_recv()
-        total = total + R.ar[k - 1]
-    R.asum[...] = total.astype(bf16)
-    sg.start()
-    own(R.asum, O.sm.at[pc.s], 1).start()
+    lax.fori_loop(0, 2, hid_column, 0)
+    sg.relay(1)
+    for t in range(nt):
+        xg(t).relay(1)
+    sg.relay(2)
+    for t in range(nt):
+        xg(t).relay(2)
     arrived(R.cbr, R.cb0, R.cb1)
     R.cbr[pc.s] = R.cb[pc.s]
     low = R.cbr[0].astype(f32)
@@ -925,6 +1001,7 @@
     for k in range(1, S):
         direct(R.cbd, O.gbc, R.cd0, R.cd1, lax.rem(pc.s + k, S))
     own(R.cbd, O.gbc.at[pc.s], 4).start()
+    lax.fori_loop(2, pc.Z, hid_column, 0)
     own(R.ored, O.go_s.at[pc.s], 5).wait()
     og.wait_across()
     for k in range(1, F):
@@ -934,8 +1011,9 @@
             fsdp=to,
         ).start()
     own(O.go_s.at[pl.ds(pc.f * per, per)], O.go.at[pc.f], 3).start()
-    xg.relay(1)
-    sg.relay(1)
+    sg.relay(3)
+    for t in range(nt):
+        xg(t).relay(3)
 
     mine = tok[...].astype(f32)
     if tight(cfg):
@@ -954,14 +1032,10 @@
 
         lax.fori_loop(0, S, add, 0)
         O.block[...] = R.total[...].astype(bf16)
-    xg.relay(2)
-    sg.relay(2)
     scale = lax.rsqrt(jnp.mean(mine * mine, axis=1, keepdims=True) + epsilon)
     e = hid.total() * small[6:7, :]
     mean = jnp.mean(e * mine, axis=1, keepdims=True)
     O.input[...] = cot[...].astype(f32) + scale * e - scale * scale * scale * mine * mean
-    xg.relay(3)
-    sg.relay(3)
 
     zg.wait_across()
     for k in range(1, F):
@@ -970,10 +1044,11 @@
         rcopy(r, r, R.gs0.at[0], R.gs1.at[o], fsdp=pc.f).wait_recv()
     arrived(O.gbc, R.cd0, R.cd1)
     sg.wait_across()
-    xg.wait_across()
+    for t in range(nt):
+        xg(t).wait_across()
+        own_x(t).wait()
     own(R.zred, O.gz.at[pc.s], 0).wait()
     own(R.asum, O.sm.at[pc.s], 1).wait()
-    own(R.xred, O.gx.at[pc.s], 2).wait()
     own(O.go_s.at[pl.ds(pc.f * per, per)], O.go.at[pc.f], 3).wait()
     own(R.cbd, O.gbc.at[pc.s], 4).wait()
     if tight(cfg):
@@ -982,8 +1057,11 @@
         sent(R.mn.at[0], R.ms0, R.ms1)
     sent(R.cb.at[0], R.cb0, R.cb1)
     sent(R.cbd, R.cd0, R.cd1)
-    for a in [hid, zs, os_, xs, bs, zg, og, xg, sg] + wogs:
+    for a in [hid, zs, os_, bs, zg, og, sg] + wogs:
         a.drain()
+    for t in range(nt):
+        xs(t).drain()
+        xg(t).drain()
     for k in range(1, F):
         r = R.ar.at[k - 1]
         rcopy(r, r, R.as0.at[k - 1], R.as1.at[0], fsdp=pc.f).wait_send()
@@ -1002,10 +1080,12 @@
     V = pltpu.VMEM
     sem = pltpu.SemaphoreType.DMA
     seq = gather_sems(4, S // 4)
+    nt = cp // 128
     out = SimpleNamespace(
         acc=V((16, D), f32),
         asum=V((16, D), bf16),
-        ar=V((F - 1, 16, D), f32),
+        accb=V((16, D), bf16),
+        ar=V((F - 1, 16, D), bf16),
         hacc=V((2, 8, 128), f32),
         dstate=V((N, cp), f32),
         head=V((8, C), f32),
@@ -1019,9 +1099,9 @@
         op=V((F, cr, D), bf16),
         orecv=V((F - 1, cr, D), bf16),
         ored=V((cr, D), bf16),
-        xp=V((F, Dl, cp), bf16),
-        xr=V((F - 1, Dl, cp), bf16),
-        xred=V((Dl, cp), bf16),
+        xp=V((nt, F, Dl, 128), bf16),
+        xr=V((nt, F - 1, Dl, 128), bf16),
+        xred=V((nt, Dl, 128), bf16),
         cp_=V((F, Dl, 2 * N), bf16),
         cr_=V((F - 1, Dl, 2 * N), bf16),
         cb=V((S, bh, 2 * N), bf16),
@@ -1033,7 +1113,8 @@
         cb0=sem((S,)), cb1=sem((S,)), cd0=sem((S,)), cd1=sem((S,)),
         zs0=sem((F,)), zs1=sem((F,)), gz0=seq[0], gz1=seq[1],
         os0=sem((F,)), os1=sem((F,)), go0=seq[0], go1=seq[1],
-        xs0=sem((F,)), xs1=sem((F,)), gx0=seq[0], gx1=seq[1],
+        xs0=sem((nt, F)), xs1=sem((nt, F)), xsem=sem((nt,)),
+        gx0=sem((nt,) + seq[0].shape), gx1=sem((nt,) + seq[1].shape),
         hs0=sem((S,)), hs1=sem((Z, X - 1)), hs2=sem((Z,)), hs3=sem((Z - 1,)),
     )
     if tight(cfg):
@@ -1048,12 +1129,15 @@
     return out
 
 
-def assemble(cfg, dims, gz, gx, gbc, go, sm, win, step, conv, bias, gate, norm, heads, wout):
+def assemble(cfg, dims, gz, gx, gbc, go, sm, win, step, conv, bias, gate, norm, h0, h1, h2, wout):
     S, F, T, D, cp, WC = cfg
     inner, nheads, cols = dims
     for g in range(S):
         win[:, g * cols : (g + 1) * cols] = gz[g, :, :cols].astype(f32)
-        win[:, inner + g * cols : inner + (g + 1) * cols] = gx[g, :, :cols].astype(f32)
+        for t in range(gx.shape[0]):
+            n = min(128, cols - 128 * t)
+            at = inner + g * cols + 128 * t
+            win[:, at : at + n] = gx[t, g, :, :n].astype(f32)
     wout[...] = go[0, 0].astype(f32)
     C = cp + 2 * N
     hg = nheads // S
@@ -1075,16 +1159,15 @@
         xs = jnp.concatenate([a[0:8, :cols] for a in v] + [total[0:8, cp:C]], axis=1)
         xs = mine(xs, (inner + 2 * N) // F)
         conv[...] = xs[0:4]
-        bias[...] = xs[4:5]
-        gate[...] = mine(jnp.concatenate([a[0:8, :cols] for a in v], axis=1), inner // F)[5:6]
-        norm[...] = mine(total[0:8], Dl)[6:7]
+        bias[...] = xs[4]
+        gate[...] = mine(jnp.concatenate([a[0:8, :cols] for a in v], axis=1), inner // F)[5]
+        norm[...] = mine(total[0:8], Dl)[6]
         n = nheads // F
         zero = jnp.zeros((8, 128 - nheads), f32)
-        for i in range(3):
+        for i, ref in enumerate((h0, h1, h2)):
             hs = [a[0:8, 128 * i : 128 * i + hg] for a in v]
-            heads[i : i + 1, :] = mine(jnp.concatenate(hs + [zero], axis=1), n)[7:8]
-        cols_t = [mine(a[8:16], Dl).T[:, :hg] for a in v]
-        step[...] = jnp.concatenate(cols_t, axis=1)
+            ref[...] = mine(jnp.concatenate(hs + [zero], axis=1), n)[7]
+        step[...] = jnp.concatenate([mine(a[8:16], Dl)[:hg] for a in v], axis=0)
 
 
 def shards(tokens, in_weight, step_weight, conv_kernel, conv_bias, step_bias, log_decay,
@@ -1111,9 +1194,8 @@
     def part(a, start, size, axis):
         return lax.dynamic_slice_in_dim(a, start, size, axis)
 
-    step = padc(part(step_weight, s * (heads // S), heads // S, 1), 128)
     if cols % 128 == 0:
-        wsrc = (in_weight, step)
+        wsrc = (in_weight,)
     else:
         wsrc = (
             jnp.concatenate(
@@ -1121,7 +1203,6 @@
                     padc(part(in_weight, s * cols, cols, 1), cp),
                     padc(part(in_weight, inner + s * cols, cols, 1), cp),
                     in_weight[:, 2 * inner :],
-                    step,
                 ],
                 axis=1,
             ),
@@ -1132,31 +1213,31 @@
         )
     else:
         wo = out_weight.reshape(per, cols, D)
-    vectors = list(conv_kernel) + [
-        conv_bias, gate_gain, norm_gain, step_bias, log_decay, skip_gain,
-    ]
-    flat = jnp.concatenate([padc(a, -(-a.shape[0] // 128) * 128) for a in vectors])[None]
+    flat = (conv_kernel, conv_bias, gate_gain, norm_gain, step_bias, log_decay, skip_gain)
+    nt = cp // 128
     scratch = {**vars(fwd_scratch(cfg)), **vars(bwd_scratch(cfg))}
     names = list(scratch)
     outs = dict(
         block=jax.ShapeDtypeStruct((T, D), bf16),
         input=jax.ShapeDtypeStruct((T, D), f32),
         gz=jax.ShapeDtypeStruct((S, Dl, cp), bf16),
-        gx=jax.ShapeDtypeStruct((S, Dl, cp), bf16),
+        gx=jax.ShapeDtypeStruct((nt, S, Dl, 128), bf16),
         gbc=jax.ShapeDtypeStruct((S, bh, 2 * N), bf16),
         go=jax.ShapeDtypeStruct((F, per, cr, D), bf16),
         go_s=jax.ShapeDtypeStruct((S, cr, D), bf16),
         sm=jax.ShapeDtypeStruct((S, 16, D), bf16),
     )
     on = list(outs)
-    nw = len(wsrc)
-
-    def kern(tok, cot, wo, flat, *rest):
+    nw = 1
+    nf = len(flat)
+
+    def kern(tok, cot, wo, step, *rest):
+        flat, rest = rest[:nf], rest[nf:]
         O = SimpleNamespace(**dict(zip(on, rest[nw : nw + len(on)])))
         R = SimpleNamespace(**dict(zip(names, rest[nw + len(on) :])))
         if tight(cfg):
             R.bp = R.cot_all
-        wogs = body_fwd(cfg, dims, tok, cot, rest[:nw], wo, flat, R)
+        wogs = body_fwd(cfg, dims, tok, cot, rest[:nw], wo, step, flat, R)
         body_bwd(cfg, dims, tok, cot, wogs, R, O)
 
     v = pl.BlockSpec(memory_space=pltpu.VMEM)
@@ -1164,13 +1245,13 @@
     res = pl.pallas_call(
         kern,
         out_shape=[outs[n] for n in on],
-        in_specs=[v, v, hbm, v] + [hbm] * nw,
+        in_specs=[v, v, hbm, v] + [v] * nf + [hbm] * nw,
         out_specs=[v, v] + [hbm] * (len(on) - 2),
         scratch_shapes=[scratch[n] for n in names],
         compiler_params=pltpu.CompilerParams(
             collective_id=0, has_side_effects=True, vmem_limit_bytes=VMEM_LIMIT
         ),
-    )(tokens[0], cotangent[0], wo, flat, *wsrc)
+    )(tokens[0], cotangent[0], wo, step_weight.T, *flat, *wsrc)
     G = SimpleNamespace(**dict(zip(on, res)))
     pieces = cols // cr
     steps = per * pieces
@@ -1187,36 +1268,36 @@
         lambda *refs: assemble(cfg, dims, *refs),
         grid=(steps,),
         out_shape=[
-            out(Dl, 2 * inner + 2 * N), out(Dl, heads), out(4, cl), out(1, cl), out(1, gl),
-            out(1, Dl), out(3, hl), out(per * cols, D),
+            out(Dl, 2 * inner + 2 * N), out(heads, Dl), out(4, cl), out(cl), out(gl),
+            out(Dl), out(hl), out(hl), out(hl), out(per * cols, D),
         ],
         in_specs=[
             pl.BlockSpec((S, rows, cp), lambda i: (0, i, 0)),
-            pl.BlockSpec((S, rows, cp), lambda i: (0, i, 0)),
+            pl.BlockSpec((nt, S, rows, 128), lambda i: (0, 0, i, 0)),
             pl.BlockSpec((rows, 2 * N), lambda i: (i, 0)),
             pl.BlockSpec((1, 1, cr, D), lambda i: (lax.rem(i, pieces), i // pieces, 0, 0)),
             whole(S, 16, D),
         ],
         out_specs=[
             pl.BlockSpec((rows, 2 * inner + 2 * N), lambda i: (i, 0)),
-            whole(Dl, heads), whole(4, cl), whole(1, cl), whole(1, gl), whole(1, Dl),
-            whole(3, hl),
+            whole(heads, Dl), whole(4, cl), whole(cl), whole(gl), whole(Dl), whole(hl),
+            whole(hl), whole(hl),
             pl.BlockSpec((cr, D), lambda i: (i, 0)),
         ],
     )(G.gz, G.gx, G.gbc.reshape(Dl, 2 * N), G.go, G.sm)
-    win, stepg, conv, bias, gate, norm, hd, wout = joined
+    win, stepg, conv, bias, gate, norm, hd0, hd1, hd2, wout = joined
     return (
         G.block[None],
         G.input[None],
         win,
-        stepg,
+        stepg.T,
         conv,
-        bias[0],
-        hd[0],
-        hd[1],
-        hd[2],
-        gate[0],
-        norm[0],
+        bias,
+        hd0,
+        hd1,
+        hd2,
+        gate,
+        norm,
         wout,
     )
 

time: 272 us -> 247 us (0.908)
  local copies, waits for them, and re-layouts: 13.7 us -> 1.64 us
  Pallas kernels: 253 us -> 244 us
  other arithmetic: 3.85 us -> 0 us
    pallas_call x1, Pallas kernels: 242 us -> 233 us  [shards(): pl.pallas_call(kern, out_shape=[outs[n] for n in on], in_specs=[v, v, hbm...]
    unnamed x17 -> x6, local copies, waits for them, and re-layouts: 6.61 us -> 1.64 us
    pallas_call x3 -> x0, other arithmetic: 3.85 us -> none  [shards(): pl.pallas_call(lambda *refs: assemble(cfg, dims, *refs), grid=(steps,), o...]
    pad x9 -> x0, local copies, waits for them, and re-layouts: 3.36 us -> none  [padc(): return jnp.pad(a, [(0, 0)] * (a.ndim - 1) + [(0, to - a.shape[-1])])]
where the time goes in v5:
time: 247 us; the launch traced here: 246 us
  Pallas kernels  244 us (99%)
    pallas_call x1, Pallas kernels, shards(): pl.pallas_call(kern, out_shape=[outs[n] for n in on], in_specs=[v, v, hbm...  233 us
    pallas_call x1, Pallas kernels, shards(): pl.pallas_call(lambda *refs: assemble(cfg, dims, *refs), grid=(steps,), o...  10.2 us

profile of v5, /device:TPU:0, one launch (start us, length us, event | category | flops | bytes accessed | tf_op | source)
XLA Modules:
  0.0 245.9 jit_solution(7996751135767722523)
XLA Ops:
  0.6 233.3 %shard_map.211 = (bf16[128,1536]{1,0:T(8,128)(2,1)}, f32[128,1536]{1,0:T(8,128)}, bf16[8,384,384]{2,1,0:T(8,128)(2,1)}, bf16[3,8,384,128]{3,2,1,0:T(8,128)(2,1)}...) custom-call(bf16[128,1536]{1,0:T(8,128)(2,1)} %bitcast.10, ...), custom_call_target="tpu_custom_call" | custom-call | tf_op jit(solution)/shard_map/pallas_call | solution.py:1245
  234.0 0.0 copy-start.1
  234.0 0.0 copy-start
  234.0 10.2 %shard_map.212 = (f32[384,6400]{1,0:T(8,128)}, f32[48,384]{1,0:T(8,128)}, f32[4,832]{1,0:T(4,128)}, f32[832]{0:T(1024)}, f32[768]{0:T(1024)}, /*index=5*/f32[384...) custom-call(bf16[8,384,384]{2,1,0:T(8,128)(2,1)} %get-tuple-element.31.refs_0_, ...), custom_call_target="tpu_custom_call" | custom-call | tf_op jit(solution)/shard_map/pallas_call | solution.py:1267
  244.2 0.0 copy-done.1
  244.2 0.7 copy.26
  245.0 0.0 copy-done
  245.0 0.9 copy.27
Async XLA Ops:
  234.0 10.3 %copy-start.1 = (bf16[128,1536]{1,0:T(8,128)(2,1)S(1)}, bf16[128,1536]{1,0:T(8,128)(2,1)}, u32[]{:S(2)}) copy-start(bf16[128,1536]{1,0:T(8,128)(2,1)} %get-tuple-element.29) | copy-start | bytes 1179652
  234.0 11.0 %copy-start = (f32[128,1536]{1,0:T(8,128)S(1)}, f32[128,1536]{1,0:T(8,128)}, u32[]{:S(2)}) copy-start(f32[128,1536]{1,0:T(8,128)} %get-tuple-element.30) | copy-start | bytes 2359300

commit v6 on v5

--- a/solution.py
+++ b/solution.py
@@ -575,9 +575,18 @@
 
 
 class Scatter:
-    def __init__(self, pc, part, rx, rz, sems):
-        self.pc, self.part, self.rx, self.rz = pc, part, rx, rz
-        self.ssx, self.rsx, self.ssz, self.rsz = sems
+    def __init__(self, pc, part, rx, rz, rn, sems):
+        self.pc, self.part, self.rx, self.rz, self.rn = pc, part, rx, rz, rn
+        self.ssx, self.rsx, self.ssz, self.rsz, self.rsn = sems
+        self.near = jnp.logical_or(pc.z == 1, pc.z == 2)
+
+    @staticmethod
+    def sems(S):
+        sem = pltpu.SemaphoreType.DMA
+        return sem((S,)), sem((4, S // 4 - 1)), sem((4,)), sem((2,)), sem((2,))
+
+    def got(self, ref, sem):
+        rcopy(ref, ref, sem, sem, seq=self.pc.s).wait_recv()
 
     def across(self, b):
         pc = self.pc
@@ -591,29 +600,50 @@
                 seq=pc.z * pc.X + xb,
             ).start()
 
+    def other(self, zb):
+        return zb // 2 != self.pc.z // 2
+
     def column(self, zb):
         pc = self.pc
         b = zb * pc.X + pc.x
         total = self.part[b].astype(f32)
         for q in range(pc.X - 1):
-            r = self.rx.at[zb, q]
-            rcopy(r, r, self.ssx.at[0], self.rsx.at[zb, q], seq=pc.s).wait_recv()
+            self.got(self.rx.at[zb, q], self.rsx.at[zb, q])
             total = total + self.rx[zb, q].astype(f32)
         self.part[b] = total.astype(bf16)
 
-        @pl.when(zb != pc.z)
-        def _():
-            slot = lax.rem(pc.z - zb - 1 + pc.Z, pc.Z)
+        @pl.when(jnp.logical_and(zb != pc.z, jnp.logical_not(self.other(zb))))
+        def _():
             rcopy(
-                self.part.at[b], self.rz.at[slot], self.ssz.at[zb], self.rsz.at[slot], seq=b
+                self.part.at[b], self.rz.at[0], self.ssz.at[zb], self.rsz.at[0], seq=b
             ).start()
 
+        @pl.when(jnp.logical_and(self.other(zb), jnp.logical_not(self.near)))
+        def _():
+            slot = lax.rem(zb, 2)
+            rcopy(
+                self.part.at[b], self.rn.at[slot], self.ssz.at[zb], self.rsn.at[slot],
+                seq=(pc.z + 1 - 2 * lax.rem(pc.z, 2)) * pc.X + pc.x,
+            ).start()
+
+    def merge(self, zb):
+        pc = self.pc
+
+        @pl.when(jnp.logical_and(self.other(zb), self.near))
+        def _():
+            b = zb * pc.X + pc.x
+            slot = lax.rem(zb, 2)
+            self.got(self.rn.at[slot], self.rsn.at[slot])
+            total = self.part[b].astype(f32) + self.rn[slot].astype(f32)
+            self.part[b] = total.astype(bf16)
+            rcopy(
+                self.part.at[b], self.rz.at[1], self.ssz.at[zb], self.rsz.at[1], seq=b
+            ).start()
+
     def total(self):
-        pc = self.pc
-        out = self.part[pc.s].astype(f32)
-        for q in range(pc.Z - 1):
-            r = self.rz.at[q]
-            rcopy(r, r, self.ssz.at[0], self.rsz.at[q], seq=pc.s).wait_recv()
+        out = self.part[self.pc.s].astype(f32)
+        for q in range(2):
+            self.got(self.rz.at[q], self.rsz.at[q])
             out = out + self.rz[q].astype(f32)
         return out
 
@@ -672,8 +702,8 @@
     pc = Place(S, F)
     small = R.small
     if tight(cfg):
-        blk = Scatter(pc, R.bp, R.brx, R.brz, (R.bs0, R.bs1, R.bs2, R.bs3))
-    hid = Scatter(pc, R.tok_all, R.hrx, R.hrz, (R.hs0, R.hs1, R.hs2, R.hs3))
+        blk = Scatter(pc, R.bp, R.brx, R.brz, R.brn, (R.bs0, R.bs1, R.bs2, R.bs3, R.bs4))
+    hid = Scatter(pc, R.tok_all, R.hrx, R.hrz, R.hrn, (R.hs0, R.hs1, R.hs2, R.hs3, R.hs4))
     zs = Shared(pc, R.zp, R.zr, R.zs0, R.zs1)
     os_ = Shared(pc, R.op, R.orecv, R.os0, R.os1)
     nt = cp // 128
@@ -803,13 +833,17 @@
             def _():
                 blk.column(pc.Z - 1 - i)
 
+            @pl.when(jnp.logical_and(i >= pc.Z, i < 2 * pc.Z))
+            def _():
+                blk.merge(2 * pc.Z - 1 - i)
+
         @pl.when(i == 1)
         def _():
             R.zred[...] = zs.total().astype(bf16)
             zg.start()
             own(R.zred, O.gz.at[pc.s], 0).start()
 
-        @pl.when(i == 2)
+        @pl.when(i == 4)
         def _():
             R.ored[...] = os_.total().astype(bf16)
             og.start()
@@ -819,9 +853,9 @@
         def _():
             zg.relay(i - 3)
 
-        @pl.when(jnp.logical_and(i >= 6, i < 6 + pc.Z - 2))
-        def _():
-            og.relay(i - 5)
+        @pl.when(i == 7)
+        def _():
+            og.relay(1)
 
         taps, summed, sig, raw, dt, rate, cum = chunk_inputs(c, R.ext, R.rawb, small, cp)
         act = summed * sig
@@ -975,8 +1009,9 @@
     R.asum[...] = total.astype(bf16)
     sg.start()
     own(R.asum, O.sm.at[pc.s], 1).start()
+    og.relay(2)
+    settle(0)
     og.relay(3)
-    settle(0)
     for t in range(1, nt):
         settle(t)
     low = bs.total()
@@ -989,6 +1024,9 @@
     sg.relay(1)
     for t in range(nt):
         xg(t).relay(1)
+    lax.fori_loop(2, pc.Z, hid_column, 0)
+    for zb in (3, 2):
+        hid.merge(zb)
     sg.relay(2)
     for t in range(nt):
         xg(t).relay(2)
@@ -1001,7 +1039,6 @@
     for k in range(1, S):
         direct(R.cbd, O.gbc, R.cd0, R.cd1, lax.rem(pc.s + k, S))
     own(R.cbd, O.gbc.at[pc.s], 4).start()
-    lax.fori_loop(2, pc.Z, hid_column, 0)
     own(R.ored, O.go_s.at[pc.s], 5).wait()
     og.wait_across()
     for k in range(1, F):
@@ -1014,6 +1051,8 @@
     sg.relay(3)
     for t in range(nt):
         xg(t).relay(3)
+    for zb in (1, 0):
+        hid.merge(zb)
 
     mine = tok[...].astype(f32)
     if tight(cfg):
@@ -1092,7 +1131,8 @@
         mn_t=V((cp, L), bf16),
         dpx=V((L, WC - cp), bf16),
         hrx=V((Z, X - 1, T, D), bf16),
-        hrz=V((Z - 1, T, D), bf16),
+        hrz=V((2, T, D), bf16),
+        hrn=V((2, T, D), bf16),
         zp=V((F, Dl, cp), bf16),
         zr=V((F - 1, Dl, cp), bf16),
         zred=V((Dl, cp), bf16),
@@ -1115,12 +1155,13 @@
         os0=sem((F,)), os1=sem((F,)), go0=seq[0], go1=seq[1],
         xs0=sem((nt, F)), xs1=sem((nt, F)), xsem=sem((nt,)),
         gx0=sem((nt,) + seq[0].shape), gx1=sem((nt,) + seq[1].shape),
-        hs0=sem((S,)), hs1=sem((Z, X - 1)), hs2=sem((Z,)), hs3=sem((Z - 1,)),
     )
+    out.hs0, out.hs1, out.hs2, out.hs3, out.hs4 = Scatter.sems(S)
     if tight(cfg):
         out.brx = V((Z, X - 1, T, D), bf16)
-        out.brz = V((Z - 1, T, D), bf16)
-        out.bs0, out.bs1, out.bs2, out.bs3 = out.hs0, out.hs1, out.hs2, out.hs3
+        out.brz = V((2, T, D), bf16)
+        out.brn = V((2, T, D), bf16)
+        out.bs0, out.bs1, out.bs2, out.bs3, out.bs4 = Scatter.sems(S)
     else:
         out.mn = V((S, T, cp), bf16)
         out.mall = V((S, T, cp), bf16)

time: 247 us -> 232 us (0.939)
  Pallas kernels: 244 us -> 226 us
    pallas_call x1, Pallas kernels: 233 us -> 216 us  [shards(): pl.pallas_call(kern, out_shape=[outs[n] for n in on], in_specs=[v, v, hbm...]
where the time goes in v6:
time: 232 us; the launch traced here: 228 us
  Pallas kernels  226 us (97%)
    pallas_call x1, Pallas kernels, shards(): pl.pallas_call(kern, out_shape=[outs[n] for n in on], in_specs=[v, v, hbm...  216 us
    pallas_call x1, Pallas kernels, shards(): pl.pallas_call(lambda *refs: assemble(cfg, dims, *refs), grid=(steps,), o...  10.2 us

profile of v6, /device:TPU:0, one launch (start us, length us, event | category | flops | bytes accessed | tf_op | source)
XLA Modules:
  0.0 228.4 jit_solution(9927620862026258135)
XLA Ops:
  0.6 215.8 %shard_map.211 = (bf16[128,1536]{1,0:T(8,128)(2,1)}, f32[128,1536]{1,0:T(8,128)}, bf16[8,384,384]{2,1,0:T(8,128)(2,1)}, bf16[3,8,384,128]{3,2,1,0:T(8,128)(2,1)}...) custom-call(bf16[128,1536]{1,0:T(8,128)(2,1)} %bitcast.10, ...), custom_call_target="tpu_custom_call" | custom-call | tf_op jit(solution)/shard_map/pallas_call | solution.py:1286
  216.5 0.0 copy-start.1
  216.5 0.0 copy-start
  216.5 10.2 %shard_map.212 = (f32[384,6400]{1,0:T(8,128)}, f32[48,384]{1,0:T(8,128)}, f32[4,832]{1,0:T(4,128)}, f32[832]{0:T(1024)}, f32[768]{0:T(1024)}, /*index=5*/f32[384...) custom-call(bf16[8,384,384]{2,1,0:T(8,128)(2,1)} %get-tuple-element.31.refs_0_, ...), custom_call_target="tpu_custom_call" | custom-call | tf_op jit(solution)/shard_map/pallas_call | solution.py:1308
  226.8 0.0 copy-done.1
  226.8 0.7 copy.26
  227.5 0.0 copy-done
  227.5 0.9 copy.27
Async XLA Ops:
  216.5 10.3 %copy-start.1 = (bf16[128,1536]{1,0:T(8,128)(2,1)S(1)}, bf16[128,1536]{1,0:T(8,128)(2,1)}, u32[]{:S(2)}) copy-start(bf16[128,1536]{1,0:T(8,128)(2,1)} %get-tuple-element.29) | copy-start | bytes 1179652
  216.5 11.0 %copy-start = (f32[128,1536]{1,0:T(8,128)S(1)}, f32[128,1536]{1,0:T(8,128)}, u32[]{:S(2)}) copy-start(f32[128,1536]{1,0:T(8,128)} %get-tuple-element.30) | copy-start | bytes 2359300

commit v7 on v6

--- a/solution.py
+++ b/solution.py
@@ -1024,6 +1024,23 @@
     sg.relay(1)
     for t in range(nt):
         xg(t).relay(1)
+    mine = tok[...].astype(f32)
+    if tight(cfg):
+        O.block[...] = (mine + blk.total()).astype(bf16)
+    else:
+        for g in wogs[1:]:
+            g.wait_across()
+        arrived(R.mall, R.ms0, R.ms1)
+        R.mall[pc.s] = R.mn[pc.s]
+        R.total[...] = mine
+
+        def add(g, carry):
+            w = R.w_out[lax.rem(g, per), g // per]
+            R.total[...] += mm(R.mall[g], w)
+            return carry
+
+        lax.fori_loop(0, S, add, 0)
+        O.block[...] = R.total[...].astype(bf16)
     lax.fori_loop(2, pc.Z, hid_column, 0)
     for zb in (3, 2):
         hid.merge(zb)
@@ -1054,23 +1071,6 @@
     for zb in (1, 0):
         hid.merge(zb)
 
-    mine = tok[...].astype(f32)
-    if tight(cfg):
-        O.block[...] = (mine + blk.total()).astype(bf16)
-    else:
-        for g in wogs[1:]:
-            g.wait_across()
-        arrived(R.mall, R.ms0, R.ms1)
-        R.mall[pc.s] = R.mn[pc.s]
-        R.total[...] = mine
-
-        def add(g, carry):
-            w = R.w_out[lax.rem(g, per), g // per]
-            R.total[...] += mm(R.mall[g], w)
-            return carry
-
-        lax.fori_loop(0, S, add, 0)
-        O.block[...] = R.total[...].astype(bf16)
     scale = lax.rsqrt(jnp.mean(mine * mine, axis=1, keepdims=True) + epsilon)
     e = hid.total() * small[6:7, :]
     mean = jnp.mean(e * mine, axis=1, keepdims=True)
@@ -1170,8 +1170,12 @@
     return out
 
 
-def assemble(cfg, dims, gz, gx, gbc, go, sm, win, step, conv, bias, gate, norm, h0, h1, h2, wout):
+def assemble(cfg, dims, gz, gx, gbc, go, sm, *refs):
     S, F, T, D, cp, WC = cfg
+    n = (len(refs) - 10) // 2
+    for a, b in zip(refs[:n], refs[n + 10 :]):
+        b[...] = a[...]
+    win, step, conv, bias, gate, norm, h0, h1, h2, wout = refs[n : n + 10]
     inner, nheads, cols = dims
     for g in range(S):
         win[:, g * cols : (g + 1) * cols] = gz[g, :, :cols].astype(f32)
@@ -1305,31 +1309,37 @@
     def out(*shape):
         return jax.ShapeDtypeStruct(shape, f32)
 
+    through = [G.block, G.input] if T % (16 * steps) == 0 else []
+    tok_rows = [pl.BlockSpec((T // steps, D), lambda i: (i, 0)) for _ in through]
     joined = pl.pallas_call(
         lambda *refs: assemble(cfg, dims, *refs),
         grid=(steps,),
         out_shape=[
             out(Dl, 2 * inner + 2 * N), out(heads, Dl), out(4, cl), out(cl), out(gl),
             out(Dl), out(hl), out(hl), out(hl), out(per * cols, D),
-        ],
+        ]
+        + [jax.ShapeDtypeStruct(a.shape, a.dtype) for a in through],
         in_specs=[
             pl.BlockSpec((S, rows, cp), lambda i: (0, i, 0)),
             pl.BlockSpec((nt, S, rows, 128), lambda i: (0, 0, i, 0)),
             pl.BlockSpec((rows, 2 * N), lambda i: (i, 0)),
             pl.BlockSpec((1, 1, cr, D), lambda i: (lax.rem(i, pieces), i // pieces, 0, 0)),
             whole(S, 16, D),
-        ],
+        ]
+        + tok_rows,
         out_specs=[
             pl.BlockSpec((rows, 2 * inner + 2 * N), lambda i: (i, 0)),
             whole(heads, Dl), whole(4, cl), whole(cl), whole(gl), whole(Dl), whole(hl),
             whole(hl), whole(hl),
             pl.BlockSpec((cr, D), lambda i: (i, 0)),
-        ],
-    )(G.gz, G.gx, G.gbc.reshape(Dl, 2 * N), G.go, G.sm)
-    win, stepg, conv, bias, gate, norm, hd0, hd1, hd2, wout = joined
+        ]
+        + tok_rows,
+    )(G.gz, G.gx, G.gbc.reshape(Dl, 2 * N), G.go, G.sm, *through)
+    win, stepg, conv, bias, gate, norm, hd0, hd1, hd2, wout = joined[:10]
+    block, grad = joined[10:] if through else (G.block, G.input)
     return (
-        G.block[None],
-        G.input[None],
+        block[None],
+        grad[None],
         win,
         stepg.T,
         conv,

time: 232 us -> 231 us (level)
  no operation moved by 1% of the time
where the time goes in v7:
time: 231 us; the launch traced here: 227 us
  Pallas kernels  227 us (98%)
    pallas_call x1, Pallas kernels, shards(): pl.pallas_call(kern, out_shape=[outs[n] for n in on], in_specs=[v, v, hbm...  216 us
    pallas_call x1, Pallas kernels, shards(): pl.pallas_call(lambda *refs: assemble(cfg, dims, *refs), grid=(steps,), o...  10.8 us

profile of v7, /device:TPU:0, one launch (start us, length us, event | category | flops | bytes accessed | tf_op | source)
XLA Modules:
  0.0 227.2 jit_solution(3654217913124896744)
XLA Ops:
  0.6 215.8 %shard_map.211 = (bf16[128,1536]{1,0:T(8,128)(2,1)}, f32[128,1536]{1,0:T(8,128)}, bf16[8,384,384]{2,1,0:T(8,128)(2,1)}, bf16[3,8,384,128]{3,2,1,0:T(8,128)(2,1)}...) custom-call(bf16[128,1536]{1,0:T(8,128)(2,1)} %bitcast.9, ...), custom_call_target="tpu_custom_call" | custom-call | tf_op jit(solution)/shard_map/pallas_call | solution.py:1290
  216.5 10.8 %shard_map.212 = (f32[384,6400]{1,0:T(8,128)}, f32[48,384]{1,0:T(8,128)}, f32[4,832]{1,0:T(4,128)}, f32[832]{0:T(1024)}, f32[768]{0:T(1024)}, /*index=5*/f32[384...) custom-call(bf16[8,384,384]{2,1,0:T(8,128)(2,1)} %get-tuple-element., ...), custom_call_target="tpu_custom_call" | custom-call | tf_op jit(solution)/shard_map/pallas_call | solution.py:1314

commit v8 on v7

--- a/solution.py
+++ b/solution.py
@@ -1189,7 +1189,7 @@
     Dl = D // F
     win[:, 2 * inner :] = gbc[...].astype(f32)
 
-    @pl.when(pl.program_id(0) == 0)
+    @pl.when(pl.program_id(0) == 2)
     def _():
         f = lax.axis_index("fsdp")
 

time: 231 us -> 231 us (level)
  no operation moved by 1% of the time
where the time goes in v8:
time: 231 us; the launch traced here: 227 us
  Pallas kernels  227 us (98%)
    pallas_call x1, Pallas kernels, shards(): pl.pallas_call(kern, out_shape=[outs[n] for n in on], in_specs=[v, v, hbm...  216 us
    pallas_call x1, Pallas kernels, shards(): pl.pallas_call(lambda *refs: assemble(cfg, dims, *refs), grid=(steps,), o...  10.8 us

profile of v8, /device:TPU:0, one launch (start us, length us, event | category | flops | bytes accessed | tf_op | source)
XLA Modules:
  0.0 227.2 jit_solution(1465730929140186584)
XLA Ops:
  0.6 215.8 %shard_map.211 = (bf16[128,1536]{1,0:T(8,128)(2,1)}, f32[128,1536]{1,0:T(8,128)}, bf16[8,384,384]{2,1,0:T(8,128)(2,1)}, bf16[3,8,384,128]{3,2,1,0:T(8,128)(2,1)}...) custom-call(bf16[128,1536]{1,0:T(8,128)(2,1)} %bitcast.9, ...), custom_call_target="tpu_custom_call" | custom-call | tf_op jit(solution)/shard_map/pallas_call | solution.py:1290
  216.5 10.8 %shard_map.212 = (f32[384,6400]{1,0:T(8,128)}, f32[48,384]{1,0:T(8,128)}, f32[4,832]{1,0:T(4,128)}, f32[832]{0:T(1024)}, f32[768]{0:T(1024)}, /*index=5*/f32[384...) custom-call(bf16[8,384,384]{2,1,0:T(8,128)(2,1)} %get-tuple-element., ...), custom_call_target="tpu_custom_call" | custom-call | tf_op jit(solution)/shard_map/pallas_call | solution.py:1314
